TPU v7x, 32 devices: a whole 2x2x4 slice. The times are simulated.
32 devices in a mesh: dp: 8 (over z, core), mp: 4 (over y, x).
Axes of the slice: x: 2, y: 2, z: 4, core: 2. Of those that a mesh axis runs over, the one named last changes fastest.
Arguments:
- patches: bfloat16 [256, 256, 1280], P(('dp', 'mp')), may hold values from -6 to 6
- position: bfloat16 [256, 1280], replicated, may hold values from -3 to 3
- keep: int32 [256, 64], P(('dp', 'mp')), may hold values from 0 to 255, as said below
- counts: int32 [256], replicated, may hold values from 1 to 64, as said below
- offsets: int32 [256], replicated, may hold values from 0 to 10239, as said below
- ln_gain: float32 [1, 2, 1280], replicated, may hold values from 0.25 to 1.75
- ln_bias: float32 [1, 2, 1280], replicated, may hold values from -2 to 2
- w_qkv: bfloat16 [1, 3, 1280, 1280], P(None, None, 'dp', 'mp')
- b_qkv: float32 [1, 3, 1280], P(None, None, 'mp'), may hold values from -3 to 3
- w_o: bfloat16 [1, 1280, 1280], P(None, 'mp', 'dp'), may hold values from -0.15625 to 0.15625
- b_o: float32 [1, 1280], replicated, may hold values from -1.5 to 1.5
- w_up: bfloat16 [1, 1280, 5120], P(None, 'dp', 'mp'), may hold values from -0.15625 to 0.15625
- b_up: float32 [1, 5120], P(None, 'mp'), may hold values from -3 to 3
- w_down: bfloat16 [1, 5120, 1280], P(None, 'mp', 'dp'), may hold values from -0.078125 to 0.078125
- b_down: float32 [1, 1280], replicated, may hold values from -1.5 to 1.5
Outputs:
- encoded: bfloat16 [10240, 1280], P(('dp', 'mp'))
Inputs may be any that keep to these rules, and one draw needn't show every extreme that they name: `keep`: the first counts[i] entries of row i are distinct and name image i's visible patches; later entries are unused. `counts`: some image has exactly 64 visible patches. Image i, held by dp index s = i // 32, occupies packed rows offsets[i] to offsets[i] + counts[i] - 1, all inside the aligned block of 160 rows numbered d * 8 + s for some shard d; no two images share a row.
All inputs are finite; a program needn't handle non-finite values.
Results may differ from a plain program's by a relative error of at most 0.015.
Values may be sent and summed in bfloat16 or wider, within the bound.
No kernel may reach another device: no remote copies, remote signals or barrier semaphores. Data moves between devices by JAX's collectives and lax.ppermute only.
A program may use at most 64 MiB of HBM per device.

v0:
```python
import math

import jax
import jax.numpy as jnp
from jax import lax
from jax.sharding import PartitionSpec as P

HEAD = 80


def norm_rows(values, gain_row, shift_row):
    row_mean = jnp.mean(values, axis=-1, keepdims=True)
    centred = values - row_mean
    spread = jnp.mean(centred * centred, axis=-1, keepdims=True)
    return (centred * lax.rsqrt(spread + 1e-06) * gain_row + shift_row).astype(jnp.bfloat16)


def gather_rows(normed):
    return lax.all_gather(normed, "mp", axis=0, tiled=True)


def fold_rows(gathered, weight):
    return jnp.einsum(
        "rd,tdc->trc",
        gathered,
        lax.all_gather(weight, "dp", axis=1, tiled=True),
        preferred_element_type=jnp.float32,
    )


def project_sum(left, weight):
    partials = jnp.dot(
        left, lax.all_gather(weight, "dp", axis=1, tiled=True), preferred_element_type=jnp.float32
    )
    return lax.psum_scatter(
        partials.astype(jnp.bfloat16), "mp", scatter_dimension=0, tiled=True
    ).astype(jnp.float32)


def attend(projected, labels, block_rows):
    row_count = projected.shape[1]
    blocks = row_count // block_rows
    head_count = projected.shape[2] // HEAD
    shaped = projected.reshape(3, blocks, block_rows, head_count, HEAD)
    scores = jnp.einsum(
        "bqhe,bkhe->bhqk", shaped[0], shaped[1], preferred_element_type=jnp.float32
    ) * (1.0 / math.sqrt(HEAD))
    labels_block = labels.reshape(blocks, block_rows)
    matches = labels_block[:, None, :, None] == labels_block[:, None, None, :]
    scores = jnp.where(matches, scores, -jnp.inf)
    row_max = jnp.max(scores, axis=-1, keepdims=True)
    weights = jnp.exp(scores - row_max)
    probabilities = (weights / jnp.sum(weights, axis=-1, keepdims=True)).astype(jnp.bfloat16)
    attended = jnp.einsum(
        "bhqk,bkhe->bqhe", probabilities, shaped[2], preferred_element_type=jnp.float32
    )
    return attended.reshape(row_count, head_count * HEAD).astype(jnp.bfloat16)


def group_rows(item_count, unit_rows):
    factor = 1
    while item_count % (factor * 2) == 0 and factor * unit_rows < 512:
        factor = factor * 2
    return factor * unit_rows


def run_layers(
    stream, labels, block_rows, ln_gain, ln_bias, w_qkv, b_qkv, w_o, b_o, w_up, b_up, w_down, b_down
):
    normed = norm_rows(stream.astype(jnp.float32), ln_gain[0, 0], ln_bias[0, 0])
    projected = (fold_rows(gather_rows(normed), w_qkv[0]) + b_qkv[0][:, None, :]).astype(
        jnp.bfloat16
    )
    attended = attend(projected, labels, block_rows)
    residual = stream.astype(jnp.float32) + project_sum(attended, w_o[0]) + b_o[0]
    normed_mlp = norm_rows(residual, ln_gain[0, 1], ln_bias[0, 1])
    up_proj = fold_rows(gather_rows(normed_mlp), w_up[0][None])[0] + b_up[0]
    hidden = jax.nn.gelu(up_proj, approximate=False).astype(jnp.bfloat16)
    stream = (residual + project_sum(hidden, w_down[0]) + b_down[0]).astype(jnp.bfloat16)
    return stream


def per_device(
    patches,
    position,
    keep,
    counts,
    offsets,
    ln_gain,
    ln_bias,
    w_qkv,
    b_qkv,
    w_o,
    b_o,
    w_up,
    b_up,
    w_down,
    b_down,
):
    local_images = patches.shape[0]
    keep_most = keep.shape[1]
    column_count = patches.shape[2]
    shard_count = lax.axis_size("dp")
    group_size = lax.axis_size("mp")
    images_here = local_images * group_size
    per_slot = (images_here + shard_count - 1) // shard_count
    slot_rows = max(keep_most + 16, per_slot * keep_most * 5 // 8)
    pack_rows = slot_rows * shard_count
    local_rows = pack_rows // group_size
    dp_index = lax.axis_index("dp")
    mp_index = lax.axis_index("mp")
    first_image = dp_index * images_here
    group_counts = lax.dynamic_slice_in_dim(counts, first_image, images_here)
    group_offsets = lax.dynamic_slice_in_dim(offsets, first_image, images_here)
    picked = jnp.take_along_axis(patches, keep[:, :, None], axis=1)
    placed = jnp.take(position, keep, axis=0)
    tokens = (picked.astype(jnp.float32) + placed.astype(jnp.float32)).astype(jnp.bfloat16)
    positions_in = jnp.arange(keep_most, dtype=jnp.int32)
    group_live = positions_in[None, :] < group_counts[:, None]
    shard_index = group_offsets // pack_rows
    base_row = (
        shard_index * slot_rows + group_offsets - shard_index * pack_rows - dp_index * slot_rows
    )
    target = jnp.where(group_live, base_row[:, None] + positions_in[None, :], pack_rows).reshape(-1)
    layer_weights = (ln_gain, ln_bias, w_qkv, b_qkv, w_o, b_o, w_up, b_up, w_down, b_down)
    image_ids = jnp.arange(counts.shape[0], dtype=jnp.int32)
    packed_rows = dp_index * pack_rows + jnp.arange(pack_rows, dtype=jnp.int32)
    inside = (packed_rows[:, None] >= offsets[None, :]) & (
        packed_rows[:, None] < (offsets + counts)[None, :]
    )
    labels = jnp.max(jnp.where(inside, image_ids[None, :] + 1, 0), axis=1) - 1
    featured = lax.all_to_all(
        tokens.reshape(-1, column_count), "mp", split_axis=1, concat_axis=0, tiled=True
    )
    buffer_rows = (
        jnp.zeros((pack_rows, featured.shape[1]), jnp.bfloat16)
        .at[target]
        .set(featured, mode="drop")
    )
    stream = lax.all_to_all(
        lax.all_to_all(buffer_rows, "dp", split_axis=0, concat_axis=0, tiled=True),
        "mp",
        split_axis=0,
        concat_axis=1,
        tiled=True,
    )
    stream = run_layers(stream, labels, group_rows(shard_count, slot_rows), *layer_weights)
    own_labels = lax.dynamic_slice_in_dim(labels, mp_index * local_rows, local_rows)
    output = jnp.where(own_labels[:, None] >= 0, stream, jnp.zeros_like(stream))
    return output


def solution(mesh):
    in_specs = (
        P(("dp", "mp"), None, None),
        P(),
        P(("dp", "mp"), None),
        P(),
        P(),
        P(),
        P(),
        P(None, None, "dp", "mp"),
        P(None, None, "mp"),
        P(None, "mp", "dp"),
        P(),
        P(None, "dp", "mp"),
        P(None, "mp"),
        P(None, "mp", "dp"),
        P(),
    )
    out_specs = P(("dp", "mp"), None)
    return jax.shard_map(
        per_device, mesh=mesh, in_specs=in_specs, out_specs=out_specs, check_vma=False
    )
```

profile of v0, /device:TPU:0, one launch (start us, length us, event | category | flops | bytes accessed | tf_op | source)
XLA Modules:
  0.0 429.3 jit_solution(11046292865014236250)
XLA Ops:
  6.5 0.8 compare_select_fusion.1
  7.3 0.7 bitcast_or_fusion
  8.0 0.7 compare_and_fusion
  8.7 0.1 reshape.184
  8.8 2.1 gather_fusion
  10.9 1.5 copy.54
  12.4 0.1 reshape.190
  12.5 8.7 %gather_fusion.1 = bf16[512,1280]{1,0:T(8,128)(2,1)S(1)} fusion(bf16[8,256,1280]{2,1,0:T(8,128)(2,1)} %param.15, s32[512]{0:T(512)S(1)} %reshape.190), kind=kCustom, calls=%fused_computation.1 | custom fusion | bytes 2625536 | tf_op jit(solution)/shard_map/jit(take_along_axis)/gather | solution.py:115
  21.1 1.5 copy.53
  22.6 0.1 broadcast_in_dim.84
  22.7 3.3 add_convert_fusion.1
  26.0 5.2 %all-to-all-start = ((bf16[512,4,320]{0,2,1:T(8,128)(2,1)}), bf16[512,4,320]{0,2,1:T(8,128)(2,1)S(1)}, u32[]{:S(2)}, u32[]{:S(2)}) async-start(bf16[512,4,320]{0,2,1:T(8,128)(2,1)} %add_convert_fusion.1), calls=%async_computation | async-start | bytes 2621440 | tf_op jit(solution)/shard_map/all_to_all | solution.py:132
  31.2 0.7 all-gather.15.cloned.1.call-update
  31.9 0.1 dynamic_slice.10
  32.0 0.1 subtract_subtract_fusion
  32.1 0.1 add_select_fusion
  32.1 0.1 select_n.76
  32.2 15.4 %all-to-all-done = bf16[512,4,320]{0,2,1:T(8,128)(2,1)S(1)} async-done(((bf16[512,4,320]{0,2,1:T(8,128)(2,1)}), bf16[512,4,320]{0,2,1:T(8,128)(2,1)S(1)}, u32[]{:S(2)}, u32[]{:S(2)}) %all-to-all-start) | async-done | bytes 1310752 | tf_op jit(solution)/shard_map/all_to_all | solution.py:132
  47.6 1.6 copy.65
  49.2 10.0 %scatter_custom_fusion = bf16[1280,320]{1,0:T(8,128)(2,1)S(1)} fusion(s32[2048]{0:T(1024)S(1)} %bitcast.59, bf16[2048,320]{1,0:T(8,128)(2,1)} %bitcast.57, bf16[]{:T(256)} %constant.58.clone.1), kind=kCustom, calls=%fused_computation.64 | custom fusion | bytes 819712 | tf_op jit(solution)/shard_map/scatter | solution.py:138
  59.2 32.4 %all_to_all.38 = bf16[8,160,320]{2,1,0:T(8,128)(2,1)} all-to-all(bf16[8,160,320]{2,1,0:T(8,128)(2,1)S(1)} %bitcast.55), channel_id=1, replica_groups=mesh['dp'=8,'mp'=4] {'dp'}, dimensions={0} | all-to-all | bytes 1638400 | tf_op jit(solution)/shard_map/all_to_all | solution.py:141
  91.6 3.6 all-to-all-start.2
  95.3 0.1 slice_reduce_fusion.2
  95.3 13.2 %all-to-all-done.2 = bf16[4,320,320]{2,1,0:T(8,128)(2,1)S(1)} async-done(((bf16[4,320,320]{2,1,0:T(8,128)(2,1)}), bf16[4,320,320]{2,1,0:T(8,128)(2,1)S(1)}, u32[]{:S(2)}, u32[]{:S(2)}) %all-to-all-start.2) | async-done | bytes 819232 | tf_op jit(solution)/shard_map/all_to_all | solution.py:140
  108.5 0.1 convert_bitcast_fusion
  108.6 2.5 copy.57
  111.2 2.4 reshape.181
  113.6 0.2 convert_reduce_fusion
  113.8 0.4 fusion.24
  114.3 1.2 add_convert_fusion.4
  115.6 0.0 reduce-scatter.3.cloned.1.call-start
  115.7 0.5 select_reduce_fusion
  116.2 1.4 broadcast_compare_fusion
  117.6 17.2 %all-gather.1 = bf16[1,320,1280]{1,2,0:T(8,128)(2,1)} all-gather(bf16[1,320,160]{1,2,0:T(8,128)(2,1)S(1)} %copy-done.5), channel_id=3, replica_groups=mesh['dp'=8,'mp'=4] {'dp'}, dimensions={2}, use_global_device_ids=true | all-gather | bytes 921600 | tf_op jit(solution)/shard_map/all_gather | solution.py:33
  134.8 23.6 %all-gather.9.cloned.1.call-done = bf16[1280,1280]{1,0:T(8,128)(2,1)} async-done(((bf16[320,1280]{1,0:T(8,128)(2,1)}), bf16[1280,1280]{1,0:T(8,128)(2,1)}) %all-gather.9.cloned.1.call-update) | async-done | bytes 3276816 | tf_op jit(solution)/shard_map/all_gather | solution.py:19
  158.4 6.2 %fusion.19 = bf16[3,1280,320]{1,2,0:T(8,128)(2,1)S(1)} fusion(bf16[1280,1280]{1,0:T(8,128)(2,1)} %all-gather.9.cloned.1.call-done, bf16[1,3,1280,320]{3,2,1,0:T(8,128)(2,1)} %all-gather.15.cloned.1.call-done, f32[3,320]{1,0:T(4,128)S(1)} %bitcast.60), kind=kOutput, calls=%fused_computation.38 | convolution fusion | flops 3148185600 | bytes 8195840 | tf_op jit(solution)/shard_map/rd,tdc->trc/dot_general | solution.py:23
  164.7 1.3 fusion.48
  166.0 2.8 squeeze.21
  168.8 2.8 squeeze.22
  171.6 1.1 squeeze.20
  172.7 10.9 %fusion.49 = (f32[2,4,640]{2,1,0:T(4,128)S(1)}, f32[2,4,640,640]{2,3,1,0:T(8,128)}) fusion(pred[2,640,640]{1,2,0:T(8,128)(4,1)} %broadcast_compare_fusion, bf16[2,640,4,80]{1,0,3,2:T(2,128)(2,1)} %squeeze.22, bf16[2,640,4,80]{1,0,3,2:T(2,128)(2,1)} %squeeze.21), kind=kOutput, calls=%fused_computation.92 | convolution fusion | flops 537395840 | bytes 15585280 | tf_op jit(solution)/shard_map/sub | solution.py:52
  183.7 6.0 %fusion.28 = bf16[2,640,4,80]{1,3,2,0:T(8,128)(2,1)S(1)} fusion(f32[2,4,640,640]{2,3,1,0:T(8,128)} %get-tuple-element.13, f32[2,4,640]{2,1,0:T(4,128)S(1)} %get-tuple-element.12, bf16[2,640,4,80]{1,0,3,2:T(2,128)(2,1)S(1)} %copy-done.4), kind=kOutput, calls=%fused_computation.55 | convolution fusion | flops 531251200 | bytes 14766080 | tf_op jit(solution)/shard_map/bhqk,bkhe->bqhe/dot_general | solution.py:54
  189.6 0.8 copy.63
  190.5 0.1 copy.68
  190.6 0.2 copy-done.3
  190.8 3.6 convolution_convert_fusion.1
  194.5 0.0 all-gather.13.cloned.1.call-start
  194.5 0.5 all-gather.13.cloned.1.call-update
  195.1 0.3 all-gather.11.cloned.1.call-start
  195.4 44.3 %reduce-scatter.3.cloned.1.call-done = bf16[320,1280]{1,0:T(8,128)(2,1)} async-done(((bf16[1280,1280]{1,0:T(8,128)(2,1)}), bf16[320,1280]{1,0:T(8,128)(2,1)}) %reduce-scatter.3.cloned.1.call-update) | async-done | bytes 819216 | tf_op jit(solution)/shard_map/reduce_scatter | solution.py:35
  239.7 1.5 fusion.47
  241.2 1.6 multiply_reduce_fusion
  242.8 1.3 add_convert_fusion.3
  244.1 0.0 all-gather.17.cloned.1.call-start
  244.2 0.5 all-gather.17.cloned.1.call-update
  244.8 35.7 %all-gather.13.cloned.1.call-done = bf16[1,1280,1280]{2,1,0:T(8,128)(2,1)} async-done(((bf16[1,160,1280]{2,1,0:T(8,128)(2,1)}), bf16[1,1280,1280]{2,1,0:T(8,128)(2,1)}) %all-gather.13.cloned.1.call-update) | async-done | bytes 3276816 | tf_op jit(solution)/shard_map/all_gather | solution.py:26
  280.5 45.5 %all-gather.11.cloned.1.call-done = bf16[1280,1280]{1,0:T(8,128)(2,1)} async-done(((bf16[320,1280]{1,0:T(8,128)(2,1)}), bf16[1280,1280]{1,0:T(8,128)(2,1)}) %all-gather.11.cloned.1.call-update) | async-done | bytes 3276816 | tf_op jit(solution)/shard_map/all_gather | solution.py:19
  326.0 21.0 %fusion.4 = bf16[1280,1280]{1,0:T(8,128)(2,1)} fusion(bf16[1280,1280]{1,0:T(8,128)(2,1)} %all-gather.11.cloned.1.call-done, bf16[1,1280,1280]{2,1,0:T(8,128)(2,1)} %all-gather.13.cloned.1.call-done, f32[1280]{0:T(1024)S(1)} %reduce.9), kind=kOutput, calls=%fused_computation.14 | convolution fusion | flops 4302438400 | bytes 9835520 | tf_op jit(solution)/shard_map/rd,tdc->trc/dot_general | solution.py:23
  347.0 19.9 %all-gather.17.cloned.1.call-done = bf16[1,1280,1280]{1,2,0:T(8,128)(2,1)} async-done(((bf16[1,1280,160]{1,2,0:T(8,128)(2,1)}), bf16[1,1280,1280]{1,2,0:T(8,128)(2,1)}) %all-gather.17.cloned.1.call-update) | async-done | bytes 3276816 | tf_op jit(solution)/shard_map/all_gather | solution.py:33
  366.9 9.1 %convolution_convert_fusion = bf16[1280,1280]{1,0:T(8,128)(2,1)} fusion(bf16[1280,1280]{1,0:T(8,128)(2,1)} %fusion.4, bf16[1,1280,1280]{1,2,0:T(8,128)(2,1)} %all-gather.17.cloned.1.call-done), kind=kOutput, calls=%fused_computation.10 | convolution fusion | flops 4195942400 | bytes 9830400 | tf_op jit(solution)/shard_map/dot_general | solution.py:32
  375.9 0.7 copy-done.11
  376.6 0.1 dynamic-slice_compare_fusion
  376.7 43.3 %reduce-scatter.5.cloned.1.call-done = bf16[320,1280]{1,0:T(8,128)(2,1)} async-done(((bf16[1280,1280]{1,0:T(8,128)(2,1)}), bf16[320,1280]{1,0:T(8,128)(2,1)}) %reduce-scatter.5.cloned.1.call-update) | async-done | bytes 819216 | tf_op jit(solution)/shard_map/reduce_scatter | solution.py:35
  420.0 2.4 fusion.30
  (49 shorter events, 0.3 us)
Async XLA Ops:
  6.5 2.2 copy-start
  22.7 9.2 %copy-start.13 = (s32[256]{0:T(256)S(1)}, s32[256]{0:T(256)}, u32[]{:S(2)}) copy-start(s32[256]{0:T(256)} %param.18) | copy-start | bytes 3076
  22.7 9.3 %copy-start.8 = (s32[256]{0:T(256)S(1)}, s32[256]{0:T(256)}, u32[]{:S(2)}) copy-start(s32[256]{0:T(256)} %param.19) | copy-start | bytes 3076
  26.0 21.6 %all-to-all-start = ((bf16[512,4,320]{0,2,1:T(8,128)(2,1)}), bf16[512,4,320]{0,2,1:T(8,128)(2,1)S(1)}, u32[]{:S(2)}, u32[]{:S(2)}) async-start(bf16[512,4,320]{0,2,1:T(8,128)(2,1)} %add_convert_fusion.1), calls=%async_computation | async-start | bytes 2621440 | tf_op jit(solution)/shard_map/all_to_all | solution.py:132
  31.2 103.7 %all-gather.15.cloned.1.call-start = ((), (), s32[]{:S(2)}) async-start(), calls=%async_computation.10 | async-start | bytes 3317760 | tf_op jit(solution)/shard_map/all_gather | solution.py:26
  47.6 47.7 %copy-start.6 = (f32[1,2,1280]{2,1,0:T(2,128)S(1)}, f32[1,2,1280]{2,1,0:T(2,128)}, u32[]{:S(2)}) copy-start(f32[1,2,1280]{2,1,0:T(2,128)} %param.21) | copy-start | bytes 30724
  47.6 47.7 %copy-start.7 = (f32[1,2,1280]{2,1,0:T(2,128)S(1)}, f32[1,2,1280]{2,1,0:T(2,128)}, u32[]{:S(2)}) copy-start(f32[1,2,1280]{2,1,0:T(2,128)} %param.20) | copy-start | bytes 30724
  91.6 16.9 %all-to-all-start.2 = ((bf16[4,320,320]{2,1,0:T(8,128)(2,1)}), bf16[4,320,320]{2,1,0:T(8,128)(2,1)S(1)}, u32[]{:S(2)}, u32[]{:S(2)}) async-start(bf16[4,320,320]{2,1,0:T(8,128)(2,1)} %bitcast.7), calls=%async_computation.2 | async-start | bytes 1966080 | tf_op jit(solution)/shard_map/all_to_all | solution.py:140
  95.3 63.2 %all-gather.9.cloned.1.call-start = ((), (), s32[]{:S(2)}) async-start(), calls=%async_computation.5 | async-start | bytes 4096000 | tf_op jit(solution)/shard_map/all_gather | solution.py:19
  113.6 2.1 copy-start.12
  113.6 4.0 copy-start.5
  115.6 124.1 %reduce-scatter.3.cloned.1.call-start = ((), (), s32[]{:S(2)}) async-start(), calls=%async_computation.6 | async-start | bytes 4096000 | tf_op jit(solution)/shard_map/reduce_scatter | solution.py:35
  172.7 10.9 %copy-start.4 = (bf16[2,640,4,80]{1,0,3,2:T(2,128)(2,1)S(1)}, bf16[2,640,4,80]{1,0,3,2:T(2,128)(2,1)}, u32[]{:S(2)}) copy-start(bf16[2,640,4,80]{1,0,3,2:T(2,128)(2,1)} %squeeze.20) | copy-start | bytes 2457604
  189.6 1.2 copy-start.3
  194.5 0.9 copy-start.9
  194.5 86.0 %all-gather.13.cloned.1.call-start = ((), (), s32[]{:S(2)}) async-start(), calls=%async_computation.8 | async-start | bytes 3686400 | tf_op jit(solution)/shard_map/all_gather | solution.py:26
  195.1 131.0 %all-gather.11.cloned.1.call-start = ((), (), s32[]{:S(2)}) async-start(), calls=%async_computation.7 | async-start | bytes 4096000 | tf_op jit(solution)/shard_map/all_gather | solution.py:19
  239.7 3.1 copy-start.2
  241.2 3.6 copy-start.10
  244.1 122.7 %all-gather.17.cloned.1.call-start = ((), (), s32[]{:S(2)}) async-start(), calls=%async_computation.11 | async-start | bytes 3686400 | tf_op jit(solution)/shard_map/all_gather | solution.py:33
  244.7 175.3 %reduce-scatter.5.cloned.1.call-start = ((), (), s32[]{:S(2)}) async-start(), calls=%async_computation.9 | async-start | bytes 4096000 | tf_op jit(solution)/shard_map/reduce_scatter | solution.py:35
  375.9 0.7 copy-start.11
  375.9 46.5 %copy-start.1 = (bf16[256,1280]{1,0:T(8,128)(2,1)S(1)}, bf16[256,1280]{1,0:T(8,128)(2,1)}, u32[]{:S(2)}) copy-start(bf16[256,1280]{1,0:T(8,128)(2,1)} %param.16) | copy-start | bytes 1966084
Sparse Core Ops, SparseCore 0:
  33.6 40.4 all-gather.14
  115.7 42.7 all-gather.8
  194.6 44.9 reduce-scatter.2
  241.1 39.2 all-gather.12
  282.2 43.8 all-gather.10
  327.5 39.2 all-gather.16
  376.1 43.8 reduce-scatter.4
where the time goes:
time: 430 us; the launch traced here: 429 us
  waiting for transfers between devices  243 us (57%)
  matrix products  56.8 us (13%)
  blocking collectives  49.6 us (12%)
  local copies, waits for them, and re-layouts  40.6 us (9%)
  other arithmetic  16.6 us (4%)
  between operations  13.7 us (3%)
  starting transfers between devices  9.26 us (2%)
    reduce_scatter x2, waiting for transfers between devices, project_sum(): lax.psum_scatter(partials.astype(jnp.bfloat16), 'mp', scatter_dimension=0...  87.6 us
    all_gather x2, waiting for transfers between devices, gather_rows(): return lax.all_gather(normed, 'mp', axis=0, tiled=True)  69.2 us
    all_gather x2, waiting for transfers between devices, fold_rows(): lax.all_gather(weight, 'dp', axis=1, tiled=True)  35.7 us
    all_to_all x1, blocking collectives, per_device(): lax.all_to_all(buffer_rows, 'dp', split_axis=0, concat_axis=0, tiled=True)  32.4 us
    dot_general x2, matrix products, fold_rows(): jnp.einsum('rd,tdc->trc', gathered, lax.all_gather(weight, 'dp', axis=1,...  27.2 us
    all_gather x1, waiting for transfers between devices, project_sum(): lax.all_gather(weight, 'dp', axis=1, tiled=True)  19.9 us
    all_gather x1, blocking collectives, project_sum(): lax.all_gather(weight, 'dp', axis=1, tiled=True)  17.2 us
    all_to_all x1, waiting for transfers between devices, per_device(): lax.all_to_all(tokens.reshape(-1, column_count), 'mp', split_axis=1, conc...  15.4 us
  transfers between devices with their start and end apart: 9, of which 8 were waited for; matrix products, arithmetic and copies ran while one was open for 11% of the time, Pallas kernels for 0%

commit v1 on v0

v1 whole, which is shorter than its diff:
```python
import functools
import math

import jax
import jax.numpy as jnp
from jax import lax
from jax.experimental import pallas as pl
from jax.experimental.pallas import tpu as pltpu
from jax.sharding import PartitionSpec as P


HEAD = 80
LANES = 128
BF = jnp.bfloat16
F32 = jnp.float32
NT = (((1,), (1,)), ((), ()))


def cost(flops, moved):
    return pl.CostEstimate(flops=int(flops), bytes_accessed=int(moved), transcendentals=0)


def params(mib=48):
    return pltpu.CompilerParams(vmem_limit_bytes=mib * 1024 * 1024)


def embed_kernel(place_ref, keep_ref, patches_ref, position_ref, *refs):
    out_refs, token_ref = refs[:-1], refs[-1]
    per, patch_count, _ = patches_ref.shape
    row = keep_ref[0].astype(F32)
    tokens = row.shape[1]
    kept = jnp.broadcast_to(row, (tokens, tokens)).T
    reps = (patch_count + tokens - 1) // tokens
    wide = jnp.concatenate([kept] * reps, axis=1)[:, :patch_count]
    lane = lax.broadcasted_iota(jnp.int32, (tokens, patch_count), 1).astype(F32)
    onehot = jnp.where(wide == lane, 1.0, 0.0).astype(BF)
    each = tokens // per
    placed = jnp.dot(onehot, position_ref[...], preferred_element_type=F32)
    picked = jnp.concatenate(
        [
            jnp.dot(onehot[i * each : (i + 1) * each], patches_ref[i], preferred_element_type=F32)
            for i in range(per)
        ],
        axis=0,
    )
    token_ref[...] = (picked + placed).T.astype(BF).reshape(token_ref.shape)
    for k, ref in enumerate(out_refs):
        ref[...] = token_ref[jnp.bitwise_xor(place_ref[0], k)]


def embed(place, patches, position, keep, n_mp):
    images, patch_count, width = patches.shape
    keep_most = keep.shape[1]
    per = max(1, min(images, LANES // keep_most))
    steps = images // per
    tokens = per * keep_most
    return pl.pallas_call(
        embed_kernel,
        grid=(steps,),
        in_specs=[
            pl.BlockSpec(memory_space=pltpu.SMEM),
            pl.BlockSpec((1, 1, tokens), lambda i: (i, 0, 0)),
            pl.BlockSpec((per, patch_count, width), lambda i: (i, 0, 0)),
            pl.BlockSpec((patch_count, width), lambda i: (0, 0)),
        ],
        out_specs=[pl.BlockSpec((width // n_mp, tokens), lambda i: (0, i))] * n_mp,
        out_shape=[jax.ShapeDtypeStruct((width // n_mp, images * keep_most), BF)] * n_mp,
        scratch_shapes=[pltpu.VMEM((n_mp, width // n_mp, tokens), BF)],
        compiler_params=params(24),
        cost_estimate=cost(4e9, patches.size * 2),
        name="embed",
    )(place, keep.reshape(steps, 1, tokens), patches, position)


def pack_kernel(fold, slot_rows, group, n_src, place_ref, target_ref, *refs):
    feat_refs, out_refs = refs[:n_src], refs[n_src:]
    width, tokens = feat_refs[0].shape
    d = place_ref[1]
    piece = slot_rows // fold
    for g in range(0, len(out_refs), group):
        row = jnp.concatenate(
            [
                lax.broadcasted_iota(jnp.int32, (slot_rows, tokens), 0)
                + jnp.bitwise_xor(d, g + b) * slot_rows
                for b in range(group)
            ],
            axis=0,
        )
        total = jnp.zeros((group * slot_rows, width), F32)
        for j in range(n_src):
            at = jnp.bitwise_xor(place_ref[0], j)
            onehot = jnp.where(row == target_ref[at], 1.0, 0.0).astype(BF)
            total = total + lax.dot_general(onehot, feat_refs[j][...], NT, preferred_element_type=F32)
        for b in range(group):
            start = b * slot_rows
            chunks = [total[start + f * piece : start + (f + 1) * piece] for f in range(fold)]
            out_refs[g + b][...] = jnp.concatenate(chunks, axis=1).astype(BF)


def pack(place, featured, target, slots, slot_rows, fold):
    width, tokens = featured[0].shape
    smem = pl.BlockSpec(memory_space=pltpu.SMEM)
    vmem = pl.BlockSpec(memory_space=pltpu.VMEM)
    return pl.pallas_call(
        functools.partial(pack_kernel, fold, slot_rows, min(4, slots), len(featured)),
        in_specs=[smem] + [vmem] * (1 + len(featured)),
        out_specs=[vmem] * slots,
        out_shape=[jax.ShapeDtypeStruct((slot_rows // fold, fold * width), BF)] * slots,
        compiler_params=params(24),
        cost_estimate=cost(4e9, width * tokens * 8),
        name="pack",
    )(place, target, *featured)


def unfold(values, fold):
    width = values.shape[2] // fold
    values = values.astype(F32)
    pieces = [
        values[s, :, f * width : (f + 1) * width] for s in range(values.shape[0]) for f in range(fold)
    ]
    return jnp.concatenate(pieces, axis=0)


def fetch_start(groups, block, spm, buf_ref, sem_ref):
    for k, pieces in enumerate(groups):
        per = pieces[0].shape[0] // spm
        for i, piece in enumerate(pieces):

            def start(piece=piece, i=i, k=k):
                at = pl.ds((block - i * per) * spm, spm)
                pltpu.make_async_copy(piece.at[at], buf_ref.at[k], sem_ref.at[k]).start()

            here = len(pieces) == 1 or jnp.logical_and(block >= i * per, block < (i + 1) * per)
            if isinstance(block, int):
                if i * per <= block < (i + 1) * per:
                    start()
            elif here is True:
                start()
            else:
                pl.when(here)(start)


def fetch_wait(groups, spm, buf_ref, sem_ref):
    for k, pieces in enumerate(groups):
        pltpu.make_async_copy(pieces[0].at[pl.ds(0, spm)], buf_ref.at[k], sem_ref.at[k]).wait()


def cut(refs, counts):
    groups, at = [], 0
    for count in counts:
        groups.append(refs[at : at + count])
        at += count
    return groups, refs[at:]


def owner_block(place_ref, dest, spm):
    return jnp.bitwise_xor(jnp.bitwise_xor(place_ref[0], dest), place_ref[1] // spm)


def attend_block(block, gathered, me, refs, hc, spm):
    weight_ref, bias_ref, gain_ref, shift_ref, labrow, labcol, norm_ref = refs
    n_mp = len(gathered)
    _, width = gathered[0].shape
    full = width * n_mp
    mean = sum(jnp.sum(b, axis=1, keepdims=True) for b in gathered) * (1.0 / full)
    gathered = [b - mean for b in gathered]
    spread = sum(jnp.sum(b * b, axis=1, keepdims=True) for b in gathered) * (1.0 / full)
    scale = lax.rsqrt(spread + 1e-06)
    for k in range(n_mp):
        which = jnp.bitwise_xor(me, k)
        norm_ref[which] = (gathered[k] * scale * gain_ref[which] + shift_ref[which]).astype(BF)
    normed = jnp.concatenate([norm_ref[j] for j in range(n_mp)], axis=1)
    start = hc // LANES * LANES
    lead = hc - start
    qkv = jnp.dot(normed, weight_ref[:, start:], preferred_element_type=F32)
    query = qkv[:, lead : lead + hc] + bias_ref[:, :hc]
    query = (query * (1.0 / math.sqrt(HEAD))).astype(BF)
    key = (qkv[:, lead + hc : lead + 2 * hc] + bias_ref[:, hc : 2 * hc]).astype(BF)
    value = (qkv[:, lead + 2 * hc :] + bias_ref[:, 2 * hc :]).astype(BF)
    slot_rows = labcol.shape[1]
    heads = hc // HEAD
    lane_head = lax.broadcasted_iota(jnp.int32, (slot_rows, hc), 1) // HEAD
    results = []
    for s in range(spm):
        at = slice(s * slot_rows, (s + 1) * slot_rows)
        q, kk, v = query[at], key[at], value[at]
        zero = jnp.zeros_like(q)
        stacked = jnp.concatenate([jnp.where(lane_head == h, q, zero) for h in range(heads)], axis=0)
        scores = lax.dot_general(stacked, kk, NT, preferred_element_type=F32)
        same = labcol[block * spm + s] == labrow[block * spm + s]
        outs = jnp.zeros((slot_rows, hc), F32)
        for h in range(heads):
            sh = jnp.where(same, scores[h * slot_rows : (h + 1) * slot_rows], -jnp.inf)
            e = jnp.exp(sh - jnp.max(sh, axis=1, keepdims=True))
            prob = (e * (1.0 / jnp.sum(e, axis=1, keepdims=True))).astype(BF)
            outs = jnp.where(lane_head == h, jnp.dot(prob, v, preferred_element_type=F32), outs)
        results.append(outs)
    return jnp.concatenate(results, axis=1).astype(BF)


def attend_kernel(counts, blocks, last, spm, fold, hc, place_ref, *refs):
    n_mp = len(counts)
    groups, refs = cut(refs, counts)
    operands, refs = list(refs[:6]), refs[6:]
    prior, refs = (refs[0], refs[1:]) if last else (None, refs)
    outs = n_mp if last else 1
    out_refs, (norm_ref, buf_ref, sem_ref, mine_ref) = refs[:outs], refs[outs:]
    for i, block in enumerate(blocks):
        fetch_start(groups, block, spm, buf_ref.at[i], sem_ref.at[i])
    for i, block in enumerate(blocks):
        fetch_wait(groups, spm, buf_ref.at[i], sem_ref.at[i])
        gathered = [unfold(buf_ref[i, k], fold) for k in range(n_mp)]
        value = attend_block(block, gathered, place_ref[0], operands + [norm_ref], hc, spm)
        if last:
            mine_ref[i] = value
        else:
            out_refs[0][i] = value
    if last:
        for k in range(n_mp):
            block = owner_block(place_ref, k, spm)
            before = prior[jnp.minimum(block, blocks[0] - 1)]
            later = mine_ref[jnp.maximum(block - blocks[0], 0)]
            out_refs[k][...] = jnp.where(block < blocks[0], before, later)


def attend(place, gathered, blocks, prior, fold, hc, operands, spm):
    n_mp = len(gathered)
    _, piece, lanes = gathered[0][0].shape
    slot_rows = operands[4].shape[2]
    flat = sum(gathered, [])
    smem = pl.BlockSpec(memory_space=pltpu.SMEM)
    vmem = pl.BlockSpec(memory_space=pltpu.VMEM)
    last = prior is not None
    shape = (slot_rows, spm * hc)
    if last:
        out_shape = [jax.ShapeDtypeStruct(shape, BF)] * n_mp
    else:
        out_shape = [jax.ShapeDtypeStruct((len(blocks), *shape), BF)]
    return pl.pallas_call(
        functools.partial(
            attend_kernel, [len(g) for g in gathered], blocks, last, spm, fold, hc
        ),
        in_specs=[smem]
        + [pl.BlockSpec(memory_space=pltpu.HBM)] * len(flat)
        + [vmem] * (len(operands) + last),
        out_specs=[vmem] * len(out_shape),
        scratch_shapes=[
            pltpu.VMEM((n_mp, spm * slot_rows, lanes // fold), BF),
            pltpu.VMEM((len(blocks), n_mp, spm, piece, lanes), BF),
            pltpu.SemaphoreType.DMA((len(blocks), n_mp)),
            pltpu.VMEM((len(blocks), *shape), BF),
        ],
        out_shape=out_shape,
        compiler_params=params(24),
        cost_estimate=cost(len(blocks) * 4e9, operands[0].size * 4),
        name="attend",
    )(place, *flat, *operands, *([prior] if last else []))


def own_kernel(counts, spm, fold, place_ref, *refs):
    n_mp = len(counts)
    groups, (bias_ref, out_ref, buf_ref, sem_ref) = cut(refs, counts)
    fetch_start(groups, owner_block(place_ref, 0, spm), spm, buf_ref, sem_ref)
    fetch_wait(groups, spm, buf_ref, sem_ref)
    blocks = [unfold(buf_ref[k], fold) for k in range(n_mp)]
    ordered = []
    for j in range(n_mp):
        value = blocks[0]
        for k in range(1, n_mp):
            value = jnp.where(jnp.bitwise_xor(place_ref[0], k) == j, blocks[k], value)
        ordered.append(value)
    out_ref[...] = jnp.concatenate(ordered, axis=1) + bias_ref[...]


def own_rows(place, gathered, fold, bias, spm):
    n_mp = len(gathered)
    _, piece, lanes = gathered[0][0].shape
    features = sum(gathered, [])
    vmem = pl.BlockSpec(memory_space=pltpu.VMEM)
    return pl.pallas_call(
        functools.partial(own_kernel, [len(g) for g in gathered], spm, fold),
        in_specs=[pl.BlockSpec(memory_space=pltpu.SMEM)]
        + [pl.BlockSpec(memory_space=pltpu.HBM)] * len(features)
        + [vmem],
        out_specs=vmem,
        out_shape=jax.ShapeDtypeStruct((spm * piece * fold, bias.shape[1]), F32),
        scratch_shapes=[
            pltpu.VMEM((n_mp, spm, piece, lanes), BF),
            pltpu.SemaphoreType.DMA((n_mp,)),
        ],
        compiler_params=params(16),
        cost_estimate=cost(1e9, 4 * bias.size * piece),
        name="own",
    )(place, *features, bias)


def project_kernel(out_counts, spm, hc, place_ref, base_ref, *refs):
    n_mp = len(out_counts)
    att_refs, at = refs[:n_mp], n_mp
    own_ref, at = refs[at], at + 1
    half = own_ref.shape[0] // 2
    core = place_ref[1] % 2
    mine, mate = None, None
    for k, count in enumerate(out_counts):
        left = jnp.concatenate([att_refs[k][:, s * hc : (s + 1) * hc] for s in range(spm)], axis=0)
        if k == 0:
            pair = [
                [own_ref[pl.ds(pl.multiple_of(c * half, 128), half)]] for c in (core, 1 - core)
            ]
        else:
            pair = [[r[...] for r in refs[at : at + count]], [r[...] for r in refs[at + count : at + 2 * count]]]
            at += 2 * count
        sums = [
            jnp.concatenate(
                [lax.dot_general(left, w, NT, preferred_element_type=F32) for w in ws], axis=1
            )
            for ws in pair
        ]
        mine, mate = (sums[0], sums[1]) if mine is None else (mine + sums[0], mate + sums[1])
    total = jnp.concatenate(
        [jnp.where(core == 0, mine, mate), jnp.where(core == 0, mate, mine)], axis=1
    )
    gain_ref, shift_ref, res_ref, out_ref = refs[at:]
    value = base_ref[...] + total
    res_ref[...] = value
    mean = jnp.mean(value, axis=1, keepdims=True)
    value = value - mean
    spread = jnp.mean(value * value, axis=1, keepdims=True)
    out_ref[...] = (value * lax.rsqrt(spread + 1e-06) * gain_ref[...] + shift_ref[...]).astype(BF)


def project(place, base, hc, attended, out_weights, gain, shift, spm):
    n_mp = len(attended)
    weights = sum([sum(w, []) for w in out_weights], [])
    vmem = pl.BlockSpec(memory_space=pltpu.VMEM)
    return pl.pallas_call(
        functools.partial(project_kernel, [len(w[0]) for w in out_weights], spm, hc),
        in_specs=[pl.BlockSpec(memory_space=pltpu.SMEM)] + [vmem] * (n_mp + len(weights) + 3),
        out_specs=[vmem] * 2,
        out_shape=[jax.ShapeDtypeStruct(base.shape, F32), jax.ShapeDtypeStruct(base.shape, BF)],
        compiler_params=params(20),
        cost_estimate=cost(3e9, 16 * base.size),
        name="project",
    )(place, base, *attended, *weights, gain, shift)


def mlp_kernel(count, *refs):
    in_refs, (up_ref, bias_ref, down_ref), out_refs = refs[:count], refs[count : count + 3], refs[count + 4 :]
    rows = jnp.concatenate([r[...] for r in in_refs], axis=0)
    hidden_width = up_ref.shape[1]
    step = 256 if hidden_width % 256 == 0 else LANES
    hidden = []
    for c in range(0, hidden_width, step):
        at = slice(c, c + step)
        up = jnp.dot(rows, up_ref[:, at], preferred_element_type=F32) + bias_ref[:, at]
        hidden.append((0.5 * up * (1.0 + lax.erf(up * math.sqrt(0.5)))).astype(BF))
    hidden = jnp.concatenate(hidden, axis=1)
    each, width = out_refs[0].shape
    for c in range(0, width, 256):
        part = lax.dot_general(hidden, down_ref[c : c + 256], NT, preferred_element_type=F32)
        for i, ref in enumerate(out_refs):
            ref[:, c : c + 256] = part[i * each : (i + 1) * each].astype(BF)


def mlp(rows, outs, up, bias, down, after):
    width = down.shape[0]
    total = sum(r.shape[0] for r in rows)
    vmem = pl.BlockSpec(memory_space=pltpu.VMEM)
    return pl.pallas_call(
        functools.partial(mlp_kernel, len(rows)),
        in_specs=[vmem] * (len(rows) + 3) + [pl.BlockSpec(memory_space=pl.ANY)],
        out_specs=[vmem] * outs,
        out_shape=[jax.ShapeDtypeStruct((total // outs, width), BF)] * outs,
        compiler_params=params(20),
        cost_estimate=cost(total * up.size * 4, up.size * 4),
    )(*rows, up, bias, down, after)


def finish_kernel(adds, pieces, spm, place_ref, *refs):
    add_refs, (res_ref, bias_ref, lab_ref, out_ref) = refs[:adds], refs[adds:]
    each = res_ref.shape[0] // pieces
    labels = lab_ref[...].reshape(res_ref.shape[0], 1)
    turn = place_ref[1] % spm
    for s in range(pieces):
        at = slice(s * each, (s + 1) * each)
        value = res_ref[at] + bias_ref[...]
        for i in range(s, adds, pieces):
            value = value + add_refs[i][...].astype(F32)
        value = jnp.where(labels[at] >= 0, value, 0.0).astype(BF)
        out_ref[pl.ds(pl.multiple_of(jnp.bitwise_xor(turn, s) * each, 16), each)] = value


def finish(place, added, pieces, residual, bias, labels, spm):
    smem = pl.BlockSpec(memory_space=pltpu.SMEM)
    vmem = pl.BlockSpec(memory_space=pltpu.VMEM)
    return pl.pallas_call(
        functools.partial(finish_kernel, len(added), pieces, spm),
        in_specs=[smem] + [vmem] * (len(added) + 3),
        out_specs=vmem,
        out_shape=jax.ShapeDtypeStruct(residual.shape, BF),
        compiler_params=params(16),
        cost_estimate=cost(1e9, residual.size * 8),
        name="finish",
    )(place, *added, residual, bias, labels)


def hop(value, k, n):
    return lax.ppermute(value, "mp", [(i, i ^ k) for i in range(n)])


def after(value, *others):
    return lax.optimization_barrier((value, *others))[0]


def gather_blocks(value, n):
    if n != 4:
        return [[value]] + [[hop(value, k, n)] for k in range(1, n)]
    half = value.shape[0] // 2
    x = hop(value, 1, n)
    y = hop(value, 2, n)
    far = [hop(x[:half], 2, n), hop(y[half:], 1, n)]
    return [[value], [x], [y], far]


def plus(a, b):
    return (a.astype(F32) + b.astype(F32)).astype(BF)


def scatter_blocks(partials, n):
    own = list(partials[0])
    if n != 4 or len(own) != 2:
        for k in range(1, n):
            own += [hop(p, k, n) for p in partials[k]]
        return own
    far, x, y = partials[3], partials[1], partials[2]
    x0, y1 = hop(x[0], 1, n), hop(y[1], 2, n)
    first, second = hop(far[0], 1, n), hop(far[1], 2, n)
    y0, x1 = hop(plus(y[0], first), 2, n), hop(plus(x[1], second), 1, n)
    return own + [x0, x1, y0, y1]


def per_device(
    patches,
    position,
    keep,
    counts,
    offsets,
    ln_gain,
    ln_bias,
    w_qkv,
    b_qkv,
    w_o,
    b_o,
    w_up,
    b_up,
    w_down,
    b_down,
):
    local_images, _, width = patches.shape
    keep_most = keep.shape[1]
    n_dp, n_mp = lax.axis_size("dp"), lax.axis_size("mp")
    d, m = lax.axis_index("dp"), lax.axis_index("mp")
    images_here = local_images * n_mp
    per_slot = (images_here + n_dp - 1) // n_dp
    slot_rows = max(keep_most + 16, per_slot * keep_most * 5 // 8)
    pack_rows = slot_rows * n_dp
    spm = n_dp // n_mp
    feat = width // n_mp
    hc = w_qkv.shape[3]
    place = jnp.stack([m, d]).astype(jnp.int32)

    tokens = embed(place, patches, position, keep, n_mp)
    featured = [tokens[0]] + [hop(tokens[k], k, n_mp) for k in range(1, n_mp)]

    w_qkv, w_o = after(w_qkv, tokens[0]), after(w_o, tokens[0])
    mixed = jnp.concatenate([w_o[0].T, w_qkv[0, 0], w_qkv[0, 1], w_qkv[0, 2]], axis=1)
    mixed = lax.all_gather(mixed, "dp", axis=0, tiled=True)
    own = mixed[:, :hc]
    part = lax.dynamic_slice_in_dim(own, (d % 2) * (width // 2), width // 2)
    mate = [(i, i ^ 1) for i in range(n_dp)]
    out_weights = [[[own]]]
    for pieces in gather_blocks(part, n_mp)[1:]:
        out_weights.append([pieces, [lax.ppermute(p, "dp", mate) for p in pieces]])

    first_image = d * images_here
    group_counts = lax.dynamic_slice_in_dim(counts, first_image, images_here)
    group_offsets = lax.dynamic_slice_in_dim(offsets, first_image, images_here)
    shard_index = group_offsets // pack_rows
    base_row = shard_index * slot_rows + group_offsets - shard_index * pack_rows - d * slot_rows
    spot = jnp.arange(keep_most, dtype=jnp.int32)
    target = jnp.where(
        spot[None, :] < group_counts[:, None], base_row[:, None] + spot[None, :], pack_rows
    ).reshape(n_mp, 1, local_images * keep_most)
    fold = 2
    packed = pack(place, featured, target, n_dp, slot_rows, fold)
    half = n_dp // 2
    moved = [packed[0]]
    for i in range(1, n_dp):
        moved.append(lax.ppermute(packed[i], "dp", [(j, j ^ i) for j in range(n_dp)]))
    near = jnp.stack(moved[:half])
    far = jnp.stack(moved[half:])
    halves = [near, far]
    up = lax.all_gather(w_up[0], "dp", axis=0, tiled=True)
    down = lax.all_gather(w_down[0].T, "dp", axis=0, tiled=True)

    image_ids = jnp.arange(counts.shape[0], dtype=jnp.int32)
    slots = jnp.bitwise_xor(jnp.arange(n_dp, dtype=jnp.int32), d)
    packed_rows = d * pack_rows + slots[:, None] * slot_rows + jnp.arange(slot_rows, dtype=jnp.int32)
    packed_rows = packed_rows.reshape(pack_rows)
    inside = (packed_rows[:, None] >= offsets[None, :]) & (
        packed_rows[:, None] < (offsets + counts)[None, :]
    )
    labels = jnp.max(jnp.where(inside, image_ids[None, :] + 1, 0), axis=1) - 1
    labrow = labels.reshape(n_dp, 1, slot_rows)
    labcol = labels.reshape(n_dp, slot_rows, 1)

    moved = [gather_blocks(h, n_mp) for h in halves]
    gathered = [sum(pieces, []) for pieces in zip(*moved)]
    gain = ln_gain[0, 0].reshape(n_mp, 1, feat)
    shift = ln_bias[0, 0].reshape(n_mp, 1, feat)
    bias = b_qkv[0].reshape(1, 3 * hc)
    operands = (mixed, bias, gain, shift, labrow, labcol)
    count = n_dp // spm
    ahead = list(range(count // 2))
    prior = attend(place, moved[0], ahead, None, fold, hc, operands, spm)[0]
    attended = attend(
        place, gathered, list(range(count // 2, count)), prior, fold, hc, operands, spm
    )
    attended = [attended[0]] + [hop(attended[k], k, n_mp) for k in range(1, n_mp)]
    base = own_rows(place, gathered, fold, b_o, spm)
    residual, normed = project(
        place, base, hc, attended, out_weights, ln_gain[0, 1:2], ln_bias[0, 1:2], spm
    )
    blocks = gather_blocks(normed, n_mp)
    partials = [None] * n_mp
    last = normed
    groups = [[0], [2, 1], [3]] if n_mp == 4 else [[k] for k in range(n_mp)]
    for group in groups:
        outs = mlp(sum([blocks[k] for k in group], []), 2 * len(group), up, b_up, down, last)
        last = outs[0]
        for i, k in enumerate(group):
            partials[k] = outs[2 * i : 2 * i + 2]
    added = scatter_blocks(partials, n_mp)
    own_labels = lax.dynamic_slice_in_dim(labcol, jnp.bitwise_xor(m, d // spm) * spm, spm)
    return finish(place, added, 2, residual, b_down, own_labels, spm)


def solution(mesh):
    in_specs = (
        P(("dp", "mp"), None, None),
        P(),
        P(("dp", "mp"), None),
        P(),
        P(),
        P(),
        P(),
        P(None, None, "dp", "mp"),
        P(None, None, "mp"),
        P(None, "mp", "dp"),
        P(),
        P(None, "dp", "mp"),
        P(None, "mp"),
        P(None, "mp", "dp"),
        P(),
    )
    out_specs = P(("dp", "mp"), None)

    return jax.shard_map(
        per_device, mesh=mesh, in_specs=in_specs, out_specs=out_specs, check_vma=False
    )
```

time: 430 us -> 215 us (0.50)
  waiting for transfers between devices: 243 us -> 82.9 us
  matrix products: 56.8 us -> 0 us
  blocking collectives: 49.6 us -> 0 us
  Pallas kernels: 0 us -> 46.3 us
  starting transfers between devices: 9.26 us -> 42.9 us
  local copies, waits for them, and re-layouts: 40.6 us -> 24.1 us
  other arithmetic: 16.6 us -> 3.85 us
    all_gather x5 -> x3, waiting for transfers between devices: 125 us -> 0.01 us  [the longest x1 0.01 us: per_device(): mixed = lax.all_gather(mixed, 'dp', axis=0, tiled=True)]
    reduce_scatter x2 -> x0, waiting for transfers between devices: 87.6 us -> none  [project_sum(): lax.psum_scatter(partials.astype(jnp.bfloat16), 'mp', scatter_dimension=0...]
    ppermute x0 -> x39, waiting for transfers between devices: none -> 81.5 us  [the longest x28 63.6 us: hop(): return lax.ppermute(value, 'mp', [(i, i ^ k) for i in range(n)])]
    pallas_call x0 -> x10, Pallas kernels: none -> 46.3 us  [the longest x2 19.5 us: attend(): pl.pallas_call(functools.partial(attend_kernel, [len(g) for g in gathered...]
    dot_general x5 -> x0, matrix products: 45.8 us -> none  [the longest x2 27.2 us: fold_rows(): jnp.einsum('rd,tdc->trc', gathered, lax.all_gather(weight, 'dp', axis=1,...]
    ppermute x0 -> x39, starting transfers between devices: none -> 42.8 us  [the longest x28 32.2 us: hop(): return lax.ppermute(value, 'mp', [(i, i ^ k) for i in range(n)])]
    all_to_all x1 -> x0, blocking collectives: 32.4 us -> none  [per_device(): lax.all_to_all(buffer_rows, 'dp', split_axis=0, concat_axis=0, tiled=True)]
    all_to_all x2 -> x0, waiting for transfers between devices: 28.5 us -> none  [the longest x1 15.4 us: per_device(): lax.all_to_all(tokens.reshape(-1, column_count), 'mp', split_axis=1, conc...]
  transfers between devices with their start and end apart: 9 -> 42, of which waited for: 8 -> 16; matrix products, arithmetic and copies ran while one was open for 11% -> 7% of each run, Pallas kernels for 0% -> 17%
where the time goes in v1:
time: 215 us; the launch traced here: 214 us
  waiting for transfers between devices  82.9 us (39%)
  Pallas kernels  46.3 us (22%)
  starting transfers between devices  42.9 us (20%)
  local copies, waits for them, and re-layouts  24.1 us (11%)
  between operations  13.5 us (6%)
  other arithmetic  3.85 us (2%)
    ppermute x28, waiting for transfers between devices, hop(): return lax.ppermute(value, 'mp', [(i, i ^ k) for i in range(n)])  63.6 us
    ppermute x28, starting transfers between devices, hop(): return lax.ppermute(value, 'mp', [(i, i ^ k) for i in range(n)])  32.2 us
    pallas_call x2, Pallas kernels, attend(): pl.pallas_call(functools.partial(attend_kernel, [len(g) for g in gathered...  19.5 us
    ppermute x7, waiting for transfers between devices, per_device(): lax.ppermute(packed[i], 'dp', [(j, j ^ i) for j in range(n_dp)])  17.9 us
    unnamed x54, local copies, waits for them, and re-layouts  11.8 us
    pallas_call x3, Pallas kernels, mlp(): pl.pallas_call(functools.partial(mlp_kernel, len(rows)), in_specs=[vmem]...  11.4 us
    ppermute x7, starting transfers between devices, per_device(): lax.ppermute(packed[i], 'dp', [(j, j ^ i) for j in range(n_dp)])  10.1 us
    slice x8, local copies, waits for them, and re-layouts, gather_blocks(): far = [hop(x[:half], 2, n), hop(y[half:], 1, n)]  4.49 us
  transfers between devices with their start and end apart: 42, of which 16 were waited for; matrix products, arithmetic and copies ran while one was open for 7% of the time, Pallas kernels for 17%

profile of v1, /device:TPU:0, one launch (start us, length us, event | category | flops | bytes accessed | tf_op | source)
XLA Modules:
  0.0 213.6 jit_solution(17126026182748786691)
XLA Ops:
  7.4 2.5 %copy-done.19 = bf16[8,256,1280]{2,1,0:T(8,128)(2,1)S(1)} copy-done((bf16[8,256,1280]{2,1,0:T(8,128)(2,1)S(1)}, bf16[8,256,1280]{2,1,0:T(8,128)(2,1)}, u32[]{:S(2)}) %copy-start.19) | copy-done | bytes 5242904
  9.9 1.1 copy-done.20
  11.0 3.3 %embed.1 = (bf16[320,512]{1,0:T(8,128)(2,1)S(1)}, bf16[320,512]{1,0:T(8,128)(2,1)S(1)}, bf16[320,512]{1,0:T(8,128)(2,1)S(1)}, bf16[320,512]{1,0:T(8,128)(2,1)S(1)}) custom-call(s32[2]{0:T(128)S(1)} %pad_add_fusion.place_ref, s32[4,1,128]{2,1,0:T(1,128)S(1)} %reshape.142.keep_ref, bf16[8,256,1280]{2,1,0:T(8,128)(2,1)S(1)} %copy-done.19, ...), custom_call_target="tpu_custom_call" | custom-call | flops 4000000000 | bytes 5242880 | tf_op jit(solution)/shard_map/embed/pallas_call | solution.py:57
  14.3 1.0 concatenate.3
  16.8 3.0 %collective-permute-start = (bf16[320,512]{1,0:T(8,128)(2,1)S(1)}, bf16[320,512]{1,0:T(8,128)(2,1)S(1)}, u32[]{:S(2)}, u32[]{:S(2)}) collective-permute-start(bf16[320,512]{1,0:T(8,128)(2,1)S(1)} %get-tuple-element.34), channel_id=1, source_target_pairs={{0,1},{1,0},{2,3},{3,2},{4,5},{5,4},{6,7},{7,6},{8,9},{9,8},{10,11... | collective-permute-start | bytes 983048 | tf_op jit(solution)/shard_map/ppermute | solution.py:408
  19.9 1.5 collective-permute-start.1
  22.2 1.2 slice_bitcast_fusion.3
  23.4 5.0 %collective-permute-done.refs_1_ = bf16[320,512]{1,0:T(8,128)(2,1)S(1)} collective-permute-done((bf16[320,512]{1,0:T(8,128)(2,1)S(1)}, bf16[320,512]{1,0:T(8,128)(2,1)S(1)}, u32[]{:S(2)}, u32[]{:S(2)}) %collective-permute-start) | collective-permute-done | bytes 327712 | tf_op jit(solution)/shard_map/ppermute | solution.py:408
  28.4 7.6 %collective-permute-done.1.refs_2_ = bf16[320,512]{1,0:T(8,128)(2,1)S(1)} collective-permute-done((bf16[320,512]{1,0:T(8,128)(2,1)S(1)}, bf16[320,512]{1,0:T(8,128)(2,1)S(1)}, u32[]{:S(2)}, u32[]{:S(2)}) %collective-permute-start.1) | collective-permute-done | bytes 327712 | tf_op jit(solution)/shard_map/ppermute | solution.py:408
  36.0 3.5 %pack.1 = (bf16[80,640]{1,0:T(8,128)(2,1)S(1)}, bf16[80,640]{1,0:T(8,128)(2,1)S(1)}, bf16[80,640]{1,0:T(8,128)(2,1)S(1)}, bf16[80,640]{1,0:T(8,128)(2,1)S(1)}, b...) custom-call(s32[2]{0:T(128)S(1)} %pad_add_fusion.place_ref, ...), custom_call_target="tpu_custom_call" | custom-call | flops 4000000000 | bytes 1310720 | tf_op jit(solution)/shard_map/pack/pallas_call | solution.py:104
  39.6 1.7 collective-permute-start.4
  41.5 2.6 %collective-permute-start.6 = (bf16[80,640]{1,0:T(8,128)(2,1)S(1)}, bf16[80,640]{1,0:T(8,128)(2,1)S(1)}, u32[]{:S(2)}, u32[]{:S(2)}) collective-permute-start(bf16[80,640]{1,0:T(8,128)(2,1)S(1)} %get-tuple-element.41), channel_id=1, source_target_pairs={{0,16},{4,20},{8,24},{12,28},{16,0},{20,4},{24,8},{28,12},{1,17},{... | collective-permute-start | bytes 307208 | tf_op jit(solution)/shard_map/ppermute | solution.py:499
  44.1 3.6 %collective-permute-start.8 = (bf16[80,640]{1,0:T(8,128)(2,1)S(1)}, bf16[80,640]{1,0:T(8,128)(2,1)S(1)}, u32[]{:S(2)}, u32[]{:S(2)}) collective-permute-start(bf16[80,640]{1,0:T(8,128)(2,1)S(1)} %get-tuple-element.43), channel_id=1, source_target_pairs={{0,24},{4,28},{8,16},{12,20},{16,8},{20,12},{24,0},{28,4},{1,25},{... | collective-permute-start | bytes 307208 | tf_op jit(solution)/shard_map/ppermute | solution.py:499
  47.7 7.9 %collective-permute-done.4 = bf16[80,640]{1,0:T(8,128)(2,1)S(1)} collective-permute-done((bf16[80,640]{1,0:T(8,128)(2,1)S(1)}, bf16[80,640]{1,0:T(8,128)(2,1)S(1)}, u32[]{:S(2)}, u32[]{:S(2)}) %collective-permute-start.4) | collective-permute-done | bytes 102432 | tf_op jit(solution)/shard_map/ppermute | solution.py:499
  55.6 2.0 collective-permute-start.9
  57.6 3.6 %collective-permute-done.5 = bf16[80,640]{1,0:T(8,128)(2,1)S(1)} collective-permute-done((bf16[80,640]{1,0:T(8,128)(2,1)S(1)}, bf16[80,640]{1,0:T(8,128)(2,1)S(1)}, u32[]{:S(2)}, u32[]{:S(2)}) %collective-permute-start.5) | collective-permute-done | bytes 102432 | tf_op jit(solution)/shard_map/ppermute | solution.py:499
  61.3 1.4 collective-permute-start.10
  63.4 3.8 %collective-permute-done.8 = bf16[80,640]{1,0:T(8,128)(2,1)S(1)} collective-permute-done((bf16[80,640]{1,0:T(8,128)(2,1)S(1)}, bf16[80,640]{1,0:T(8,128)(2,1)S(1)}, u32[]{:S(2)}, u32[]{:S(2)}) %collective-permute-start.8) | collective-permute-done | bytes 102432 | tf_op jit(solution)/shard_map/ppermute | solution.py:499
  67.2 2.5 %collective-permute-done.9 = bf16[80,640]{1,0:T(8,128)(2,1)S(1)} collective-permute-done((bf16[80,640]{1,0:T(8,128)(2,1)S(1)}, bf16[80,640]{1,0:T(8,128)(2,1)S(1)}, u32[]{:S(2)}, u32[]{:S(2)}) %collective-permute-start.9) | collective-permute-done | bytes 102432 | tf_op jit(solution)/shard_map/ppermute | solution.py:499
  69.8 1.5 collective-permute-start.11
  71.3 1.5 collective-permute-start.13
  74.1 1.5 collective-permute-start.14
  78.2 1.3 reduce
  79.5 1.4 reshape_squeeze.9.refs_6_.refs_11_
  80.8 1.3 collective-permute-done.11.refs_3_
  82.9 1.5 collective-permute-start.16
  85.1 1.5 collective-permute-start.17
  86.5 1.3 slice.68.refs_4_
  88.5 1.0 collective-permute-start.23
  89.5 1.9 copy-done.6
  92.8 9.8 %attend.2.refs_16_ = bf16[2,160,640]{2,1,0:T(8,128)(2,1)S(1)} custom-call(s32[2]{0:T(128)S(1)} %copy-done.17, bf16[4,80,640]{2,1,0:T(8,128)(2,1)S(1)} %pad_maximum_fusion.refs_0_, bf16[4,80,640]{2,1,0:T(8,128)(2,1)S(1)} %collective-permute-done.10.refs_2_.refs_1_, bf16[4,80,640]{2,1,0:T(8,128)(2,1)S(1)} %collective-permute-done.12.refs_4_.refs_2_, ...), custom_call_target="tpu_custom_call" | custom-call | flops 8000000000 | bytes 6553600 | tf_op jit(solution)/shard_map/attend/pallas_call | solution.py:239
  102.6 9.8 %attend.3 = (bf16[160,640]{1,0:T(8,128)(2,1)S(1)}, bf16[160,640]{1,0:T(8,128)(2,1)S(1)}, bf16[160,640]{1,0:T(8,128)(2,1)S(1)}, bf16[160,640]{1,0:T(8,128)(2,1)S(1)}) custom-call(s32[2]{0:T(128)S(1)} %copy-done.17, bf16[4,80,640]{2,1,0:T(8,128)(2,1)S(1)} %pad_maximum_fusion.refs_0_, bf16[4,80,640]{2,1,0:T(8,128)(2,1)S(1)} %pad_maximum_fusion.1.refs_1_, ...), custom_call_target="tpu_custom_call" | custom-call | flops 8000000000 | bytes 6553600 | tf_op jit(solution)/shard_map/attend/pallas_call | solution.py:239
  112.4 1.1 collective-permute-start.18
  113.5 1.5 collective-permute-start.19
  115.6 1.1 collective-permute-start.26
  116.7 3.6 %collective-permute-done.18.refs_1_ = bf16[160,640]{1,0:T(8,128)(2,1)S(1)} collective-permute-done((bf16[160,640]{1,0:T(8,128)(2,1)S(1)}, bf16[160,640]{1,0:T(8,128)(2,1)S(1)}, u32[]{:S(2)}, u32[]{:S(2)}) %collective-permute-start.18) | collective-permute-done | bytes 204832 | tf_op jit(solution)/shard_map/ppermute | solution.py:408
  120.9 1.5 collective-permute-start.20
  122.4 1.1 collective-permute-done.25.refs_9_
  124.0 2.4 %own.1.base_ref = f32[320,1280]{1,0:T(8,128)S(1)} custom-call(s32[2]{0:T(128)S(1)} %copy-done.17, bf16[4,80,640]{2,1,0:T(8,128)(2,1)S(1)} %pad_maximum_fusion.refs_0_, bf16[4,80,640]{2,1,0:T(8,128)(2,1)S(1)} %pad_maximum_fusion.1.refs_1_, bf16[4,80,640]{2,1,0:T(8,128)(2,1)S(1)} %collective-permute-done.10.refs_2_.refs_1_, ...), custom_call_target="tpu_custom_call" | custom-call | flops 1000000000 | bytes 409600 | tf_op jit(solution)/shard_map/own/pallas_call | solution.py:280
  126.5 2.3 %collective-permute-done.20.refs_3_ = bf16[160,640]{1,0:T(8,128)(2,1)S(1)} collective-permute-done((bf16[160,640]{1,0:T(8,128)(2,1)S(1)}, bf16[160,640]{1,0:T(8,128)(2,1)S(1)}, u32[]{:S(2)}, u32[]{:S(2)}) %collective-permute-start.20) | collective-permute-done | bytes 204832 | tf_op jit(solution)/shard_map/ppermute | solution.py:408
  128.8 3.6 %project.1 = (f32[320,1280]{1,0:T(8,128)S(1)}, bf16[320,1280]{1,0:T(8,128)(2,1)S(1)}) custom-call(s32[2]{0:T(128)S(1)} %copy-done.17, f32[320,1280]{1,0:T(8,128)S(1)} %own.1.base_ref, bf16[160,640]{1,0:T(8,128)(2,1)S(1)} %get-tuple-element.47.refs_0_, bf16[160,640]{1,0:T(8,128)(2,1)S(1)} %collective-permute-done.18.refs_1_, ...), custom_call_target="tpu_custom_call" | custom-call | flops 3000000000 | bytes 6553600 | tf_op jit(solution)/shard_map/project/pallas_call | solution.py:336
  132.3 0.9 collective-permute-start.30
  133.2 1.3 collective-permute-start.29
  134.5 17.3 %collective-permute-done.30.refs_1_ = bf16[320,1280]{1,0:T(8,128)(2,1)S(1)} collective-permute-done((bf16[320,1280]{1,0:T(8,128)(2,1)S(1)}, bf16[320,1280]{1,0:T(8,128)(2,1)S(1)}, u32[]{:S(2)}, u32[]{:S(2)}) %collective-permute-start.30) | collective-permute-done | bytes 819232 | tf_op jit(solution)/shard_map/ppermute | solution.py:408
  152.6 1.1 collective-permute-start.32
  154.7 1.0 collective-permute-start.33
  155.8 1.9 copy-done
  157.7 1.9 copy-done.2
  159.6 2.5 %shard_map.145 = (bf16[160,1280]{1,0:T(8,128)(2,1)S(1)}, bf16[160,1280]{1,0:T(8,128)(2,1)S(1)}) custom-call(bf16[320,1280]{1,0:T(8,128)(2,1)S(1)} %get-tuple-element.51.refs_0_.refs_4_, bf16[1280,1280]{1,0:T(8,128)(2,1)S(1)} %bitcast.27, f32[1,1280]{1,0:T(1,128)S(1)} %copy-done.11, bf16[1280,1280]{1,0:T(8,128)(2,1)S(1)} %copy-done, ...), custom_call_target="tpu_custom_call" | custom-call | flops 2097152000 | bytes 6553600 | tf_op jit(solution)/shard_map/pallas_call | solution.py:369
  162.9 5.4 %shard_map.146 = (bf16[160,1280]{1,0:T(8,128)(2,1)S(1)}, bf16[160,1280]{1,0:T(8,128)(2,1)}, bf16[160,1280]{1,0:T(8,128)(2,1)}, bf16[160,1280]{1,0:T(8,128)(2,1)S(1)}) custom-call(bf16[320,1280]{1,0:T(8,128)(2,1)S(1)} %copy-done.10, bf16[320,1280]{1,0:T(8,128)(2,1)S(1)} %copy-done.8, bf16[1280,1280]{1,0:T(8,128)(2,1)S(1)} %bitcast.28, ...), custom_call_target="tpu_custom_call" | custom-call | flops 4194304000 | bytes 6553600 | tf_op jit(solution)/shard_map/pallas_call | solution.py:369
  168.3 3.6 %shard_map.147 = (bf16[160,1280]{1,0:T(8,128)(2,1)S(1)}, bf16[160,1280]{1,0:T(8,128)(2,1)S(1)}) custom-call(bf16[160,1280]{1,0:T(8,128)(2,1)} %collective-permute-done.32.refs_0_, bf16[160,1280]{1,0:T(8,128)(2,1)} %collective-permute-done.33.refs_1_, bf16[1280,1280]{1,0:T(8,128)(2,1)S(1)} %bitcast.29, f32[1,1280]{1,0:T(1,128)S(1)} %copy-done.11, ...), custom_call_target="tpu_custom_call" | custom-call | flops 2097152000 | bytes 6553600 | tf_op jit(solution)/shard_map/pallas_call | solution.py:369
  171.9 1.1 collective-permute-start.36
  173.0 1.0 collective-permute-start.31
  174.0 0.9 collective-permute-start.38
  174.9 1.2 collective-permute-start.34
  176.0 8.3 %collective-permute-done.36 = bf16[160,1280]{1,0:T(8,128)(2,1)S(1)} collective-permute-done((bf16[160,1280]{1,0:T(8,128)(2,1)S(1)}, bf16[160,1280]{1,0:T(8,128)(2,1)S(1)}, u32[]{:S(2)}, u32[]{:S(2)}) %collective-permute-start.36) | collective-permute-done | bytes 409632 | tf_op jit(solution)/shard_map/ppermute | solution.py:408
  184.3 0.9 add_convert_fusion
  185.2 0.9 collective-permute-start.37
  186.0 9.3 %collective-permute-done.34 = bf16[160,1280]{1,0:T(8,128)(2,1)S(1)} collective-permute-done((bf16[160,1280]{1,0:T(8,128)(2,1)S(1)}, bf16[160,1280]{1,0:T(8,128)(2,1)S(1)}, u32[]{:S(2)}, u32[]{:S(2)}) %collective-permute-start.34) | collective-permute-done | bytes 409632 | tf_op jit(solution)/shard_map/ppermute | solution.py:408
  195.3 0.8 add_convert_fusion.1
  196.1 1.0 collective-permute-start.35
  197.2 3.4 %collective-permute-done.37.refs_4_ = bf16[160,1280]{1,0:T(8,128)(2,1)} collective-permute-done((bf16[160,1280]{1,0:T(8,128)(2,1)}, bf16[160,1280]{1,0:T(8,128)(2,1)}, u32[]{:S(2)}, u32[]{:S(2)}) %collective-permute-start.37) | collective-permute-done | bytes 409632 | tf_op jit(solution)/shard_map/ppermute | solution.py:408
  200.6 3.8 %collective-permute-done.35.refs_3_ = bf16[160,1280]{1,0:T(8,128)(2,1)} collective-permute-done((bf16[160,1280]{1,0:T(8,128)(2,1)}, bf16[160,1280]{1,0:T(8,128)(2,1)}, u32[]{:S(2)}, u32[]{:S(2)}) %collective-permute-start.35) | collective-permute-done | bytes 409632 | tf_op jit(solution)/shard_map/ppermute | solution.py:408
  204.4 2.6 %finish.1 = bf16[320,1280]{1,0:T(8,128)(2,1)} custom-call(s32[2]{0:T(128)S(1)} %copy-done.18, bf16[160,1280]{1,0:T(8,128)(2,1)S(1)} %get-tuple-element.52.refs_5_.refs_0_, bf16[160,1280]{1,0:T(8,128)(2,1)S(1)} %copy-done.5, bf16[160,1280]{1,0:T(8,128)(2,1)S(1)} %collective-permute-done.31.refs_2_, bf16[160,1280]{1,0:T(8,128)(2,1)} %collective-permute-done.35.refs_3_, ...), custom_call_target="tpu_custom_call" | custom-call | flops 1000000000 | bytes 3276800 | tf_op jit(solution)/shard_map/finish/pallas_call | solution.py:396
  (131 shorter events, 16.0 us)
Async XLA Ops:
  6.5 80.0 %all-gather.5.cloned.1.call-start = ((), (), s32[]{:S(2)}) async-start(), calls=%async_computation | async-start | bytes 3686400 | tf_op jit(solution)/shard_map/all_gather | solution.py:477
  7.4 2.5 %copy-start.19 = (bf16[8,256,1280]{2,1,0:T(8,128)(2,1)S(1)}, bf16[8,256,1280]{2,1,0:T(8,128)(2,1)}, u32[]{:S(2)}) copy-start(bf16[8,256,1280]{2,1,0:T(8,128)(2,1)} %patches_ref.1) | copy-start | bytes 15728644
  10.9 25.1 %copy-start.16 = (s32[2]{0:T(128)}, s32[2]{0:T(128)S(1)}, u32[]{:S(2)}) copy-start(s32[2]{0:T(128)S(1)} %pad_add_fusion.place_ref) | copy-start | bytes 28
  11.0 3.3 %copy-start.21 = (bf16[1,3,160,320]{3,2,1,0:T(8,128)(2,1)S(1)}, bf16[1,3,160,320]{3,2,1,0:T(8,128)(2,1)}, u32[]{:S(2)}) copy-start(bf16[1,3,160,320]{3,2,1,0:T(8,128)(2,1)} %param.22) | copy-start | bytes 921604
  11.0 3.4 %copy-start.22 = (bf16[1,320,160]{1,2,0:T(8,128)(2,1)S(1)}, bf16[1,320,160]{1,2,0:T(8,128)(2,1)}, u32[]{:S(2)}) copy-start(bf16[1,320,160]{1,2,0:T(8,128)(2,1)} %param.24) | copy-start | bytes 307204
  14.2 7.2 %copy-start.25 = (s32[256]{0:T(256)S(1)}, s32[256]{0:T(256)}, u32[]{:S(2)}) copy-start(s32[256]{0:T(256)} %param.19) | copy-start | bytes 3076
  14.2 7.5 %copy-start.26 = (s32[256]{0:T(256)S(1)}, s32[256]{0:T(256)}, u32[]{:S(2)}) copy-start(s32[256]{0:T(256)} %param.18) | copy-start | bytes 3076
  14.3 7.9 %copy-start.23 = (f32[1,2,1280]{2,1,0:T(2,128)S(1)}, f32[1,2,1280]{2,1,0:T(2,128)}, u32[]{:S(2)}) copy-start(f32[1,2,1280]{2,1,0:T(2,128)} %param.21) | copy-start | bytes 30724
  14.3 7.9 %copy-start.24 = (f32[1,2,1280]{2,1,0:T(2,128)S(1)}, f32[1,2,1280]{2,1,0:T(2,128)}, u32[]{:S(2)}) copy-start(f32[1,2,1280]{2,1,0:T(2,128)} %param.20) | copy-start | bytes 30724
  15.3 140.4 %all-gather.7.cloned.1.call-start = ((), (), s32[]{:S(2)}) async-start(), calls=%async_computation.1 | async-start | bytes 3686400 | tf_op jit(solution)/shard_map/all_gather | solution.py:504
  16.1 139.7 %all-gather.9.cloned.1.call-start = ((), (), s32[]{:S(2)}) async-start(), calls=%async_computation.2 | async-start | bytes 3686400 | tf_op jit(solution)/shard_map/all_gather | solution.py:503
  16.8 11.6 %collective-permute-start = (bf16[320,512]{1,0:T(8,128)(2,1)S(1)}, bf16[320,512]{1,0:T(8,128)(2,1)S(1)}, u32[]{:S(2)}, u32[]{:S(2)}) collective-permute-start(bf16[320,512]{1,0:T(8,128)(2,1)S(1)} %get-tuple-element.34), channel_id=1, source_target_pairs={{0,1},{1,0},{2,3},{3,2},{4,5},{5,4},{6,7},{7,6},{8,9},{9,8},{10,11... | collective-permute-start | bytes 983048 | tf_op jit(solution)/shard_map/ppermute | solution.py:408
  19.9 16.2 %collective-permute-start.1 = (bf16[320,512]{1,0:T(8,128)(2,1)S(1)}, bf16[320,512]{1,0:T(8,128)(2,1)S(1)}, u32[]{:S(2)}, u32[]{:S(2)}) collective-permute-start(bf16[320,512]{1,0:T(8,128)(2,1)S(1)} %get-tuple-element.35), channel_id=1, source_target_pairs={{0,2},{1,3},{2,0},{3,1},{4,6},{5,7},{6,4},{7,5},{8,10},{9,11},{10,... | collective-permute-start | bytes 983048 | tf_op jit(solution)/shard_map/ppermute | solution.py:408
  21.4 14.7 %collective-permute-start.2 = (bf16[320,512]{1,0:T(8,128)(2,1)S(1)}, bf16[320,512]{1,0:T(8,128)(2,1)S(1)}, u32[]{:S(2)}, u32[]{:S(2)}) collective-permute-start(bf16[320,512]{1,0:T(8,128)(2,1)S(1)} %get-tuple-element.36), channel_id=1, source_target_pairs={{0,3},{1,2},{2,1},{3,0},{4,7},{5,6},{6,5},{7,4},{8,11},{9,10},{10,... | collective-permute-start | bytes 983048 | tf_op jit(solution)/shard_map/ppermute | solution.py:408
  39.5 4.5 %collective-permute-start.3 = (bf16[80,640]{1,0:T(8,128)(2,1)S(1)}, bf16[80,640]{1,0:T(8,128)(2,1)S(1)}, u32[]{:S(2)}, u32[]{:S(2)}) collective-permute-start(bf16[80,640]{1,0:T(8,128)(2,1)S(1)} %get-tuple-element.38), channel_id=1, source_target_pairs={{0,4},{4,0},{8,12},{12,8},{16,20},{20,16},{24,28},{28,24},{1,5},{5... | collective-permute-start | bytes 307208 | tf_op jit(solution)/shard_map/ppermute | solution.py:499
  39.6 16.0 %collective-permute-start.4 = (bf16[80,640]{1,0:T(8,128)(2,1)S(1)}, bf16[80,640]{1,0:T(8,128)(2,1)S(1)}, u32[]{:S(2)}, u32[]{:S(2)}) collective-permute-start(bf16[80,640]{1,0:T(8,128)(2,1)S(1)} %get-tuple-element.39), channel_id=1, source_target_pairs={{0,8},{4,12},{8,0},{12,4},{16,24},{20,28},{24,16},{28,20},{1,9},{5... | collective-permute-start | bytes 307208 | tf_op jit(solution)/shard_map/ppermute | solution.py:499
  41.3 19.9 %collective-permute-start.5 = (bf16[80,640]{1,0:T(8,128)(2,1)S(1)}, bf16[80,640]{1,0:T(8,128)(2,1)S(1)}, u32[]{:S(2)}, u32[]{:S(2)}) collective-permute-start(bf16[80,640]{1,0:T(8,128)(2,1)S(1)} %get-tuple-element.40), channel_id=1, source_target_pairs={{0,12},{4,8},{8,4},{12,0},{16,28},{20,24},{24,20},{28,16},{1,13},{... | collective-permute-start | bytes 307208 | tf_op jit(solution)/shard_map/ppermute | solution.py:499
  41.5 21.2 %collective-permute-start.6 = (bf16[80,640]{1,0:T(8,128)(2,1)S(1)}, bf16[80,640]{1,0:T(8,128)(2,1)S(1)}, u32[]{:S(2)}, u32[]{:S(2)}) collective-permute-start(bf16[80,640]{1,0:T(8,128)(2,1)S(1)} %get-tuple-element.41), channel_id=1, source_target_pairs={{0,16},{4,20},{8,24},{12,28},{16,0},{20,4},{24,8},{28,12},{1,17},{... | collective-permute-start | bytes 307208 | tf_op jit(solution)/shard_map/ppermute | solution.py:499
  44.1 19.4 %collective-permute-start.7 = (bf16[80,640]{1,0:T(8,128)(2,1)S(1)}, bf16[80,640]{1,0:T(8,128)(2,1)S(1)}, u32[]{:S(2)}, u32[]{:S(2)}) collective-permute-start(bf16[80,640]{1,0:T(8,128)(2,1)S(1)} %get-tuple-element.42), channel_id=1, source_target_pairs={{0,20},{4,16},{8,28},{12,24},{16,4},{20,0},{24,12},{28,8},{1,21},{... | collective-permute-start | bytes 307208 | tf_op jit(solution)/shard_map/ppermute | solution.py:499
  44.1 23.1 %collective-permute-start.8 = (bf16[80,640]{1,0:T(8,128)(2,1)S(1)}, bf16[80,640]{1,0:T(8,128)(2,1)S(1)}, u32[]{:S(2)}, u32[]{:S(2)}) collective-permute-start(bf16[80,640]{1,0:T(8,128)(2,1)S(1)} %get-tuple-element.43), channel_id=1, source_target_pairs={{0,24},{4,28},{8,16},{12,20},{16,8},{20,12},{24,0},{28,4},{1,25},{... | collective-permute-start | bytes 307208 | tf_op jit(solution)/shard_map/ppermute | solution.py:499
  55.6 14.1 %collective-permute-start.9 = (bf16[80,640]{1,0:T(8,128)(2,1)S(1)}, bf16[80,640]{1,0:T(8,128)(2,1)S(1)}, u32[]{:S(2)}, u32[]{:S(2)}) collective-permute-start(bf16[80,640]{1,0:T(8,128)(2,1)S(1)} %get-tuple-element.44), channel_id=1, source_target_pairs={{0,28},{4,24},{8,20},{12,16},{16,12},{20,8},{24,4},{28,0},{1,29},{... | collective-permute-start | bytes 307208 | tf_op jit(solution)/shard_map/ppermute | solution.py:499
  61.3 12.1 %collective-permute-start.10 = (bf16[4,80,640]{2,1,0:T(8,128)(2,1)S(1)}, bf16[4,80,640]{2,1,0:T(8,128)(2,1)S(1)}, u32[]{:S(2)}, u32[]{:S(2)}) collective-permute-start(bf16[4,80,640]{2,1,0:T(8,128)(2,1)S(1)} %pad_maximum_fusion.refs_0_), channel_id=1, source_target_pairs={{0,1},{1,0},{2,3},{3,2},{4,5},{5,4},{6,7},{7,6},{8,9},{9,8},{10,11... | collective-permute-start | bytes 1228808 | tf_op jit(solution)/shard_map/ppermute | solution.py:408
  62.7 12.9 %collective-permute-start.12 = (bf16[4,80,640]{2,1,0:T(8,128)(2,1)S(1)}, bf16[4,80,640]{2,1,0:T(8,128)(2,1)S(1)}, u32[]{:S(2)}, u32[]{:S(2)}) collective-permute-start(bf16[4,80,640]{2,1,0:T(8,128)(2,1)S(1)} %pad_maximum_fusion.refs_0_), channel_id=1, source_target_pairs={{0,2},{1,3},{2,0},{3,1},{4,6},{5,7},{6,4},{7,5},{8,10},{9,11},{10,... | collective-permute-start | bytes 1228808 | tf_op jit(solution)/shard_map/ppermute | solution.py:408
  69.8 12.4 %collective-permute-start.11 = (bf16[4,80,640]{2,1,0:T(8,128)(2,1)S(1)}, bf16[4,80,640]{2,1,0:T(8,128)(2,1)S(1)}, u32[]{:S(2)}, u32[]{:S(2)}) collective-permute-start(bf16[4,80,640]{2,1,0:T(8,128)(2,1)S(1)} %pad_maximum_fusion.1.refs_1_), channel_id=1, source_target_pairs={{0,1},{1,0},{2,3},{3,2},{4,5},{5,4},{6,7},{7,6},{8,9},{9,8},{10,11... | collective-permute-start | bytes 1228808 | tf_op jit(solution)/shard_map/ppermute | solution.py:408
  71.3 13.0 %collective-permute-start.13 = (bf16[4,80,640]{2,1,0:T(8,128)(2,1)S(1)}, bf16[4,80,640]{2,1,0:T(8,128)(2,1)S(1)}, u32[]{:S(2)}, u32[]{:S(2)}) collective-permute-start(bf16[4,80,640]{2,1,0:T(8,128)(2,1)S(1)} %pad_maximum_fusion.1.refs_1_), channel_id=1, source_target_pairs={{0,2},{1,3},{2,0},{3,1},{4,6},{5,7},{6,4},{7,5},{8,10},{9,11},{10,... | collective-permute-start | bytes 1228808 | tf_op jit(solution)/shard_map/ppermute | solution.py:408
  74.1 14.5 %collective-permute-start.14 = (bf16[2,80,640]{2,1,0:T(8,128)(2,1)}, bf16[2,80,640]{2,1,0:T(8,128)(2,1)S(1)}, u32[]{:S(2)}, u32[]{:S(2)}) collective-permute-start(bf16[2,80,640]{2,1,0:T(8,128)(2,1)} %slice.64), channel_id=1, source_target_pairs={{0,2},{1,3},{2,0},{3,1},{4,6},{5,7},{6,4},{7,5},{8,10},{9,11},{10,... | collective-permute-start | bytes 614408 | tf_op jit(solution)/shard_map/ppermute | solution.py:408
  76.2 13.3 %collective-permute-start.15 = (bf16[2,80,640]{2,1,0:T(8,128)(2,1)}, bf16[2,80,640]{2,1,0:T(8,128)(2,1)S(1)}, u32[]{:S(2)}, u32[]{:S(2)}) collective-permute-start(bf16[2,80,640]{2,1,0:T(8,128)(2,1)} %slice.65), channel_id=1, source_target_pairs={{0,1},{1,0},{2,3},{3,2},{4,5},{5,4},{6,7},{7,6},{8,9},{9,8},{10,11... | collective-permute-start | bytes 614408 | tf_op jit(solution)/shard_map/ppermute | solution.py:408
  82.9 19.7 %collective-permute-start.16 = (bf16[2,80,640]{2,1,0:T(8,128)(2,1)}, bf16[2,80,640]{2,1,0:T(8,128)(2,1)}, u32[]{:S(2)}, u32[]{:S(2)}) collective-permute-start(bf16[2,80,640]{2,1,0:T(8,128)(2,1)} %slice.66), channel_id=1, source_target_pairs={{0,2},{1,3},{2,0},{3,1},{4,6},{5,7},{6,4},{7,5},{8,10},{9,11},{10,... | collective-permute-start | bytes 614408 | tf_op jit(solution)/shard_map/ppermute | solution.py:408
  85.1 17.6 %collective-permute-start.17 = (bf16[2,80,640]{2,1,0:T(8,128)(2,1)}, bf16[2,80,640]{2,1,0:T(8,128)(2,1)}, u32[]{:S(2)}, u32[]{:S(2)}) collective-permute-start(bf16[2,80,640]{2,1,0:T(8,128)(2,1)} %slice.67), channel_id=1, source_target_pairs={{0,1},{1,0},{2,3},{3,2},{4,5},{5,4},{6,7},{7,6},{8,9},{9,8},{10,11... | collective-permute-start | bytes 614408 | tf_op jit(solution)/shard_map/ppermute | solution.py:408
  87.9 27.1 %collective-permute-start.21 = (bf16[640,320]{1,0:T(8,128)(2,1)S(1)}, bf16[640,320]{1,0:T(8,128)(2,1)S(1)}, u32[]{:S(2)}, u32[]{:S(2)}) collective-permute-start(bf16[640,320]{1,0:T(8,128)(2,1)S(1)} %constant_dynamic-slice_fusion.1), channel_id=1, source_target_pairs={{0,1},{1,0},{2,3},{3,2},{4,5},{5,4},{6,7},{7,6},{8,9},{9,8},{10,11... | collective-permute-start | bytes 1228808 | tf_op jit(solution)/shard_map/ppermute | solution.py:408
  88.5 27.1 %collective-permute-start.23 = (bf16[640,320]{1,0:T(8,128)(2,1)S(1)}, bf16[640,320]{1,0:T(8,128)(2,1)S(1)}, u32[]{:S(2)}, u32[]{:S(2)}) collective-permute-start(bf16[640,320]{1,0:T(8,128)(2,1)S(1)} %constant_dynamic-slice_fusion.1), channel_id=1, source_target_pairs={{0,2},{1,3},{2,0},{3,1},{4,6},{5,7},{6,4},{7,5},{8,10},{9,11},{10,... | collective-permute-start | bytes 1228808 | tf_op jit(solution)/shard_map/ppermute | solution.py:408
  89.5 1.9 copy-start.6
  102.6 21.4 %copy-start.13 = (f32[1,1280]{1,0:T(1,128)S(1)}, f32[1,1280]{1,0:T(1,128)}, u32[]{:S(2)}) copy-start(f32[1,1280]{1,0:T(1,128)} %refs_10_.1) | copy-start | bytes 15364
  112.4 8.0 %collective-permute-start.18 = (bf16[160,640]{1,0:T(8,128)(2,1)S(1)}, bf16[160,640]{1,0:T(8,128)(2,1)S(1)}, u32[]{:S(2)}, u32[]{:S(2)}) collective-permute-start(bf16[160,640]{1,0:T(8,128)(2,1)S(1)} %get-tuple-element.48), channel_id=1, source_target_pairs={{0,1},{1,0},{2,3},{3,2},{4,5},{5,4},{6,7},{7,6},{8,9},{9,8},{10,11... | collective-permute-start | bytes 614408 | tf_op jit(solution)/shard_map/ppermute | solution.py:408
  113.5 7.4 %collective-permute-start.19 = (bf16[160,640]{1,0:T(8,128)(2,1)S(1)}, bf16[160,640]{1,0:T(8,128)(2,1)S(1)}, u32[]{:S(2)}, u32[]{:S(2)}) collective-permute-start(bf16[160,640]{1,0:T(8,128)(2,1)S(1)} %get-tuple-element.49), channel_id=1, source_target_pairs={{0,2},{1,3},{2,0},{3,1},{4,6},{5,7},{6,4},{7,5},{8,10},{9,11},{10,... | collective-permute-start | bytes 614408 | tf_op jit(solution)/shard_map/ppermute | solution.py:408
  115.0 8.5 %collective-permute-start.25 = (bf16[320,320]{1,0:T(8,128)(2,1)S(1)}, bf16[320,320]{1,0:T(8,128)(2,1)S(1)}, u32[]{:S(2)}, u32[]{:S(2)}) collective-permute-start(bf16[320,320]{1,0:T(8,128)(2,1)S(1)} %slice.69), channel_id=1, source_target_pairs={{0,2},{1,3},{2,0},{3,1},{4,6},{5,7},{6,4},{7,5},{8,10},{9,11},{10,... | collective-permute-start | bytes 614408 | tf_op jit(solution)/shard_map/ppermute | solution.py:408
  115.6 7.9 %collective-permute-start.26 = (bf16[320,320]{1,0:T(8,128)(2,1)S(1)}, bf16[320,320]{1,0:T(8,128)(2,1)S(1)}, u32[]{:S(2)}, u32[]{:S(2)}) collective-permute-start(bf16[320,320]{1,0:T(8,128)(2,1)S(1)} %slice.70), channel_id=1, source_target_pairs={{0,1},{1,0},{2,3},{3,2},{4,5},{5,4},{6,7},{7,6},{8,9},{9,8},{10,11... | collective-permute-start | bytes 614408 | tf_op jit(solution)/shard_map/ppermute | solution.py:408
  116.7 12.0 %collective-permute-start.22 = (bf16[640,320]{1,0:T(8,128)(2,1)S(1)}, bf16[640,320]{1,0:T(8,128)(2,1)S(1)}, u32[]{:S(2)}, u32[]{:S(2)}) collective-permute-start(bf16[640,320]{1,0:T(8,128)(2,1)S(1)} %collective-permute-done.21.refs_5_), channel_id=1, source_target_pairs={{0,4},{4,0},{8,12},{12,8},{16,20},{20,16},{24,28},{28,24},{1,5},{5... | collective-permute-start | bytes 1228808 | tf_op jit(solution)/shard_map/ppermute | solution.py:483
  120.3 8.4 %collective-permute-start.24 = (bf16[640,320]{1,0:T(8,128)(2,1)S(1)}, bf16[640,320]{1,0:T(8,128)(2,1)S(1)}, u32[]{:S(2)}, u32[]{:S(2)}) collective-permute-start(bf16[640,320]{1,0:T(8,128)(2,1)S(1)} %collective-permute-done.23.refs_7_), channel_id=1, source_target_pairs={{0,4},{4,0},{8,12},{12,8},{16,20},{20,16},{24,28},{28,24},{1,5},{5... | collective-permute-start | bytes 1228808 | tf_op jit(solution)/shard_map/ppermute | solution.py:483
  120.9 7.9 %copy-start.14 = (f32[1,1280]{1,0:T(1,128)S(1)}, f32[1,1280]{1,0:T(1,128)}, u32[]{:S(2)}) copy-start(f32[1,1280]{1,0:T(1,128)} %get-tuple-element.69.refs_13_) | copy-start | bytes 15364
  120.9 7.9 %collective-permute-start.20 = (bf16[160,640]{1,0:T(8,128)(2,1)S(1)}, bf16[160,640]{1,0:T(8,128)(2,1)S(1)}, u32[]{:S(2)}, u32[]{:S(2)}) collective-permute-start(bf16[160,640]{1,0:T(8,128)(2,1)S(1)} %get-tuple-element.50), channel_id=1, source_target_pairs={{0,3},{1,2},{2,1},{3,0},{4,7},{5,6},{6,5},{7,4},{8,11},{9,10},{10,... | collective-permute-start | bytes 614408 | tf_op jit(solution)/shard_map/ppermute | solution.py:408
  123.5 5.2 %collective-permute-start.27 = (bf16[320,320]{1,0:T(8,128)(2,1)S(1)}, bf16[320,320]{1,0:T(8,128)(2,1)S(1)}, u32[]{:S(2)}, u32[]{:S(2)}) collective-permute-start(bf16[320,320]{1,0:T(8,128)(2,1)S(1)} %collective-permute-done.25.refs_9_), channel_id=1, source_target_pairs={{0,4},{4,0},{8,12},{12,8},{16,20},{20,16},{24,28},{28,24},{1,5},{5... | collective-permute-start | bytes 614408 | tf_op jit(solution)/shard_map/ppermute | solution.py:483
  123.5 5.2 %collective-permute-start.28 = (bf16[320,320]{1,0:T(8,128)(2,1)S(1)}, bf16[320,320]{1,0:T(8,128)(2,1)S(1)}, u32[]{:S(2)}, u32[]{:S(2)}) collective-permute-start(bf16[320,320]{1,0:T(8,128)(2,1)S(1)} %collective-permute-done.26.refs_10_), channel_id=1, source_target_pairs={{0,4},{4,0},{8,12},{12,8},{16,20},{20,16},{24,28},{28,24},{1,5},{5... | collective-permute-start | bytes 614408 | tf_op jit(solution)/shard_map/ppermute | solution.py:483
  132.3 23.4 %copy-start.11 = (f32[1,1280]{1,0:T(1,128)S(1)}, f32[1,1280]{1,0:T(1,128)}, u32[]{:S(2)}) copy-start(f32[1,1280]{1,0:T(1,128)} %refs_3_.3) | copy-start | bytes 15364
  132.3 19.4 %collective-permute-start.30 = (bf16[320,1280]{1,0:T(8,128)(2,1)S(1)}, bf16[320,1280]{1,0:T(8,128)(2,1)S(1)}, u32[]{:S(2)}, u32[]{:S(2)}) collective-permute-start(bf16[320,1280]{1,0:T(8,128)(2,1)S(1)} %get-tuple-element.51.refs_0_.refs_4_), channel_id=1, source_target_pairs={{0,1},{1,0},{2,3},{3,2},{4,5},{5,4},{6,7},{7,6},{8,9},{9,8},{10,11... | collective-permute-start | bytes 2457608 | tf_op jit(solution)/shard_map/ppermute | solution.py:408
  133.2 20.5 %collective-permute-start.29 = (bf16[320,1280]{1,0:T(8,128)(2,1)S(1)}, bf16[320,1280]{1,0:T(8,128)(2,1)S(1)}, u32[]{:S(2)}, u32[]{:S(2)}) collective-permute-start(bf16[320,1280]{1,0:T(8,128)(2,1)S(1)} %get-tuple-element.51.refs_0_.refs_4_), channel_id=1, source_target_pairs={{0,2},{1,3},{2,0},{3,1},{4,6},{5,7},{6,4},{7,5},{8,10},{9,11},{10,... | collective-permute-start | bytes 2457608 | tf_op jit(solution)/shard_map/ppermute | solution.py:408
  152.6 15.7 %collective-permute-start.32 = (bf16[160,1280]{1,0:T(8,128)(2,1)}, bf16[160,1280]{1,0:T(8,128)(2,1)}, u32[]{:S(2)}, u32[]{:S(2)}) collective-permute-start(bf16[160,1280]{1,0:T(8,128)(2,1)} %slice.71), channel_id=1, source_target_pairs={{0,2},{1,3},{2,0},{3,1},{4,6},{5,7},{6,4},{7,5},{8,10},{9,11},{10,... | collective-permute-start | bytes 1228808 | tf_op jit(solution)/shard_map/ppermute | solution.py:408
  154.7 13.5 %collective-permute-start.33 = (bf16[160,1280]{1,0:T(8,128)(2,1)}, bf16[160,1280]{1,0:T(8,128)(2,1)}, u32[]{:S(2)}, u32[]{:S(2)}) collective-permute-start(bf16[160,1280]{1,0:T(8,128)(2,1)} %slice.72), channel_id=1, source_target_pairs={{0,1},{1,0},{2,3},{3,2},{4,5},{5,4},{6,7},{7,6},{8,9},{9,8},{10,11... | collective-permute-start | bytes 1228808 | tf_op jit(solution)/shard_map/ppermute | solution.py:408
  155.8 1.9 copy-start
  157.7 1.9 copy-start.2
  159.6 2.5 %copy-start.1 = (bf16[1280,1280]{1,0:T(8,128)(2,1)S(1)}, bf16[1280,1280]{1,0:T(8,128)(2,1)}, u32[]{:S(2)}) copy-start(bf16[1280,1280]{1,0:T(8,128)(2,1)} %all-gather.7.cloned.1.call-done.refs_3_.refs_4_) | copy-start | bytes 9830404
  159.6 2.9 %copy-start.3 = (bf16[1,1280,1280]{2,1,0:T(8,128)(2,1)S(1)}, bf16[1,1280,1280]{2,1,0:T(8,128)(2,1)}, u32[]{:S(2)}) copy-start(bf16[1,1280,1280]{2,1,0:T(8,128)(2,1)} %all-gather.9.cloned.1.call-done) | copy-start | bytes 9830404
  159.6 3.1 %copy-start.8 = (bf16[320,1280]{1,0:T(8,128)(2,1)S(1)}, bf16[320,1280]{1,0:T(8,128)(2,1)}, u32[]{:S(2)}) copy-start(bf16[320,1280]{1,0:T(8,128)(2,1)} %copy-done.7) | copy-start | bytes 2457604
  159.6 3.3 %copy-start.10 = (bf16[320,1280]{1,0:T(8,128)(2,1)S(1)}, bf16[320,1280]{1,0:T(8,128)(2,1)}, u32[]{:S(2)}) copy-start(bf16[320,1280]{1,0:T(8,128)(2,1)} %copy-done.9) | copy-start | bytes 2457604
  162.1 6.2 %copy-start.4 = (bf16[160,1280]{1,0:T(8,128)(2,1)}, bf16[160,1280]{1,0:T(8,128)(2,1)S(1)}, u32[]{:S(2)}) copy-start(bf16[160,1280]{1,0:T(8,128)(2,1)S(1)} %get-tuple-element.53.refs_1_) | copy-start | bytes 1228804
  171.9 32.6 %copy-start.5 = (bf16[160,1280]{1,0:T(8,128)(2,1)S(1)}, bf16[160,1280]{1,0:T(8,128)(2,1)}, u32[]{:S(2)}) copy-start(bf16[160,1280]{1,0:T(8,128)(2,1)} %copy-done.4) | copy-start | bytes 1228804
  171.9 32.5 %copy-start.12 = (f32[1,1280]{1,0:T(1,128)S(1)}, f32[1,1280]{1,0:T(1,128)}, u32[]{:S(2)}) copy-start(f32[1,1280]{1,0:T(1,128)} %refs_7_.1) | copy-start | bytes 15364
  171.9 32.5 %copy-start.18 = (s32[2]{0:T(128)S(1)}, s32[2]{0:T(128)}, u32[]{:S(2)}) copy-start(s32[2]{0:T(128)} %copy-done.16) | copy-start | bytes 28
  171.9 12.4 %collective-permute-start.36 = (bf16[160,1280]{1,0:T(8,128)(2,1)S(1)}, bf16[160,1280]{1,0:T(8,128)(2,1)S(1)}, u32[]{:S(2)}, u32[]{:S(2)}) collective-permute-start(bf16[160,1280]{1,0:T(8,128)(2,1)S(1)} %get-tuple-element.58), channel_id=1, source_target_pairs={{0,1},{1,0},{2,3},{3,2},{4,5},{5,4},{6,7},{7,6},{8,9},{9,8},{10,11... | collective-permute-start | bytes 1228808 | tf_op jit(solution)/shard_map/ppermute | solution.py:408
  173.0 24.2 %collective-permute-start.31 = (bf16[160,1280]{1,0:T(8,128)(2,1)}, bf16[160,1280]{1,0:T(8,128)(2,1)S(1)}, u32[]{:S(2)}, u32[]{:S(2)}) collective-permute-start(bf16[160,1280]{1,0:T(8,128)(2,1)} %get-tuple-element.54), channel_id=1, source_target_pairs={{0,1},{1,0},{2,3},{3,2},{4,5},{5,4},{6,7},{7,6},{8,9},{9,8},{10,11... | collective-permute-start | bytes 1228808 | tf_op jit(solution)/shard_map/ppermute | solution.py:408
  174.0 23.2 %collective-permute-start.38 = (bf16[160,1280]{1,0:T(8,128)(2,1)}, bf16[160,1280]{1,0:T(8,128)(2,1)}, u32[]{:S(2)}, u32[]{:S(2)}) collective-permute-start(bf16[160,1280]{1,0:T(8,128)(2,1)} %get-tuple-element.59), channel_id=1, source_target_pairs={{0,2},{1,3},{2,0},{3,1},{4,6},{5,7},{6,4},{7,5},{8,10},{9,11},{10,... | collective-permute-start | bytes 1228808 | tf_op jit(solution)/shard_map/ppermute | solution.py:408
  174.9 20.5 %collective-permute-start.34 = (bf16[160,1280]{1,0:T(8,128)(2,1)S(1)}, bf16[160,1280]{1,0:T(8,128)(2,1)S(1)}, u32[]{:S(2)}, u32[]{:S(2)}) collective-permute-start(bf16[160,1280]{1,0:T(8,128)(2,1)S(1)} %get-tuple-element.57), channel_id=1, source_target_pairs={{0,2},{1,3},{2,0},{3,1},{4,6},{5,7},{6,4},{7,5},{8,10},{9,11},{10,... | collective-permute-start | bytes 1228808 | tf_op jit(solution)/shard_map/ppermute | solution.py:408
  185.2 15.4 %collective-permute-start.37 = (bf16[160,1280]{1,0:T(8,128)(2,1)}, bf16[160,1280]{1,0:T(8,128)(2,1)}, u32[]{:S(2)}, u32[]{:S(2)}) collective-permute-start(bf16[160,1280]{1,0:T(8,128)(2,1)} %add_convert_fusion), channel_id=1, source_target_pairs={{0,2},{1,3},{2,0},{3,1},{4,6},{5,7},{6,4},{7,5},{8,10},{9,11},{10,... | collective-permute-start | bytes 1228808 | tf_op jit(solution)/shard_map/ppermute | solution.py:408
  196.1 8.3 %collective-permute-start.35 = (bf16[160,1280]{1,0:T(8,128)(2,1)}, bf16[160,1280]{1,0:T(8,128)(2,1)}, u32[]{:S(2)}, u32[]{:S(2)}) collective-permute-start(bf16[160,1280]{1,0:T(8,128)(2,1)} %add_convert_fusion.1), channel_id=1, source_target_pairs={{0,1},{1,0},{2,3},{3,2},{4,5},{5,4},{6,7},{7,6},{8,9},{9,8},{10,11... | collective-permute-start | bytes 1228808 | tf_op jit(solution)/shard_map/ppermute | solution.py:408
  (5 other events, 5.4 us)
Sparse Core Ops, SparseCore 0:
  15.5 56.0 all-gather.4
  73.2 38.0 all-gather.6
  112.9 38.1 all-gather.8

commit v2 on v1

--- a/solution.py
+++ b/solution.py
@@ -66,7 +66,7 @@
         out_specs=[pl.BlockSpec((width // n_mp, tokens), lambda i: (0, i))] * n_mp,
         out_shape=[jax.ShapeDtypeStruct((width // n_mp, images * keep_most), BF)] * n_mp,
         scratch_shapes=[pltpu.VMEM((n_mp, width // n_mp, tokens), BF)],
-        compiler_params=params(24),
+        compiler_params=params(60),
         cost_estimate=cost(4e9, patches.size * 2),
         name="embed",
     )(place, keep.reshape(steps, 1, tokens), patches, position)
@@ -123,21 +123,22 @@
 
 def fetch_start(groups, block, spm, buf_ref, sem_ref):
     for k, pieces in enumerate(groups):
-        per = pieces[0].shape[0] // spm
-        for i, piece in enumerate(pieces):
-
-            def start(piece=piece, i=i, k=k):
-                at = pl.ds((block - i * per) * spm, spm)
+        low = 0
+        for piece in pieces:
+            high = low + piece.shape[0] // spm
+
+            def start(piece=piece, k=k, low=low):
+                at = pl.ds((block - low) * spm, spm)
                 pltpu.make_async_copy(piece.at[at], buf_ref.at[k], sem_ref.at[k]).start()
 
-            here = len(pieces) == 1 or jnp.logical_and(block >= i * per, block < (i + 1) * per)
             if isinstance(block, int):
-                if i * per <= block < (i + 1) * per:
+                if low <= block < high:
                     start()
-            elif here is True:
+            elif len(pieces) == 1:
                 start()
             else:
-                pl.when(here)(start)
+                pl.when(jnp.logical_and(block >= low, block < high))(start)
+            low = high
 
 
 def fetch_wait(groups, spm, buf_ref, sem_ref):
@@ -320,13 +321,16 @@
     total = jnp.concatenate(
         [jnp.where(core == 0, mine, mate), jnp.where(core == 0, mate, mine)], axis=1
     )
-    gain_ref, shift_ref, res_ref, out_ref = refs[at:]
+    gain_ref, shift_ref, res_ref, *out_refs = refs[at:]
     value = base_ref[...] + total
     res_ref[...] = value
     mean = jnp.mean(value, axis=1, keepdims=True)
     value = value - mean
     spread = jnp.mean(value * value, axis=1, keepdims=True)
-    out_ref[...] = (value * lax.rsqrt(spread + 1e-06) * gain_ref[...] + shift_ref[...]).astype(BF)
+    value = (value * lax.rsqrt(spread + 1e-06) * gain_ref[...] + shift_ref[...]).astype(BF)
+    each = out_refs[0].shape[0]
+    for i, ref in enumerate(out_refs):
+        ref[...] = value[i * each : (i + 1) * each]
 
 
 def project(place, base, hc, attended, out_weights, gain, shift, spm):
@@ -336,8 +340,9 @@
     return pl.pallas_call(
         functools.partial(project_kernel, [len(w[0]) for w in out_weights], spm, hc),
         in_specs=[pl.BlockSpec(memory_space=pltpu.SMEM)] + [vmem] * (n_mp + len(weights) + 3),
-        out_specs=[vmem] * 2,
-        out_shape=[jax.ShapeDtypeStruct(base.shape, F32), jax.ShapeDtypeStruct(base.shape, BF)],
+        out_specs=[vmem] * 3,
+        out_shape=[jax.ShapeDtypeStruct(base.shape, F32)]
+        + [jax.ShapeDtypeStruct((base.shape[0] // 2, base.shape[1]), BF)] * 2,
         compiler_params=params(20),
         cost_estimate=cost(3e9, 16 * base.size),
         name="project",
@@ -345,35 +350,37 @@
 
 
 def mlp_kernel(count, *refs):
-    in_refs, (up_ref, bias_ref, down_ref), out_refs = refs[:count], refs[count : count + 3], refs[count + 4 :]
+    in_refs, (weight_ref, bias_ref), out_refs = refs[:count], refs[count : count + 2], refs[count + 3 :]
     rows = jnp.concatenate([r[...] for r in in_refs], axis=0)
-    hidden_width = up_ref.shape[1]
+    hidden_width = bias_ref.shape[1]
     step = 256 if hidden_width % 256 == 0 else LANES
     hidden = []
     for c in range(0, hidden_width, step):
         at = slice(c, c + step)
-        up = jnp.dot(rows, up_ref[:, at], preferred_element_type=F32) + bias_ref[:, at]
+        up = jnp.dot(rows, weight_ref[:, at], preferred_element_type=F32) + bias_ref[:, at]
         hidden.append((0.5 * up * (1.0 + lax.erf(up * math.sqrt(0.5)))).astype(BF))
     hidden = jnp.concatenate(hidden, axis=1)
     each, width = out_refs[0].shape
     for c in range(0, width, 256):
-        part = lax.dot_general(hidden, down_ref[c : c + 256], NT, preferred_element_type=F32)
+        part = lax.dot_general(
+            hidden, weight_ref[c : c + 256, hidden_width:], NT, preferred_element_type=F32
+        )
         for i, ref in enumerate(out_refs):
             ref[:, c : c + 256] = part[i * each : (i + 1) * each].astype(BF)
 
 
-def mlp(rows, outs, up, bias, down, after):
-    width = down.shape[0]
+def mlp(rows, outs, weight, bias, after):
+    width = weight.shape[0]
     total = sum(r.shape[0] for r in rows)
     vmem = pl.BlockSpec(memory_space=pltpu.VMEM)
     return pl.pallas_call(
         functools.partial(mlp_kernel, len(rows)),
-        in_specs=[vmem] * (len(rows) + 3) + [pl.BlockSpec(memory_space=pl.ANY)],
+        in_specs=[vmem] * (len(rows) + 2) + [pl.BlockSpec(memory_space=pl.ANY)],
         out_specs=[vmem] * outs,
         out_shape=[jax.ShapeDtypeStruct((total // outs, width), BF)] * outs,
         compiler_params=params(20),
-        cost_estimate=cost(total * up.size * 4, up.size * 4),
-    )(*rows, up, bias, down, after)
+        cost_estimate=cost(total * weight.size * 2, weight.size * 2),
+    )(*rows, weight, bias, after)
 
 
 def finish_kernel(adds, pieces, spm, place_ref, *refs):
@@ -408,18 +415,17 @@
     return lax.ppermute(value, "mp", [(i, i ^ k) for i in range(n)])
 
 
-def after(value, *others):
-    return lax.optimization_barrier((value, *others))[0]
-
-
-def gather_blocks(value, n):
+def gather_blocks(values, n, direct=False):
     if n != 4:
-        return [[value]] + [[hop(value, k, n)] for k in range(1, n)]
-    half = value.shape[0] // 2
-    x = hop(value, 1, n)
-    y = hop(value, 2, n)
-    far = [hop(x[:half], 2, n), hop(y[half:], 1, n)]
-    return [[value], [x], [y], far]
+        return [values] + [[hop(v, k, n) for v in values] for k in range(1, n)]
+    x = [hop(v, 1, n) for v in values]
+    y = [hop(v, 2, n) for v in values[::-1]][::-1]
+    if direct:
+        return [values, x, y, [hop(v, 3, n) for v in values]]
+    half = values[0].shape[0] // 2
+    top, bottom = (x[0], y[1]) if len(values) == 2 else (x[0][:half], y[0][half:])
+    far = [hop(top, 2, n), hop(bottom, 1, n)]
+    return [values, x, y, far]
 
 
 def plus(a, b):
@@ -469,17 +475,16 @@
     hc = w_qkv.shape[3]
     place = jnp.stack([m, d]).astype(jnp.int32)
 
+    mixed = jnp.concatenate([w_o[0].T, w_qkv[0, 0], w_qkv[0, 1], w_qkv[0, 2]], axis=1)
+    mixed = lax.all_gather(mixed, "dp", axis=0, tiled=True)
     tokens = embed(place, patches, position, keep, n_mp)
     featured = [tokens[0]] + [hop(tokens[k], k, n_mp) for k in range(1, n_mp)]
 
-    w_qkv, w_o = after(w_qkv, tokens[0]), after(w_o, tokens[0])
-    mixed = jnp.concatenate([w_o[0].T, w_qkv[0, 0], w_qkv[0, 1], w_qkv[0, 2]], axis=1)
-    mixed = lax.all_gather(mixed, "dp", axis=0, tiled=True)
     own = mixed[:, :hc]
     part = lax.dynamic_slice_in_dim(own, (d % 2) * (width // 2), width // 2)
     mate = [(i, i ^ 1) for i in range(n_dp)]
     out_weights = [[[own]]]
-    for pieces in gather_blocks(part, n_mp)[1:]:
+    for pieces in gather_blocks([part], n_mp)[1:]:
         out_weights.append([pieces, [lax.ppermute(p, "dp", mate) for p in pieces]])
 
     first_image = d * images_here
@@ -500,8 +505,8 @@
     near = jnp.stack(moved[:half])
     far = jnp.stack(moved[half:])
     halves = [near, far]
-    up = lax.all_gather(w_up[0], "dp", axis=0, tiled=True)
-    down = lax.all_gather(w_down[0].T, "dp", axis=0, tiled=True)
+    both = jnp.concatenate([w_up[0], w_down[0].T], axis=1)
+    both = lax.all_gather(both, "dp", axis=0, tiled=True)
 
     image_ids = jnp.arange(counts.shape[0], dtype=jnp.int32)
     slots = jnp.bitwise_xor(jnp.arange(n_dp, dtype=jnp.int32), d)
@@ -514,7 +519,7 @@
     labrow = labels.reshape(n_dp, 1, slot_rows)
     labcol = labels.reshape(n_dp, slot_rows, 1)
 
-    moved = [gather_blocks(h, n_mp) for h in halves]
+    moved = [gather_blocks([h], n_mp, i == 1) for i, h in enumerate(halves)]
     gathered = [sum(pieces, []) for pieces in zip(*moved)]
     gain = ln_gain[0, 0].reshape(n_mp, 1, feat)
     shift = ln_bias[0, 0].reshape(n_mp, 1, feat)
@@ -528,15 +533,15 @@
     )
     attended = [attended[0]] + [hop(attended[k], k, n_mp) for k in range(1, n_mp)]
     base = own_rows(place, gathered, fold, b_o, spm)
-    residual, normed = project(
+    residual, *normed = project(
         place, base, hc, attended, out_weights, ln_gain[0, 1:2], ln_bias[0, 1:2], spm
     )
     blocks = gather_blocks(normed, n_mp)
     partials = [None] * n_mp
-    last = normed
+    last = normed[0]
     groups = [[0], [2, 1], [3]] if n_mp == 4 else [[k] for k in range(n_mp)]
     for group in groups:
-        outs = mlp(sum([blocks[k] for k in group], []), 2 * len(group), up, b_up, down, last)
+        outs = mlp(sum([blocks[k] for k in group], []), 2 * len(group), both, b_up, last)
         last = outs[0]
         for i, k in enumerate(group):
             partials[k] = outs[2 * i : 2 * i + 2]

time: 215 us -> 229 us (1.065); the launches traced: 214 us -> 225 us
  waiting for transfers between devices: 82.9 us -> 99.1 us
  local copies, waits for them, and re-layouts: 24.1 us -> 16.4 us
  Pallas kernels: 46.3 us -> 52.4 us
  starting transfers between devices: 42.9 us -> 40.2 us
    ppermute x7, waiting for transfers between devices: 17.9 us -> 34.1 us  [per_device(): lax.ppermute(packed[i], 'dp', [(j, j ^ i) for j in range(n_dp)])]
    unnamed x54 -> x42, local copies, waits for them, and re-layouts: 11.8 us -> 7.18 us
    slice x8 -> x4, local copies, waits for them, and re-layouts: 4.49 us -> 1.45 us  [the longest x2 0.73 us: gather_blocks(): x[0][:half]]
    ppermute x7, starting transfers between devices: 10.1 us -> 7.57 us  [per_device(): lax.ppermute(packed[i], 'dp', [(j, j ^ i) for j in range(n_dp)])]
    pallas_call x3, Pallas kernels: 11.4 us -> 13.9 us  [mlp(): pl.pallas_call(functools.partial(mlp_kernel, len(rows)), in_specs=[vmem]...]
    pallas_call x1, Pallas kernels: 3.27 us -> 5.66 us  [embed(): pl.pallas_call(embed_kernel, grid=(steps,), in_specs=[pl.BlockSpec(memory...]
    ppermute x28 -> x29, waiting for transfers between devices: 63.6 us -> 64.9 us  [hop(): return lax.ppermute(value, 'mp', [(i, i ^ k) for i in range(n)])]
    ppermute x28 -> x29, starting transfers between devices: 32.2 us -> 32 us  [hop(): return lax.ppermute(value, 'mp', [(i, i ^ k) for i in range(n)])]
  transfers between devices with their start and end apart: 42 -> 42, of which waited for: 16 -> 20; matrix products, arithmetic and copies ran while one was open for 7% -> 4% of each run, Pallas kernels for 17% -> 20%
where the time goes in v2:
time: 229 us; the launch traced here: 225 us
  waiting for transfers between devices  99.1 us (43%)
  Pallas kernels  52.4 us (23%)
  starting transfers between devices  40.2 us (18%)
  local copies, waits for them, and re-layouts  16.4 us (7%)
  between operations  13.8 us (6%)
  other arithmetic  3.37 us (1%)
    ppermute x29, waiting for transfers between devices, hop(): return lax.ppermute(value, 'mp', [(i, i ^ k) for i in range(n)])  64.9 us
    ppermute x7, waiting for transfers between devices, per_device(): lax.ppermute(packed[i], 'dp', [(j, j ^ i) for j in range(n_dp)])  34.1 us
    ppermute x29, starting transfers between devices, hop(): return lax.ppermute(value, 'mp', [(i, i ^ k) for i in range(n)])  32 us
    pallas_call x2, Pallas kernels, attend(): pl.pallas_call(functools.partial(attend_kernel, [len(g) for g in gathered...  19.6 us
    pallas_call x3, Pallas kernels, mlp(): pl.pallas_call(functools.partial(mlp_kernel, len(rows)), in_specs=[vmem]...  13.9 us
    ppermute x7, starting transfers between devices, per_device(): lax.ppermute(packed[i], 'dp', [(j, j ^ i) for j in range(n_dp)])  7.57 us
    unnamed x42, local copies, waits for them, and re-layouts  7.18 us
    pallas_call x1, Pallas kernels, embed(): pl.pallas_call(embed_kernel, grid=(steps,), in_specs=[pl.BlockSpec(memory...  5.66 us
  transfers between devices with their start and end apart: 42, of which 20 were waited for; matrix products, arithmetic and copies ran while one was open for 4% of the time, Pallas kernels for 20%

profile of v2, /device:TPU:0, one launch (start us, length us, event | category | flops | bytes accessed | tf_op | source)
XLA Modules:
  0.0 225.2 jit_solution(13417651328251956496)
XLA Ops:
  6.5 1.1 slice_bitcast_fusion
  7.7 1.9 concatenate.6
  9.6 0.9 pad_maximum_fusion
  12.0 5.7 %embed.1 = (bf16[320,512]{1,0:T(8,128)(2,1)}, bf16[320,512]{1,0:T(8,128)(2,1)}, bf16[320,512]{1,0:T(8,128)(2,1)}, bf16[320,512]{1,0:T(8,128)(2,1)}) custom-call(s32[2]{0:T(128)} %pad_add_fusion.place_ref, s32[4,1,128]{2,1,0:T(1,128)} %reshape.142.keep_ref, bf16[8,256,1280]{2,1,0:T(8,128)(2,1)} %patches_ref.1, bf16[256,1280]{1,0:T(8,128)(2,1)} %position_ref.1), custom_call_target="tpu_custom_call" | custom-call | flops 4000000000 | bytes 5242880 | tf_op jit(solution)/shard_map/embed/pallas_call | solution.py:57
  17.6 3.0 %collective-permute-start = (bf16[320,512]{1,0:T(8,128)(2,1)}, bf16[320,512]{1,0:T(8,128)(2,1)S(1)}, u32[]{:S(2)}, u32[]{:S(2)}) collective-permute-start(bf16[320,512]{1,0:T(8,128)(2,1)} %get-tuple-element.33), channel_id=1, source_target_pairs={{0,1},{1,0},{2,3},{3,2},{4,5},{5,4},{6,7},{7,6},{8,9},{9,8},{10,11... | collective-permute-start | bytes 983048 | tf_op jit(solution)/shard_map/ppermute | solution.py:415
  20.6 1.5 collective-permute-start.1
  23.6 5.8 %collective-permute-done.refs_1_ = bf16[320,512]{1,0:T(8,128)(2,1)S(1)} collective-permute-done((bf16[320,512]{1,0:T(8,128)(2,1)}, bf16[320,512]{1,0:T(8,128)(2,1)S(1)}, u32[]{:S(2)}, u32[]{:S(2)}) %collective-permute-start) | collective-permute-done | bytes 327712 | tf_op jit(solution)/shard_map/ppermute | solution.py:415
  29.4 7.6 %collective-permute-done.1.refs_2_ = bf16[320,512]{1,0:T(8,128)(2,1)S(1)} collective-permute-done((bf16[320,512]{1,0:T(8,128)(2,1)}, bf16[320,512]{1,0:T(8,128)(2,1)S(1)}, u32[]{:S(2)}, u32[]{:S(2)}) %collective-permute-start.1) | collective-permute-done | bytes 327712 | tf_op jit(solution)/shard_map/ppermute | solution.py:415
  37.0 1.0 copy-done.12
  38.0 3.5 %pack.1 = (bf16[80,640]{1,0:T(8,128)(2,1)S(1)}, bf16[80,640]{1,0:T(8,128)(2,1)S(1)}, bf16[80,640]{1,0:T(8,128)(2,1)S(1)}, bf16[80,640]{1,0:T(8,128)(2,1)S(1)}, b...) custom-call(s32[2]{0:T(128)S(1)} %copy-done.9, ...), custom_call_target="tpu_custom_call" | custom-call | flops 4000000000 | bytes 1310720 | tf_op jit(solution)/shard_map/pack/pallas_call | solution.py:104
  41.6 1.6 collective-permute-start.4
  43.4 7.9 %collective-permute-done.5 = bf16[80,640]{1,0:T(8,128)(2,1)S(1)} collective-permute-done((bf16[80,640]{1,0:T(8,128)(2,1)S(1)}, bf16[80,640]{1,0:T(8,128)(2,1)S(1)}, u32[]{:S(2)}, u32[]{:S(2)}) %collective-permute-start.5) | collective-permute-done | bytes 102432 | tf_op jit(solution)/shard_map/ppermute | solution.py:504
  51.3 2.2 collective-permute-done.4
  53.5 1.5 collective-permute-start.10
  55.1 1.5 collective-permute-start.12
  57.2 1.6 collective-permute-start.9
  58.8 1.4 collective-permute-start.8
  60.4 4.7 %collective-permute-done.10.refs_2_.refs_1_ = bf16[4,80,640]{2,1,0:T(8,128)(2,1)S(1)} collective-permute-done((bf16[4,80,640]{2,1,0:T(8,128)(2,1)S(1)}, bf16[4,80,640]{2,1,0:T(8,128)(2,1)S(1)}, u32[]{:S(2)}, u32[]{:S(2)}) %collective-permute-start.10) | collective-permute-done | bytes 409632 | tf_op jit(solution)/shard_map/ppermute | solution.py:415
  65.1 2.4 %collective-permute-start.6 = (bf16[80,640]{1,0:T(8,128)(2,1)S(1)}, bf16[80,640]{1,0:T(8,128)(2,1)S(1)}, u32[]{:S(2)}, u32[]{:S(2)}) collective-permute-start(bf16[80,640]{1,0:T(8,128)(2,1)S(1)} %get-tuple-element.40), channel_id=1, source_target_pairs={{0,16},{4,20},{8,24},{12,28},{16,0},{20,4},{24,8},{28,12},{1,17},{... | collective-permute-start | bytes 307208 | tf_op jit(solution)/shard_map/ppermute | solution.py:504
  69.0 0.7 slice.48
  69.7 1.5 collective-permute-start.14
  71.2 0.7 slice.49
  72.6 15.2 %collective-permute-done.7 = bf16[80,640]{1,0:T(8,128)(2,1)S(1)} collective-permute-done((bf16[80,640]{1,0:T(8,128)(2,1)S(1)}, bf16[80,640]{1,0:T(8,128)(2,1)S(1)}, u32[]{:S(2)}, u32[]{:S(2)}) %collective-permute-start.7) | collective-permute-done | bytes 102432 | tf_op jit(solution)/shard_map/ppermute | solution.py:504
  87.8 8.9 %collective-permute-done.6 = bf16[80,640]{1,0:T(8,128)(2,1)S(1)} collective-permute-done((bf16[80,640]{1,0:T(8,128)(2,1)S(1)}, bf16[80,640]{1,0:T(8,128)(2,1)S(1)}, u32[]{:S(2)}, u32[]{:S(2)}) %collective-permute-start.6) | collective-permute-done | bytes 102432 | tf_op jit(solution)/shard_map/ppermute | solution.py:504
  96.7 1.5 collective-permute-start.11
  98.2 2.0 collective-permute-start.16
  100.3 1.3 slice.50.refs_4_
  101.7 1.5 collective-permute-start.20
  103.2 1.9 copy-done.2
  105.1 0.7 copy-done.7
  106.5 9.3 %attend.2.refs_15_ = bf16[2,160,640]{2,1,0:T(8,128)(2,1)S(1)} custom-call(s32[2]{0:T(128)S(1)} %copy-done.10, bf16[4,80,640]{2,1,0:T(8,128)(2,1)S(1)} %pad_maximum_fusion.1.refs_0_, bf16[4,80,640]{2,1,0:T(8,128)(2,1)S(1)} %collective-permute-done.10.refs_2_.refs_1_, bf16[4,80,640]{2,1,0:T(8,128)(2,1)S(1)} %collective-permute-done.12.refs_4_.refs_2_, ...), custom_call_target="tpu_custom_call" | custom-call | flops 8000000000 | bytes 6553600 | tf_op jit(solution)/shard_map/attend/pallas_call | solution.py:240
  115.8 3.5 %collective-permute-done.13.refs_5_ = bf16[4,80,640]{2,1,0:T(8,128)(2,1)S(1)} collective-permute-done((bf16[4,80,640]{2,1,0:T(8,128)(2,1)S(1)}, bf16[4,80,640]{2,1,0:T(8,128)(2,1)S(1)}, u32[]{:S(2)}, u32[]{:S(2)}) %collective-permute-start.13) | collective-permute-done | bytes 409632 | tf_op jit(solution)/shard_map/ppermute | solution.py:415
  119.3 10.2 %attend.3 = (bf16[160,640]{1,0:T(8,128)(2,1)S(1)}, bf16[160,640]{1,0:T(8,128)(2,1)S(1)}, bf16[160,640]{1,0:T(8,128)(2,1)S(1)}, bf16[160,640]{1,0:T(8,128)(2,1)S(1)}) custom-call(s32[2]{0:T(128)S(1)} %copy-done.10, bf16[4,80,640]{2,1,0:T(8,128)(2,1)S(1)} %pad_maximum_fusion.1.refs_0_, bf16[4,80,640]{2,1,0:T(8,128)(2,1)S(1)} %pad_maximum_fusion.2.refs_1_, ...), custom_call_target="tpu_custom_call" | custom-call | flops 8000000000 | bytes 6553600 | tf_op jit(solution)/shard_map/attend/pallas_call | solution.py:240
  130.2 0.9 collective-permute-start.18
  131.2 1.2 collective-permute-start.24
  132.9 2.5 %collective-permute-done.17.refs_1_ = bf16[160,640]{1,0:T(8,128)(2,1)S(1)} collective-permute-done((bf16[160,640]{1,0:T(8,128)(2,1)S(1)}, bf16[160,640]{1,0:T(8,128)(2,1)S(1)}, u32[]{:S(2)}, u32[]{:S(2)}) %collective-permute-start.17) | collective-permute-done | bytes 204832 | tf_op jit(solution)/shard_map/ppermute | solution.py:415
  136.0 1.1 collective-permute-done.18.refs_2_
  137.1 2.0 collective-permute-start.19
  139.1 1.6 collective-permute-done.24.refs_9_
  140.7 2.3 %collective-permute-done.25.refs_10_ = bf16[320,320]{1,0:T(8,128)(2,1)S(1)} collective-permute-done((bf16[320,320]{1,0:T(8,128)(2,1)S(1)}, bf16[320,320]{1,0:T(8,128)(2,1)S(1)}, u32[]{:S(2)}, u32[]{:S(2)}) %collective-permute-start.25) | collective-permute-done | bytes 204832 | tf_op jit(solution)/shard_map/ppermute | solution.py:415
  143.0 2.9 %own.1.base_ref = f32[320,1280]{1,0:T(8,128)S(1)} custom-call(s32[2]{0:T(128)S(1)} %copy-done.10, bf16[4,80,640]{2,1,0:T(8,128)(2,1)S(1)} %pad_maximum_fusion.1.refs_0_, bf16[4,80,640]{2,1,0:T(8,128)(2,1)S(1)} %pad_maximum_fusion.2.refs_1_, bf16[4,80,640]{2,1,0:T(8,128)(2,1)S(1)} %collective-permute-done.10.refs_2_.refs_1_, ...), custom_call_target="tpu_custom_call" | custom-call | flops 1000000000 | bytes 409600 | tf_op jit(solution)/shard_map/own/pallas_call | solution.py:281
  146.0 4.3 %project.1 = (f32[320,1280]{1,0:T(8,128)S(1)}, bf16[160,1280]{1,0:T(8,128)(2,1)S(1)}, bf16[160,1280]{1,0:T(8,128)(2,1)}) custom-call(s32[2]{0:T(128)S(1)} %copy-done.10, f32[320,1280]{1,0:T(8,128)S(1)} %own.1.base_ref, bf16[160,640]{1,0:T(8,128)(2,1)S(1)} %get-tuple-element.44.refs_0_, bf16[160,640]{1,0:T(8,128)(2,1)S(1)} %collective-permute-done.17.refs_1_, ...), custom_call_target="tpu_custom_call" | custom-call | flops 3000000000 | bytes 6553600 | tf_op jit(solution)/shard_map/project/pallas_call | solution.py:340
  150.2 1.4 collective-permute-start.30
  151.7 0.7 collective-permute-start.29
  152.4 1.3 collective-permute-start.28
  154.3 8.4 %collective-permute-done.30.refs_2_ = bf16[160,1280]{1,0:T(8,128)(2,1)} collective-permute-done((bf16[160,1280]{1,0:T(8,128)(2,1)S(1)}, bf16[160,1280]{1,0:T(8,128)(2,1)}, u32[]{:S(2)}, u32[]{:S(2)}) %collective-permute-start.30) | collective-permute-done | bytes 409632 | tf_op jit(solution)/shard_map/ppermute | solution.py:415
  162.7 0.7 collective-permute-start.33
  163.4 0.9 collective-permute-done.29.refs_1_
  164.9 2.9 %copy-done = bf16[1280,2560]{1,0:T(8,128)(2,1)S(1)} copy-done((bf16[1280,2560]{1,0:T(8,128)(2,1)S(1)}, bf16[1280,2560]{1,0:T(8,128)(2,1)}, u32[]{:S(2)}) %copy-start) | copy-done | bytes 6553624
  167.8 3.6 %shard_map.145 = (bf16[160,1280]{1,0:T(8,128)(2,1)S(1)}, bf16[160,1280]{1,0:T(8,128)(2,1)S(1)}) custom-call(bf16[160,1280]{1,0:T(8,128)(2,1)S(1)} %get-tuple-element.48.refs_0_.refs_4_, bf16[160,1280]{1,0:T(8,128)(2,1)} %get-tuple-element.49.refs_1_, bf16[1280,2560]{1,0:T(8,128)(2,1)S(1)} %copy-done, f32[1,1280]{1,0:T(1,128)S(1)} %copy-done.3, ...), custom_call_target="tpu_custom_call" | custom-call | flops 2097152000 | bytes 6553600 | tf_op jit(solution)/shard_map/pallas_call | solution.py:376
  171.4 1.7 collective-permute-done.28.refs_0_
  173.1 6.7 %shard_map.146 = (bf16[160,1280]{1,0:T(8,128)(2,1)S(1)}, bf16[160,1280]{1,0:T(8,128)(2,1)}, bf16[160,1280]{1,0:T(8,128)(2,1)}, bf16[160,1280]{1,0:T(8,128)(2,1)S(1)}) custom-call(bf16[160,1280]{1,0:T(8,128)(2,1)} %collective-permute-done.28.refs_0_, bf16[160,1280]{1,0:T(8,128)(2,1)} %collective-permute-done.29.refs_1_, ...), custom_call_target="tpu_custom_call" | custom-call | flops 4194304000 | bytes 6553600 | tf_op jit(solution)/shard_map/pallas_call | solution.py:376
  179.8 1.3 collective-permute-done.33.refs_0_
  181.2 3.6 %shard_map.147 = (bf16[160,1280]{1,0:T(8,128)(2,1)S(1)}, bf16[160,1280]{1,0:T(8,128)(2,1)S(1)}) custom-call(bf16[160,1280]{1,0:T(8,128)(2,1)} %collective-permute-done.33.refs_0_, bf16[160,1280]{1,0:T(8,128)(2,1)} %collective-permute-done.34.refs_1_, bf16[1280,2560]{1,0:T(8,128)(2,1)S(1)} %copy-done.1, f32[1,1280]{1,0:T(1,128)S(1)} %copy-done.3, ...), custom_call_target="tpu_custom_call" | custom-call | flops 2097152000 | bytes 6553600 | tf_op jit(solution)/shard_map/pallas_call | solution.py:376
  185.1 0.8 collective-permute-start.32
  185.9 1.2 collective-permute-start.37
  187.1 1.7 collective-permute-start.39
  188.9 8.3 %collective-permute-done.35 = bf16[160,1280]{1,0:T(8,128)(2,1)S(1)} collective-permute-done((bf16[160,1280]{1,0:T(8,128)(2,1)S(1)}, bf16[160,1280]{1,0:T(8,128)(2,1)S(1)}, u32[]{:S(2)}, u32[]{:S(2)}) %collective-permute-start.35) | collective-permute-done | bytes 409632 | tf_op jit(solution)/shard_map/ppermute | solution.py:415
  197.9 8.5 %collective-permute-done.37 = bf16[160,1280]{1,0:T(8,128)(2,1)S(1)} collective-permute-done((bf16[160,1280]{1,0:T(8,128)(2,1)S(1)}, bf16[160,1280]{1,0:T(8,128)(2,1)S(1)}, u32[]{:S(2)}, u32[]{:S(2)}) %collective-permute-start.37) | collective-permute-done | bytes 409632 | tf_op jit(solution)/shard_map/ppermute | solution.py:415
  206.4 0.9 add_convert_fusion
  207.3 1.7 collective-permute-start.38
  209.1 4.4 %collective-permute-done.36.refs_3_ = bf16[160,1280]{1,0:T(8,128)(2,1)} collective-permute-done((bf16[160,1280]{1,0:T(8,128)(2,1)S(1)}, bf16[160,1280]{1,0:T(8,128)(2,1)}, u32[]{:S(2)}, u32[]{:S(2)}) %collective-permute-start.36) | collective-permute-done | bytes 409632 | tf_op jit(solution)/shard_map/ppermute | solution.py:415
  213.5 2.1 collective-permute-done.38.refs_4_
  215.6 2.7 %finish.1 = bf16[320,1280]{1,0:T(8,128)(2,1)} custom-call(s32[2]{0:T(128)S(1)} %copy-done.11, bf16[160,1280]{1,0:T(8,128)(2,1)S(1)} %get-tuple-element.50.refs_6_.refs_0_, bf16[160,1280]{1,0:T(8,128)(2,1)S(1)} %get-tuple-element.51.refs_1_, bf16[160,1280]{1,0:T(8,128)(2,1)} %collective-permute-done.32.refs_2_, ...), custom_call_target="tpu_custom_call" | custom-call | flops 1000000000 | bytes 3276800 | tf_op jit(solution)/shard_map/finish/pallas_call | solution.py:403
  (115 shorter events, 11.0 us)
Async XLA Ops:
  6.5 3.1 %copy-start.13 = (bf16[1,1280,160]{1,2,0:T(8,128)(2,1)S(1)}, bf16[1,1280,160]{1,2,0:T(8,128)(2,1)}, u32[]{:S(2)}) copy-start(bf16[1,1280,160]{1,2,0:T(8,128)(2,1)} %param.28) | copy-start | bytes 1228804
  6.5 3.1 %copy-start.14 = (bf16[1,160,1280]{2,1,0:T(8,128)(2,1)S(1)}, bf16[1,160,1280]{2,1,0:T(8,128)(2,1)}, u32[]{:S(2)}) copy-start(bf16[1,160,1280]{2,1,0:T(8,128)(2,1)} %param.26) | copy-start | bytes 1228804
  6.5 93.7 %all-gather.3.cloned.1.call-start = ((), (), s32[]{:S(2)}) async-start(), calls=%async_computation | async-start | bytes 3686400 | tf_op jit(solution)/shard_map/all_gather | solution.py:479
  9.5 1.1 copy-start.19
  9.6 155.4 %all-gather.5.cloned.1.call-start = ((), (), s32[]{:S(2)}) async-start(), calls=%async_computation.1 | async-start | bytes 7372800 | tf_op jit(solution)/shard_map/all_gather | solution.py:509
  12.0 10.2 %copy-start.20 = (s32[256]{0:T(256)S(1)}, s32[256]{0:T(256)}, u32[]{:S(2)}) copy-start(s32[256]{0:T(256)} %param.18) | copy-start | bytes 3076
  12.0 10.5 %copy-start.17 = (s32[256]{0:T(256)S(1)}, s32[256]{0:T(256)}, u32[]{:S(2)}) copy-start(s32[256]{0:T(256)} %param.19) | copy-start | bytes 3076
  12.0 11.0 %copy-start.15 = (f32[1,2,1280]{2,1,0:T(2,128)S(1)}, f32[1,2,1280]{2,1,0:T(2,128)}, u32[]{:S(2)}) copy-start(f32[1,2,1280]{2,1,0:T(2,128)} %param.21) | copy-start | bytes 30724
  12.0 11.0 %copy-start.16 = (f32[1,2,1280]{2,1,0:T(2,128)S(1)}, f32[1,2,1280]{2,1,0:T(2,128)}, u32[]{:S(2)}) copy-start(f32[1,2,1280]{2,1,0:T(2,128)} %param.20) | copy-start | bytes 30724
  12.0 25.1 %copy-start.9 = (s32[2]{0:T(128)S(1)}, s32[2]{0:T(128)}, u32[]{:S(2)}) copy-start(s32[2]{0:T(128)} %pad_add_fusion.place_ref) | copy-start | bytes 28
  17.6 11.8 %collective-permute-start = (bf16[320,512]{1,0:T(8,128)(2,1)}, bf16[320,512]{1,0:T(8,128)(2,1)S(1)}, u32[]{:S(2)}, u32[]{:S(2)}) collective-permute-start(bf16[320,512]{1,0:T(8,128)(2,1)} %get-tuple-element.33), channel_id=1, source_target_pairs={{0,1},{1,0},{2,3},{3,2},{4,5},{5,4},{6,7},{7,6},{8,9},{9,8},{10,11... | collective-permute-start | bytes 983048 | tf_op jit(solution)/shard_map/ppermute | solution.py:415
  20.6 16.4 %collective-permute-start.1 = (bf16[320,512]{1,0:T(8,128)(2,1)}, bf16[320,512]{1,0:T(8,128)(2,1)S(1)}, u32[]{:S(2)}, u32[]{:S(2)}) collective-permute-start(bf16[320,512]{1,0:T(8,128)(2,1)} %get-tuple-element.34), channel_id=1, source_target_pairs={{0,2},{1,3},{2,0},{3,1},{4,6},{5,7},{6,4},{7,5},{8,10},{9,11},{10,... | collective-permute-start | bytes 983048 | tf_op jit(solution)/shard_map/ppermute | solution.py:415
  22.1 14.9 %collective-permute-start.2 = (bf16[320,512]{1,0:T(8,128)(2,1)}, bf16[320,512]{1,0:T(8,128)(2,1)S(1)}, u32[]{:S(2)}, u32[]{:S(2)}) collective-permute-start(bf16[320,512]{1,0:T(8,128)(2,1)} %get-tuple-element.35), channel_id=1, source_target_pairs={{0,3},{1,2},{2,1},{3,0},{4,7},{5,6},{6,5},{7,4},{8,11},{9,10},{10,... | collective-permute-start | bytes 983048 | tf_op jit(solution)/shard_map/ppermute | solution.py:415
  37.0 1.0 copy-start.12
  38.0 30.1 %copy-start.18 = (f32[1,3,320]{2,0,1:T(1,128)S(1)}, f32[1,3,320]{2,0,1:T(1,128)}, u32[]{:S(2)}) copy-start(f32[1,3,320]{2,0,1:T(1,128)} %param.23) | copy-start | bytes 11524
  41.5 9.8 %collective-permute-start.5 = (bf16[80,640]{1,0:T(8,128)(2,1)S(1)}, bf16[80,640]{1,0:T(8,128)(2,1)S(1)}, u32[]{:S(2)}, u32[]{:S(2)}) collective-permute-start(bf16[80,640]{1,0:T(8,128)(2,1)S(1)} %get-tuple-element.39), channel_id=1, source_target_pairs={{0,12},{4,8},{8,4},{12,0},{16,28},{20,24},{24,20},{28,16},{1,13},{... | collective-permute-start | bytes 307208 | tf_op jit(solution)/shard_map/ppermute | solution.py:504
  41.6 11.8 %collective-permute-start.4 = (bf16[80,640]{1,0:T(8,128)(2,1)S(1)}, bf16[80,640]{1,0:T(8,128)(2,1)S(1)}, u32[]{:S(2)}, u32[]{:S(2)}) collective-permute-start(bf16[80,640]{1,0:T(8,128)(2,1)S(1)} %get-tuple-element.38), channel_id=1, source_target_pairs={{0,8},{4,12},{8,0},{12,4},{16,24},{20,28},{24,16},{28,20},{1,9},{5... | collective-permute-start | bytes 307208 | tf_op jit(solution)/shard_map/ppermute | solution.py:504
  43.2 10.2 %collective-permute-start.3 = (bf16[80,640]{1,0:T(8,128)(2,1)S(1)}, bf16[80,640]{1,0:T(8,128)(2,1)S(1)}, u32[]{:S(2)}, u32[]{:S(2)}) collective-permute-start(bf16[80,640]{1,0:T(8,128)(2,1)S(1)} %get-tuple-element.37), channel_id=1, source_target_pairs={{0,4},{4,0},{8,12},{12,8},{16,20},{20,16},{24,28},{28,24},{1,5},{5... | collective-permute-start | bytes 307208 | tf_op jit(solution)/shard_map/ppermute | solution.py:504
  53.5 11.6 %collective-permute-start.10 = (bf16[4,80,640]{2,1,0:T(8,128)(2,1)S(1)}, bf16[4,80,640]{2,1,0:T(8,128)(2,1)S(1)}, u32[]{:S(2)}, u32[]{:S(2)}) collective-permute-start(bf16[4,80,640]{2,1,0:T(8,128)(2,1)S(1)} %pad_maximum_fusion.1.refs_0_), channel_id=1, source_target_pairs={{0,1},{1,0},{2,3},{3,2},{4,5},{5,4},{6,7},{7,6},{8,9},{9,8},{10,11... | collective-permute-start | bytes 1228808 | tf_op jit(solution)/shard_map/ppermute | solution.py:415
  55.1 14.5 %collective-permute-start.12 = (bf16[4,80,640]{2,1,0:T(8,128)(2,1)S(1)}, bf16[4,80,640]{2,1,0:T(8,128)(2,1)S(1)}, u32[]{:S(2)}, u32[]{:S(2)}) collective-permute-start(bf16[4,80,640]{2,1,0:T(8,128)(2,1)S(1)} %pad_maximum_fusion.1.refs_0_), channel_id=1, source_target_pairs={{0,2},{1,3},{2,0},{3,1},{4,6},{5,7},{6,4},{7,5},{8,10},{9,11},{10,... | collective-permute-start | bytes 1228808 | tf_op jit(solution)/shard_map/ppermute | solution.py:415
  57.2 14.7 %collective-permute-start.9 = (bf16[80,640]{1,0:T(8,128)(2,1)S(1)}, bf16[80,640]{1,0:T(8,128)(2,1)S(1)}, u32[]{:S(2)}, u32[]{:S(2)}) collective-permute-start(bf16[80,640]{1,0:T(8,128)(2,1)S(1)} %get-tuple-element.43), channel_id=1, source_target_pairs={{0,28},{4,24},{8,20},{12,16},{16,12},{20,8},{24,4},{28,0},{1,29},{... | collective-permute-start | bytes 307208 | tf_op jit(solution)/shard_map/ppermute | solution.py:504
  58.8 13.8 %collective-permute-start.8 = (bf16[80,640]{1,0:T(8,128)(2,1)S(1)}, bf16[80,640]{1,0:T(8,128)(2,1)S(1)}, u32[]{:S(2)}, u32[]{:S(2)}) collective-permute-start(bf16[80,640]{1,0:T(8,128)(2,1)S(1)} %get-tuple-element.42), channel_id=1, source_target_pairs={{0,24},{4,28},{8,16},{12,20},{16,8},{20,12},{24,0},{28,4},{1,25},{... | collective-permute-start | bytes 307208 | tf_op jit(solution)/shard_map/ppermute | solution.py:504
  60.2 27.6 %collective-permute-start.7 = (bf16[80,640]{1,0:T(8,128)(2,1)S(1)}, bf16[80,640]{1,0:T(8,128)(2,1)S(1)}, u32[]{:S(2)}, u32[]{:S(2)}) collective-permute-start(bf16[80,640]{1,0:T(8,128)(2,1)S(1)} %get-tuple-element.41), channel_id=1, source_target_pairs={{0,20},{4,16},{8,28},{12,24},{16,4},{20,0},{24,12},{28,8},{1,21},{... | collective-permute-start | bytes 307208 | tf_op jit(solution)/shard_map/ppermute | solution.py:504
  65.1 31.6 %collective-permute-start.6 = (bf16[80,640]{1,0:T(8,128)(2,1)S(1)}, bf16[80,640]{1,0:T(8,128)(2,1)S(1)}, u32[]{:S(2)}, u32[]{:S(2)}) collective-permute-start(bf16[80,640]{1,0:T(8,128)(2,1)S(1)} %get-tuple-element.40), channel_id=1, source_target_pairs={{0,16},{4,20},{8,24},{12,28},{16,0},{20,4},{24,8},{28,12},{1,17},{... | collective-permute-start | bytes 307208 | tf_op jit(solution)/shard_map/ppermute | solution.py:504
  69.7 32.0 %collective-permute-start.14 = (bf16[2,80,640]{2,1,0:T(8,128)(2,1)}, bf16[2,80,640]{2,1,0:T(8,128)(2,1)}, u32[]{:S(2)}, u32[]{:S(2)}) collective-permute-start(bf16[2,80,640]{2,1,0:T(8,128)(2,1)} %slice.48), channel_id=1, source_target_pairs={{0,2},{1,3},{2,0},{3,1},{4,6},{5,7},{6,4},{7,5},{8,10},{9,11},{10,... | collective-permute-start | bytes 614408 | tf_op jit(solution)/shard_map/ppermute | solution.py:415
  71.9 31.3 %collective-permute-start.15 = (bf16[2,80,640]{2,1,0:T(8,128)(2,1)}, bf16[2,80,640]{2,1,0:T(8,128)(2,1)}, u32[]{:S(2)}, u32[]{:S(2)}) collective-permute-start(bf16[2,80,640]{2,1,0:T(8,128)(2,1)} %slice.49), channel_id=1, source_target_pairs={{0,1},{1,0},{2,3},{3,2},{4,5},{5,4},{6,7},{7,6},{8,9},{9,8},{10,11... | collective-permute-start | bytes 614408 | tf_op jit(solution)/shard_map/ppermute | solution.py:415
  96.7 19.1 %collective-permute-start.11 = (bf16[4,80,640]{2,1,0:T(8,128)(2,1)S(1)}, bf16[4,80,640]{2,1,0:T(8,128)(2,1)S(1)}, u32[]{:S(2)}, u32[]{:S(2)}) collective-permute-start(bf16[4,80,640]{2,1,0:T(8,128)(2,1)S(1)} %pad_maximum_fusion.2.refs_1_), channel_id=1, source_target_pairs={{0,1},{1,0},{2,3},{3,2},{4,5},{5,4},{6,7},{7,6},{8,9},{9,8},{10,11... | collective-permute-start | bytes 1228808 | tf_op jit(solution)/shard_map/ppermute | solution.py:415
  98.2 21.1 %collective-permute-start.13 = (bf16[4,80,640]{2,1,0:T(8,128)(2,1)S(1)}, bf16[4,80,640]{2,1,0:T(8,128)(2,1)S(1)}, u32[]{:S(2)}, u32[]{:S(2)}) collective-permute-start(bf16[4,80,640]{2,1,0:T(8,128)(2,1)S(1)} %pad_maximum_fusion.2.refs_1_), channel_id=1, source_target_pairs={{0,2},{1,3},{2,0},{3,1},{4,6},{5,7},{6,4},{7,5},{8,10},{9,11},{10,... | collective-permute-start | bytes 1228808 | tf_op jit(solution)/shard_map/ppermute | solution.py:415
  98.2 21.1 %collective-permute-start.16 = (bf16[4,80,640]{2,1,0:T(8,128)(2,1)S(1)}, bf16[4,80,640]{2,1,0:T(8,128)(2,1)S(1)}, u32[]{:S(2)}, u32[]{:S(2)}) collective-permute-start(bf16[4,80,640]{2,1,0:T(8,128)(2,1)S(1)} %pad_maximum_fusion.2.refs_1_), channel_id=1, source_target_pairs={{0,3},{1,2},{2,1},{3,0},{4,7},{5,6},{6,5},{7,4},{8,11},{9,10},{10,... | collective-permute-start | bytes 1228808 | tf_op jit(solution)/shard_map/ppermute | solution.py:415
  101.6 17.8 %copy-start.8 = (f32[1,960]{1,0:T(1,128)S(1)}, f32[1,960]{1,0:T(1,128)}, u32[]{:S(2)}) copy-start(f32[1,960]{1,0:T(1,128)} %reshape_squeeze.9.refs_6_.refs_10_) | copy-start | bytes 11524
  101.7 29.5 %collective-permute-start.20 = (bf16[640,320]{1,0:T(8,128)(2,1)S(1)}, bf16[640,320]{1,0:T(8,128)(2,1)S(1)}, u32[]{:S(2)}, u32[]{:S(2)}) collective-permute-start(bf16[640,320]{1,0:T(8,128)(2,1)S(1)} %constant_dynamic-slice_fusion.1), channel_id=1, source_target_pairs={{0,1},{1,0},{2,3},{3,2},{4,5},{5,4},{6,7},{7,6},{8,9},{9,8},{10,11... | collective-permute-start | bytes 1228808 | tf_op jit(solution)/shard_map/ppermute | solution.py:415
  103.2 29.2 %collective-permute-start.22 = (bf16[640,320]{1,0:T(8,128)(2,1)S(1)}, bf16[640,320]{1,0:T(8,128)(2,1)S(1)}, u32[]{:S(2)}, u32[]{:S(2)}) collective-permute-start(bf16[640,320]{1,0:T(8,128)(2,1)S(1)} %constant_dynamic-slice_fusion.1), channel_id=1, source_target_pairs={{0,2},{1,3},{2,0},{3,1},{4,6},{5,7},{6,4},{7,5},{8,10},{9,11},{10,... | collective-permute-start | bytes 1228808 | tf_op jit(solution)/shard_map/ppermute | solution.py:415
  103.2 1.9 copy-start.2
  105.1 0.7 copy-start.7
  105.8 0.7 copy-start.10
  115.8 27.2 %copy-start.5 = (f32[1,1280]{1,0:T(1,128)S(1)}, f32[1,1280]{1,0:T(1,128)}, u32[]{:S(2)}) copy-start(f32[1,1280]{1,0:T(1,128)} %refs_9_.1) | copy-start | bytes 15364
  129.6 5.8 %collective-permute-start.17 = (bf16[160,640]{1,0:T(8,128)(2,1)S(1)}, bf16[160,640]{1,0:T(8,128)(2,1)S(1)}, u32[]{:S(2)}, u32[]{:S(2)}) collective-permute-start(bf16[160,640]{1,0:T(8,128)(2,1)S(1)} %get-tuple-element.45), channel_id=1, source_target_pairs={{0,1},{1,0},{2,3},{3,2},{4,5},{5,4},{6,7},{7,6},{8,9},{9,8},{10,11... | collective-permute-start | bytes 614408 | tf_op jit(solution)/shard_map/ppermute | solution.py:415
  130.2 6.8 %collective-permute-start.18 = (bf16[160,640]{1,0:T(8,128)(2,1)S(1)}, bf16[160,640]{1,0:T(8,128)(2,1)S(1)}, u32[]{:S(2)}, u32[]{:S(2)}) collective-permute-start(bf16[160,640]{1,0:T(8,128)(2,1)S(1)} %get-tuple-element.46), channel_id=1, source_target_pairs={{0,2},{1,3},{2,0},{3,1},{4,6},{5,7},{6,4},{7,5},{8,10},{9,11},{10,... | collective-permute-start | bytes 614408 | tf_op jit(solution)/shard_map/ppermute | solution.py:415
  131.2 9.5 %collective-permute-start.24 = (bf16[320,320]{1,0:T(8,128)(2,1)S(1)}, bf16[320,320]{1,0:T(8,128)(2,1)S(1)}, u32[]{:S(2)}, u32[]{:S(2)}) collective-permute-start(bf16[320,320]{1,0:T(8,128)(2,1)S(1)} %slice.51), channel_id=1, source_target_pairs={{0,2},{1,3},{2,0},{3,1},{4,6},{5,7},{6,4},{7,5},{8,10},{9,11},{10,... | collective-permute-start | bytes 614408 | tf_op jit(solution)/shard_map/ppermute | solution.py:415
  132.3 13.6 %collective-permute-start.21 = (bf16[640,320]{1,0:T(8,128)(2,1)S(1)}, bf16[640,320]{1,0:T(8,128)(2,1)S(1)}, u32[]{:S(2)}, u32[]{:S(2)}) collective-permute-start(bf16[640,320]{1,0:T(8,128)(2,1)S(1)} %collective-permute-done.20.refs_5_), channel_id=1, source_target_pairs={{0,4},{4,0},{8,12},{12,8},{16,20},{20,16},{24,28},{28,24},{1,5},{5... | collective-permute-start | bytes 1228808 | tf_op jit(solution)/shard_map/ppermute | solution.py:488
  132.4 13.6 %collective-permute-start.23 = (bf16[640,320]{1,0:T(8,128)(2,1)S(1)}, bf16[640,320]{1,0:T(8,128)(2,1)S(1)}, u32[]{:S(2)}, u32[]{:S(2)}) collective-permute-start(bf16[640,320]{1,0:T(8,128)(2,1)S(1)} %collective-permute-done.22.refs_7_), channel_id=1, source_target_pairs={{0,4},{4,0},{8,12},{12,8},{16,20},{20,16},{24,28},{28,24},{1,5},{5... | collective-permute-start | bytes 1228808 | tf_op jit(solution)/shard_map/ppermute | solution.py:488
  135.4 7.6 %collective-permute-start.25 = (bf16[320,320]{1,0:T(8,128)(2,1)S(1)}, bf16[320,320]{1,0:T(8,128)(2,1)S(1)}, u32[]{:S(2)}, u32[]{:S(2)}) collective-permute-start(bf16[320,320]{1,0:T(8,128)(2,1)S(1)} %slice.52), channel_id=1, source_target_pairs={{0,1},{1,0},{2,3},{3,2},{4,5},{5,4},{6,7},{7,6},{8,9},{9,8},{10,11... | collective-permute-start | bytes 614408 | tf_op jit(solution)/shard_map/ppermute | solution.py:415
  137.1 8.9 %copy-start.6 = (f32[1,1280]{1,0:T(1,128)S(1)}, f32[1,1280]{1,0:T(1,128)}, u32[]{:S(2)}) copy-start(f32[1,1280]{1,0:T(1,128)} %get-tuple-element.67.refs_13_) | copy-start | bytes 15364
  137.1 8.8 %collective-permute-start.19 = (bf16[160,640]{1,0:T(8,128)(2,1)S(1)}, bf16[160,640]{1,0:T(8,128)(2,1)S(1)}, u32[]{:S(2)}, u32[]{:S(2)}) collective-permute-start(bf16[160,640]{1,0:T(8,128)(2,1)S(1)} %get-tuple-element.47), channel_id=1, source_target_pairs={{0,3},{1,2},{2,1},{3,0},{4,7},{5,6},{6,5},{7,4},{8,11},{9,10},{10,... | collective-permute-start | bytes 614408 | tf_op jit(solution)/shard_map/ppermute | solution.py:415
  140.7 5.2 %collective-permute-start.26 = (bf16[320,320]{1,0:T(8,128)(2,1)S(1)}, bf16[320,320]{1,0:T(8,128)(2,1)S(1)}, u32[]{:S(2)}, u32[]{:S(2)}) collective-permute-start(bf16[320,320]{1,0:T(8,128)(2,1)S(1)} %collective-permute-done.24.refs_9_), channel_id=1, source_target_pairs={{0,4},{4,0},{8,12},{12,8},{16,20},{20,16},{24,28},{28,24},{1,5},{5... | collective-permute-start | bytes 614408 | tf_op jit(solution)/shard_map/ppermute | solution.py:488
  143.0 2.9 %collective-permute-start.27 = (bf16[320,320]{1,0:T(8,128)(2,1)S(1)}, bf16[320,320]{1,0:T(8,128)(2,1)S(1)}, u32[]{:S(2)}, u32[]{:S(2)}) collective-permute-start(bf16[320,320]{1,0:T(8,128)(2,1)S(1)} %collective-permute-done.25.refs_10_), channel_id=1, source_target_pairs={{0,4},{4,0},{8,12},{12,8},{16,20},{20,16},{24,28},{28,24},{1,5},{5... | collective-permute-start | bytes 614408 | tf_op jit(solution)/shard_map/ppermute | solution.py:488
  146.0 19.0 %copy-start.3 = (f32[1,1280]{1,0:T(1,128)S(1)}, f32[1,1280]{1,0:T(1,128)}, u32[]{:S(2)}) copy-start(f32[1,1280]{1,0:T(1,128)} %refs_3_.3) | copy-start | bytes 15364
  150.2 12.4 %collective-permute-start.30 = (bf16[160,1280]{1,0:T(8,128)(2,1)S(1)}, bf16[160,1280]{1,0:T(8,128)(2,1)}, u32[]{:S(2)}, u32[]{:S(2)}) collective-permute-start(bf16[160,1280]{1,0:T(8,128)(2,1)S(1)} %get-tuple-element.48.refs_0_.refs_4_), channel_id=1, source_target_pairs={{0,1},{1,0},{2,3},{3,2},{4,5},{5,4},{6,7},{7,6},{8,9},{9,8},{10,11... | collective-permute-start | bytes 1228808 | tf_op jit(solution)/shard_map/ppermute | solution.py:415
  151.7 12.7 %collective-permute-start.29 = (bf16[160,1280]{1,0:T(8,128)(2,1)}, bf16[160,1280]{1,0:T(8,128)(2,1)}, u32[]{:S(2)}, u32[]{:S(2)}) collective-permute-start(bf16[160,1280]{1,0:T(8,128)(2,1)} %get-tuple-element.49.refs_1_), channel_id=1, source_target_pairs={{0,2},{1,3},{2,0},{3,1},{4,6},{5,7},{6,4},{7,5},{8,10},{9,11},{10,... | collective-permute-start | bytes 1228808 | tf_op jit(solution)/shard_map/ppermute | solution.py:415
  152.4 20.7 %collective-permute-start.28 = (bf16[160,1280]{1,0:T(8,128)(2,1)S(1)}, bf16[160,1280]{1,0:T(8,128)(2,1)}, u32[]{:S(2)}, u32[]{:S(2)}) collective-permute-start(bf16[160,1280]{1,0:T(8,128)(2,1)S(1)} %get-tuple-element.48.refs_0_.refs_4_), channel_id=1, source_target_pairs={{0,2},{1,3},{2,0},{3,1},{4,6},{5,7},{6,4},{7,5},{8,10},{9,11},{10,... | collective-permute-start | bytes 1228808 | tf_op jit(solution)/shard_map/ppermute | solution.py:415
  153.7 19.4 %collective-permute-start.31 = (bf16[160,1280]{1,0:T(8,128)(2,1)}, bf16[160,1280]{1,0:T(8,128)(2,1)}, u32[]{:S(2)}, u32[]{:S(2)}) collective-permute-start(bf16[160,1280]{1,0:T(8,128)(2,1)} %get-tuple-element.49.refs_1_), channel_id=1, source_target_pairs={{0,1},{1,0},{2,3},{3,2},{4,5},{5,4},{6,7},{7,6},{8,9},{9,8},{10,11... | collective-permute-start | bytes 1228808 | tf_op jit(solution)/shard_map/ppermute | solution.py:415
  162.7 18.5 %collective-permute-start.33 = (bf16[160,1280]{1,0:T(8,128)(2,1)}, bf16[160,1280]{1,0:T(8,128)(2,1)}, u32[]{:S(2)}, u32[]{:S(2)}) collective-permute-start(bf16[160,1280]{1,0:T(8,128)(2,1)} %collective-permute-done.30.refs_2_), channel_id=1, source_target_pairs={{0,2},{1,3},{2,0},{3,1},{4,6},{5,7},{6,4},{7,5},{8,10},{9,11},{10,... | collective-permute-start | bytes 1228808 | tf_op jit(solution)/shard_map/ppermute | solution.py:415
  164.3 16.8 %collective-permute-start.34 = (bf16[160,1280]{1,0:T(8,128)(2,1)}, bf16[160,1280]{1,0:T(8,128)(2,1)}, u32[]{:S(2)}, u32[]{:S(2)}) collective-permute-start(bf16[160,1280]{1,0:T(8,128)(2,1)} %collective-permute-done.29.refs_1_), channel_id=1, source_target_pairs={{0,1},{1,0},{2,3},{3,2},{4,5},{5,4},{6,7},{7,6},{8,9},{9,8},{10,11... | collective-permute-start | bytes 1228808 | tf_op jit(solution)/shard_map/ppermute | solution.py:415
  164.9 2.9 %copy-start = (bf16[1280,2560]{1,0:T(8,128)(2,1)S(1)}, bf16[1280,2560]{1,0:T(8,128)(2,1)}, u32[]{:S(2)}) copy-start(bf16[1280,2560]{1,0:T(8,128)(2,1)} %all-gather.5.cloned.1.call-done.refs_2_.refs_4_) | copy-start | bytes 19660804
  167.8 5.3 %copy-start.1 = (bf16[1280,2560]{1,0:T(8,128)(2,1)S(1)}, bf16[1280,2560]{1,0:T(8,128)(2,1)}, u32[]{:S(2)}) copy-start(bf16[1280,2560]{1,0:T(8,128)(2,1)} %all-gather.5.cloned.1.call-done.refs_2_.refs_4_) | copy-start | bytes 19660804
  184.7 30.8 %copy-start.4 = (f32[1,1280]{1,0:T(1,128)S(1)}, f32[1,1280]{1,0:T(1,128)}, u32[]{:S(2)}) copy-start(f32[1,1280]{1,0:T(1,128)} %refs_7_.1) | copy-start | bytes 15364
  184.7 30.8 %copy-start.11 = (s32[2]{0:T(128)S(1)}, s32[2]{0:T(128)}, u32[]{:S(2)}) copy-start(s32[2]{0:T(128)} %pad_add_fusion.place_ref) | copy-start | bytes 28
  184.8 12.4 %collective-permute-start.35 = (bf16[160,1280]{1,0:T(8,128)(2,1)S(1)}, bf16[160,1280]{1,0:T(8,128)(2,1)S(1)}, u32[]{:S(2)}, u32[]{:S(2)}) collective-permute-start(bf16[160,1280]{1,0:T(8,128)(2,1)S(1)} %get-tuple-element.55), channel_id=1, source_target_pairs={{0,2},{1,3},{2,0},{3,1},{4,6},{5,7},{6,4},{7,5},{8,10},{9,11},{10,... | collective-permute-start | bytes 1228808 | tf_op jit(solution)/shard_map/ppermute | solution.py:415
  185.1 23.9 %collective-permute-start.32 = (bf16[160,1280]{1,0:T(8,128)(2,1)}, bf16[160,1280]{1,0:T(8,128)(2,1)}, u32[]{:S(2)}, u32[]{:S(2)}) collective-permute-start(bf16[160,1280]{1,0:T(8,128)(2,1)} %get-tuple-element.52), channel_id=1, source_target_pairs={{0,1},{1,0},{2,3},{3,2},{4,5},{5,4},{6,7},{7,6},{8,9},{9,8},{10,11... | collective-permute-start | bytes 1228808 | tf_op jit(solution)/shard_map/ppermute | solution.py:415
  185.9 20.5 %collective-permute-start.37 = (bf16[160,1280]{1,0:T(8,128)(2,1)S(1)}, bf16[160,1280]{1,0:T(8,128)(2,1)S(1)}, u32[]{:S(2)}, u32[]{:S(2)}) collective-permute-start(bf16[160,1280]{1,0:T(8,128)(2,1)S(1)} %get-tuple-element.56), channel_id=1, source_target_pairs={{0,1},{1,0},{2,3},{3,2},{4,5},{5,4},{6,7},{7,6},{8,9},{9,8},{10,11... | collective-permute-start | bytes 1228808 | tf_op jit(solution)/shard_map/ppermute | solution.py:415
  187.1 21.9 %collective-permute-start.39 = (bf16[160,1280]{1,0:T(8,128)(2,1)}, bf16[160,1280]{1,0:T(8,128)(2,1)}, u32[]{:S(2)}, u32[]{:S(2)}) collective-permute-start(bf16[160,1280]{1,0:T(8,128)(2,1)} %get-tuple-element.57), channel_id=1, source_target_pairs={{0,2},{1,3},{2,0},{3,1},{4,6},{5,7},{6,4},{7,5},{8,10},{9,11},{10,... | collective-permute-start | bytes 1228808 | tf_op jit(solution)/shard_map/ppermute | solution.py:415
  197.3 16.2 %collective-permute-start.36 = (bf16[160,1280]{1,0:T(8,128)(2,1)S(1)}, bf16[160,1280]{1,0:T(8,128)(2,1)}, u32[]{:S(2)}, u32[]{:S(2)}) collective-permute-start(bf16[160,1280]{1,0:T(8,128)(2,1)S(1)} %add_convert_fusion.1), channel_id=1, source_target_pairs={{0,1},{1,0},{2,3},{3,2},{4,5},{5,4},{6,7},{7,6},{8,9},{9,8},{10,11... | collective-permute-start | bytes 1228808 | tf_op jit(solution)/shard_map/ppermute | solution.py:415
  207.3 8.3 %collective-permute-start.38 = (bf16[160,1280]{1,0:T(8,128)(2,1)}, bf16[160,1280]{1,0:T(8,128)(2,1)}, u32[]{:S(2)}, u32[]{:S(2)}) collective-permute-start(bf16[160,1280]{1,0:T(8,128)(2,1)} %add_convert_fusion), channel_id=1, source_target_pairs={{0,2},{1,3},{2,0},{3,1},{4,6},{5,7},{6,4},{7,5},{8,10},{9,11},{10,... | collective-permute-start | bytes 1228808 | tf_op jit(solution)/shard_map/ppermute | solution.py:415
Sparse Core Ops, SparseCore 0:
  9.7 43.0 all-gather.2
  54.4 77.0 all-gather.4

commit v3 on v2

--- a/solution.py
+++ b/solution.py
@@ -27,7 +27,8 @@
 def embed_kernel(place_ref, keep_ref, patches_ref, position_ref, *refs):
     out_refs, token_ref = refs[:-1], refs[-1]
     per, patch_count, _ = patches_ref.shape
-    row = keep_ref[0].astype(F32)
+    first = pl.program_id(0) * per
+    row = jnp.concatenate([keep_ref[pl.ds(first + i, 1)] for i in range(per)], axis=1).astype(F32)
     tokens = row.shape[1]
     kept = jnp.broadcast_to(row, (tokens, tokens)).T
     reps = (patch_count + tokens - 1) // tokens
@@ -59,7 +60,7 @@
         grid=(steps,),
         in_specs=[
             pl.BlockSpec(memory_space=pltpu.SMEM),
-            pl.BlockSpec((1, 1, tokens), lambda i: (i, 0, 0)),
+            pl.BlockSpec(keep.shape, lambda i: (0, 0)),
             pl.BlockSpec((per, patch_count, width), lambda i: (i, 0, 0)),
             pl.BlockSpec((patch_count, width), lambda i: (0, 0)),
         ],
@@ -69,7 +70,27 @@
         compiler_params=params(60),
         cost_estimate=cost(4e9, patches.size * 2),
         name="embed",
-    )(place, keep.reshape(steps, 1, tokens), patches, position)
+    )(place, keep, patches, position)
+
+
+def join_kernel(qkv_ref, out_ref, joined_ref):
+    joined_ref[...] = jnp.concatenate(
+        [out_ref[...]] + [qkv_ref[t] for t in range(qkv_ref.shape[0])], axis=1
+    )
+
+
+def join(w_qkv, w_o):
+    kinds, rows, width = w_qkv.shape
+    vmem = pl.BlockSpec(memory_space=pltpu.VMEM)
+    return pl.pallas_call(
+        join_kernel,
+        in_specs=[vmem] * 2,
+        out_specs=vmem,
+        out_shape=jax.ShapeDtypeStruct((rows, (kinds + 1) * width), BF),
+        compiler_params=params(60),
+        cost_estimate=cost(1e8, 4 * rows * kinds * width),
+        name="join",
+    )(w_qkv, w_o)
 
 
 def pack_kernel(fold, slot_rows, group, n_src, place_ref, target_ref, *refs):
@@ -196,71 +217,91 @@
             prob = (e * (1.0 / jnp.sum(e, axis=1, keepdims=True))).astype(BF)
             outs = jnp.where(lane_head == h, jnp.dot(prob, v, preferred_element_type=F32), outs)
         results.append(outs)
-    return jnp.concatenate(results, axis=1).astype(BF)
-
-
-def attend_kernel(counts, blocks, last, spm, fold, hc, place_ref, *refs):
+    piece = slot_rows // 2
+    return [jnp.concatenate([r[:piece], r[piece:]], axis=1).astype(BF) for r in results]
+
+
+def attend_kernel(counts, blocks, priors, spm, fold, hc, place_ref, *refs):
     n_mp = len(counts)
     groups, refs = cut(refs, counts)
     operands, refs = list(refs[:6]), refs[6:]
-    prior, refs = (refs[0], refs[1:]) if last else (None, refs)
-    outs = n_mp if last else 1
+    prior_refs, refs = refs[: len(priors)], refs[len(priors) :]
+    outs = n_mp * spm if priors else 1
     out_refs, (norm_ref, buf_ref, sem_ref, mine_ref) = refs[:outs], refs[outs:]
     for i, block in enumerate(blocks):
         fetch_start(groups, block, spm, buf_ref.at[i], sem_ref.at[i])
-    for i, block in enumerate(blocks):
+
+    def one(i, _):
         fetch_wait(groups, spm, buf_ref.at[i], sem_ref.at[i])
         gathered = [unfold(buf_ref[i, k], fold) for k in range(n_mp)]
-        value = attend_block(block, gathered, place_ref[0], operands + [norm_ref], hc, spm)
-        if last:
-            mine_ref[i] = value
-        else:
-            out_refs[0][i] = value
-    if last:
+        values = attend_block(
+            blocks[0] + i, gathered, place_ref[0], operands + [norm_ref], hc, spm
+        )
+        for s, value in enumerate(values):
+            (mine_ref if priors else out_refs[0])[i, s] = value
+        return 0
+
+    lax.fori_loop(0, len(blocks), one, 0)
+    if priors:
         for k in range(n_mp):
             block = owner_block(place_ref, k, spm)
-            before = prior[jnp.minimum(block, blocks[0] - 1)]
-            later = mine_ref[jnp.maximum(block - blocks[0], 0)]
-            out_refs[k][...] = jnp.where(block < blocks[0], before, later)
-
-
-def attend(place, gathered, blocks, prior, fold, hc, operands, spm):
+            for s in range(spm):
+                value = mine_ref[jnp.maximum(block - blocks[0], 0), s]
+                low = 0
+                for ref, count in zip(prior_refs, priors):
+                    before = ref[jnp.clip(block - low, 0, count - 1), s]
+                    value = jnp.where(
+                        jnp.logical_and(block >= low, block < low + count), before, value
+                    )
+                    low += count
+                out_refs[k * spm + s][...] = value
+
+
+def attend(place, gathered, blocks, priors, fold, hc, operands, spm):
     n_mp = len(gathered)
     _, piece, lanes = gathered[0][0].shape
     slot_rows = operands[4].shape[2]
     flat = sum(gathered, [])
     smem = pl.BlockSpec(memory_space=pltpu.SMEM)
     vmem = pl.BlockSpec(memory_space=pltpu.VMEM)
-    last = prior is not None
-    shape = (slot_rows, spm * hc)
-    if last:
-        out_shape = [jax.ShapeDtypeStruct(shape, BF)] * n_mp
+    shape = (slot_rows // 2, 2 * hc)
+    if priors:
+        out_shape = [jax.ShapeDtypeStruct(shape, BF)] * (n_mp * spm)
     else:
-        out_shape = [jax.ShapeDtypeStruct((len(blocks), *shape), BF)]
-    return pl.pallas_call(
+        out_shape = [jax.ShapeDtypeStruct((len(blocks), spm, *shape), BF)]
+    outs = pl.pallas_call(
         functools.partial(
-            attend_kernel, [len(g) for g in gathered], blocks, last, spm, fold, hc
+            attend_kernel,
+            [len(g) for g in gathered],
+            blocks,
+            [p.shape[0] for p in priors],
+            spm,
+            fold,
+            hc,
         ),
         in_specs=[smem]
         + [pl.BlockSpec(memory_space=pltpu.HBM)] * len(flat)
-        + [vmem] * (len(operands) + last),
+        + [vmem] * (len(operands) + len(priors)),
         out_specs=[vmem] * len(out_shape),
         scratch_shapes=[
             pltpu.VMEM((n_mp, spm * slot_rows, lanes // fold), BF),
             pltpu.VMEM((len(blocks), n_mp, spm, piece, lanes), BF),
             pltpu.SemaphoreType.DMA((len(blocks), n_mp)),
-            pltpu.VMEM((len(blocks), *shape), BF),
+            pltpu.VMEM((len(blocks), spm, *shape), BF),
         ],
         out_shape=out_shape,
         compiler_params=params(24),
         cost_estimate=cost(len(blocks) * 4e9, operands[0].size * 4),
         name="attend",
-    )(place, *flat, *operands, *([prior] if last else []))
+    )(place, *flat, *operands, *priors)
+    if not priors:
+        return outs[0]
+    return [outs[k * spm : (k + 1) * spm] for k in range(n_mp)]
 
 
 def own_kernel(counts, spm, fold, place_ref, *refs):
     n_mp = len(counts)
-    groups, (bias_ref, out_ref, buf_ref, sem_ref) = cut(refs, counts)
+    groups, (bias_ref, *out_refs, buf_ref, sem_ref) = cut(refs, counts)
     fetch_start(groups, owner_block(place_ref, 0, spm), spm, buf_ref, sem_ref)
     fetch_wait(groups, spm, buf_ref, sem_ref)
     blocks = [unfold(buf_ref[k], fold) for k in range(n_mp)]
@@ -270,7 +311,10 @@
         for k in range(1, n_mp):
             value = jnp.where(jnp.bitwise_xor(place_ref[0], k) == j, blocks[k], value)
         ordered.append(value)
-    out_ref[...] = jnp.concatenate(ordered, axis=1) + bias_ref[...]
+    value = jnp.concatenate(ordered, axis=1) + bias_ref[...]
+    rows = value.shape[0] // spm
+    for s in range(spm):
+        out_refs[s][...] = value[s * rows : (s + 1) * rows]
 
 
 def own_rows(place, gathered, fold, bias, spm):
@@ -283,8 +327,8 @@
         in_specs=[pl.BlockSpec(memory_space=pltpu.SMEM)]
         + [pl.BlockSpec(memory_space=pltpu.HBM)] * len(features)
         + [vmem],
-        out_specs=vmem,
-        out_shape=jax.ShapeDtypeStruct((spm * piece * fold, bias.shape[1]), F32),
+        out_specs=[vmem] * spm,
+        out_shape=[jax.ShapeDtypeStruct((piece * fold, bias.shape[1]), F32)] * spm,
         scratch_shapes=[
             pltpu.VMEM((n_mp, spm, piece, lanes), BF),
             pltpu.SemaphoreType.DMA((n_mp,)),
@@ -295,7 +339,7 @@
     )(place, *features, bias)
 
 
-def project_kernel(out_counts, spm, hc, place_ref, base_ref, *refs):
+def project_kernel(out_counts, hc, place_ref, base_ref, *refs):
     n_mp = len(out_counts)
     att_refs, at = refs[:n_mp], n_mp
     own_ref, at = refs[at], at + 1
@@ -303,7 +347,7 @@
     core = place_ref[1] % 2
     mine, mate = None, None
     for k, count in enumerate(out_counts):
-        left = jnp.concatenate([att_refs[k][:, s * hc : (s + 1) * hc] for s in range(spm)], axis=0)
+        left = jnp.concatenate([att_refs[k][:, :hc], att_refs[k][:, hc:]], axis=0)
         if k == 0:
             pair = [
                 [own_ref[pl.ds(pl.multiple_of(c * half, 128), half)]] for c in (core, 1 - core)
@@ -321,32 +365,30 @@
     total = jnp.concatenate(
         [jnp.where(core == 0, mine, mate), jnp.where(core == 0, mate, mine)], axis=1
     )
-    gain_ref, shift_ref, res_ref, *out_refs = refs[at:]
+    gain_ref, shift_ref, _, res_ref, out_ref = refs[at:]
     value = base_ref[...] + total
     res_ref[...] = value
     mean = jnp.mean(value, axis=1, keepdims=True)
     value = value - mean
     spread = jnp.mean(value * value, axis=1, keepdims=True)
-    value = (value * lax.rsqrt(spread + 1e-06) * gain_ref[...] + shift_ref[...]).astype(BF)
-    each = out_refs[0].shape[0]
-    for i, ref in enumerate(out_refs):
-        ref[...] = value[i * each : (i + 1) * each]
-
-
-def project(place, base, hc, attended, out_weights, gain, shift, spm):
+    out_ref[...] = (value * lax.rsqrt(spread + 1e-06) * gain_ref[...] + shift_ref[...]).astype(BF)
+
+
+def project(place, base, hc, attended, out_weights, gain, shift, last):
     n_mp = len(attended)
     weights = sum([sum(w, []) for w in out_weights], [])
     vmem = pl.BlockSpec(memory_space=pltpu.VMEM)
     return pl.pallas_call(
-        functools.partial(project_kernel, [len(w[0]) for w in out_weights], spm, hc),
-        in_specs=[pl.BlockSpec(memory_space=pltpu.SMEM)] + [vmem] * (n_mp + len(weights) + 3),
-        out_specs=[vmem] * 3,
-        out_shape=[jax.ShapeDtypeStruct(base.shape, F32)]
-        + [jax.ShapeDtypeStruct((base.shape[0] // 2, base.shape[1]), BF)] * 2,
+        functools.partial(project_kernel, [len(w[0]) for w in out_weights], hc),
+        in_specs=[pl.BlockSpec(memory_space=pltpu.SMEM)]
+        + [vmem] * (n_mp + len(weights) + 3)
+        + [pl.BlockSpec(memory_space=pl.ANY)],
+        out_specs=[vmem] * 2,
+        out_shape=[jax.ShapeDtypeStruct(base.shape, F32), jax.ShapeDtypeStruct(base.shape, BF)],
         compiler_params=params(20),
-        cost_estimate=cost(3e9, 16 * base.size),
+        cost_estimate=cost(2e9, 16 * base.size),
         name="project",
-    )(place, base, *attended, *weights, gain, shift)
+    )(place, base, *attended, *weights, gain, shift, last)
 
 
 def mlp_kernel(count, *refs):
@@ -383,32 +425,63 @@
     )(*rows, weight, bias, after)
 
 
-def finish_kernel(adds, pieces, spm, place_ref, *refs):
-    add_refs, (res_ref, bias_ref, lab_ref, out_ref) = refs[:adds], refs[adds:]
-    each = res_ref.shape[0] // pieces
-    labels = lab_ref[...].reshape(res_ref.shape[0], 1)
-    turn = place_ref[1] % spm
+def settle_kernel(adds, pieces, *refs):
+    add_refs, res_refs, bias_ref, out_refs = (
+        refs[:adds],
+        refs[adds : adds + pieces],
+        refs[adds + pieces],
+        refs[adds + pieces + 1 :],
+    )
     for s in range(pieces):
-        at = slice(s * each, (s + 1) * each)
-        value = res_ref[at] + bias_ref[...]
+        value = res_refs[s][...] + bias_ref[...]
         for i in range(s, adds, pieces):
             value = value + add_refs[i][...].astype(F32)
-        value = jnp.where(labels[at] >= 0, value, 0.0).astype(BF)
+        out_refs[s][...] = value
+
+
+def settle(added, residual, bias):
+    vmem = pl.BlockSpec(memory_space=pltpu.VMEM)
+    return pl.pallas_call(
+        functools.partial(settle_kernel, len(added), len(residual)),
+        in_specs=[vmem] * (len(added) + len(residual) + 1),
+        out_specs=[vmem] * len(residual),
+        out_shape=[jax.ShapeDtypeStruct(r.shape, F32) for r in residual],
+        compiler_params=params(16),
+        cost_estimate=cost(1e9, residual[0].size * 24),
+        name="settle",
+    )(*added, *residual, bias)
+
+
+def finish_kernel(adds, pieces, place_ref, *refs):
+    add_refs, res_refs, lab_ref, out_ref = (
+        refs[:adds],
+        refs[adds : adds + pieces],
+        refs[adds + pieces],
+        refs[adds + pieces + 1],
+    )
+    each = res_refs[0].shape[0]
+    turn = place_ref[1] % pieces
+    for s in range(pieces):
+        value = res_refs[s][...]
+        for i in range(s, adds, pieces):
+            value = value + add_refs[i][...].astype(F32)
+        value = jnp.where(lab_ref[s] >= 0, value, 0.0).astype(BF)
         out_ref[pl.ds(pl.multiple_of(jnp.bitwise_xor(turn, s) * each, 16), each)] = value
 
 
-def finish(place, added, pieces, residual, bias, labels, spm):
+def finish(place, added, residual, labels):
     smem = pl.BlockSpec(memory_space=pltpu.SMEM)
     vmem = pl.BlockSpec(memory_space=pltpu.VMEM)
-    return pl.pallas_call(
-        functools.partial(finish_kernel, len(added), pieces, spm),
-        in_specs=[smem] + [vmem] * (len(added) + 3),
+    rows, width = residual[0].shape
+    return pl.pallas_call(
+        functools.partial(finish_kernel, len(added), len(residual)),
+        in_specs=[smem] + [vmem] * (len(added) + len(residual) + 1),
         out_specs=vmem,
-        out_shape=jax.ShapeDtypeStruct(residual.shape, BF),
+        out_shape=jax.ShapeDtypeStruct((rows * len(residual), width), BF),
         compiler_params=params(16),
-        cost_estimate=cost(1e9, residual.size * 8),
+        cost_estimate=cost(1e9, rows * width * 16),
         name="finish",
-    )(place, *added, residual, bias, labels)
+    )(place, *added, *residual, labels)
 
 
 def hop(value, k, n):
@@ -418,8 +491,10 @@
 def gather_blocks(values, n, direct=False):
     if n != 4:
         return [values] + [[hop(v, k, n) for v in values] for k in range(1, n)]
-    x = [hop(v, 1, n) for v in values]
-    y = [hop(v, 2, n) for v in values[::-1]][::-1]
+    x, y = [], []
+    for v in values:
+        x.append(hop(v, 1, n))
+        y.append(hop(v, 2, n))
     if direct:
         return [values, x, y, [hop(v, 3, n) for v in values]]
     half = values[0].shape[0] // 2
@@ -435,14 +510,12 @@
 def scatter_blocks(partials, n):
     own = list(partials[0])
     if n != 4 or len(own) != 2:
-        for k in range(1, n):
-            own += [hop(p, k, n) for p in partials[k]]
-        return own
+        return own, [hop(p, k, n) for k in range(1, n) for p in partials[k]]
     far, x, y = partials[3], partials[1], partials[2]
     x0, y1 = hop(x[0], 1, n), hop(y[1], 2, n)
     first, second = hop(far[0], 1, n), hop(far[1], 2, n)
     y0, x1 = hop(plus(y[0], first), 2, n), hop(plus(x[1], second), 1, n)
-    return own + [x0, x1, y0, y1]
+    return own + [x0, y1], [y0, x1]
 
 
 def per_device(
@@ -475,7 +548,7 @@
     hc = w_qkv.shape[3]
     place = jnp.stack([m, d]).astype(jnp.int32)
 
-    mixed = jnp.concatenate([w_o[0].T, w_qkv[0, 0], w_qkv[0, 1], w_qkv[0, 2]], axis=1)
+    mixed = join(w_qkv[0], w_o[0].T)
     mixed = lax.all_gather(mixed, "dp", axis=0, tiled=True)
     tokens = embed(place, patches, position, keep, n_mp)
     featured = [tokens[0]] + [hop(tokens[k], k, n_mp) for k in range(1, n_mp)]
@@ -499,12 +572,13 @@
     fold = 2
     packed = pack(place, featured, target, n_dp, slot_rows, fold)
     half = n_dp // 2
+    bounds = [0, half, n_dp]
     moved = [packed[0]]
     for i in range(1, n_dp):
         moved.append(lax.ppermute(packed[i], "dp", [(j, j ^ i) for j in range(n_dp)]))
-    near = jnp.stack(moved[:half])
-    far = jnp.stack(moved[half:])
-    halves = [near, far]
+    stacks = []
+    for i in range(2):
+        stacks.append(jnp.stack(moved[bounds[i] : bounds[i + 1]]))
     both = jnp.concatenate([w_up[0], w_down[0].T], axis=1)
     both = lax.all_gather(both, "dp", axis=0, tiled=True)
 
@@ -519,35 +593,55 @@
     labrow = labels.reshape(n_dp, 1, slot_rows)
     labcol = labels.reshape(n_dp, slot_rows, 1)
 
-    moved = [gather_blocks([h], n_mp, i == 1) for i, h in enumerate(halves)]
-    gathered = [sum(pieces, []) for pieces in zip(*moved)]
+    moved = [gather_blocks([v], n_mp, i > 0) for i, v in enumerate(stacks)]
     gain = ln_gain[0, 0].reshape(n_mp, 1, feat)
     shift = ln_bias[0, 0].reshape(n_mp, 1, feat)
     bias = b_qkv[0].reshape(1, 3 * hc)
     operands = (mixed, bias, gain, shift, labrow, labcol)
-    count = n_dp // spm
-    ahead = list(range(count // 2))
-    prior = attend(place, moved[0], ahead, None, fold, hc, operands, spm)[0]
-    attended = attend(
-        place, gathered, list(range(count // 2, count)), prior, fold, hc, operands, spm
-    )
-    attended = [attended[0]] + [hop(attended[k], k, n_mp) for k in range(1, n_mp)]
+    priors = []
+    for i in range(2):
+        gathered = [sum(pieces, []) for pieces in zip(*moved[: i + 1])]
+        attended = attend(
+            place,
+            gathered,
+            list(range(bounds[i] // spm, bounds[i + 1] // spm)),
+            priors if i else [],
+            fold,
+            hc,
+            operands,
+            spm,
+        )
+        priors.append(attended)
+    pieces = []
+    for s in range(spm):
+        pieces.append(
+            [attended[0][s]] + [hop(attended[k][s], k, n_mp) for k in range(1, n_mp)]
+        )
     base = own_rows(place, gathered, fold, b_o, spm)
-    residual, *normed = project(
-        place, base, hc, attended, out_weights, ln_gain[0, 1:2], ln_bias[0, 1:2], spm
-    )
+    residual, normed = [], []
+    last = base[0]
+    for s in range(spm):
+        kept, last = project(
+            place, base[s], hc, pieces[s], out_weights, ln_gain[0, 1:2], ln_bias[0, 1:2], last
+        )
+        residual.append(kept)
+        normed.append(last)
     blocks = gather_blocks(normed, n_mp)
-    partials = [None] * n_mp
+    partials = [[None] * spm for _ in range(n_mp)]
     last = normed[0]
-    groups = [[0], [2, 1], [3]] if n_mp == 4 else [[k] for k in range(n_mp)]
+    if n_mp == 4 and spm == 2:
+        groups = [[(0, 0), (0, 1)], [(1, 0), (2, 1)], [(1, 1), (2, 0)], [(3, 0), (3, 1)]]
+    else:
+        groups = [[(k, i) for i in range(spm)] for k in range(n_mp)]
     for group in groups:
-        outs = mlp(sum([blocks[k] for k in group], []), 2 * len(group), both, b_up, last)
+        outs = mlp([blocks[k][i] for k, i in group], len(group), both, b_up, last)
         last = outs[0]
-        for i, k in enumerate(group):
-            partials[k] = outs[2 * i : 2 * i + 2]
-    added = scatter_blocks(partials, n_mp)
+        for (k, i), out in zip(group, outs):
+            partials[k][i] = out
+    early, late = scatter_blocks(partials, n_mp)
+    settled = settle(early, residual, b_down)
     own_labels = lax.dynamic_slice_in_dim(labcol, jnp.bitwise_xor(m, d // spm) * spm, spm)
-    return finish(place, added, 2, residual, b_down, own_labels, spm)
+    return finish(place, late, settled, own_labels)
 
 
 def solution(mesh):

time: 229 us -> 231 us (level)
    unnamed x42 -> x38, local copies, waits for them, and re-layouts: 7.18 us -> 9.82 us
    ppermute x29 -> x32, waiting for transfers between devices: 64.9 us -> 66.4 us  [hop(): return lax.ppermute(value, 'mp', [(i, i ^ k) for i in range(n)])]
    pallas_call x3 -> x4, Pallas kernels: 13.9 us -> 12.6 us  [mlp(): pl.pallas_call(functools.partial(mlp_kernel, len(rows)), in_specs=[vmem]...]
    pallas_call x1 -> x2, Pallas kernels: 4.25 us -> 4.96 us  [project(): pl.pallas_call(functools.partial(project_kernel, [len(w[0]) for w in out_...]
    ppermute x29 -> x32, starting transfers between devices: 32 us -> 32.3 us  [hop(): return lax.ppermute(value, 'mp', [(i, i ^ k) for i in range(n)])]
  transfers between devices with their start and end apart: 42 -> 45, of which waited for: 20 -> 19; matrix products, arithmetic and copies ran while one was open for 4% -> 4% of each run, Pallas kernels for 20% -> 20%
where the time goes in v3:
time: 231 us; the launch traced here: 228 us
  waiting for transfers between devices  101 us (44%)
  Pallas kernels  52.2 us (23%)
  starting transfers between devices  41.2 us (18%)
  local copies, waits for them, and re-layouts  14.2 us (6%)
  between operations  13.8 us (6%)
  other arithmetic  5.2 us (2%)
    ppermute x32, waiting for transfers between devices, hop(): return lax.ppermute(value, 'mp', [(i, i ^ k) for i in range(n)])  66.4 us
    ppermute x7, waiting for transfers between devices, per_device(): lax.ppermute(packed[i], 'dp', [(j, j ^ i) for j in range(n_dp)])  34.6 us
    ppermute x32, starting transfers between devices, hop(): return lax.ppermute(value, 'mp', [(i, i ^ k) for i in range(n)])  32.3 us
    pallas_call x2, Pallas kernels, attend(): pl.pallas_call(functools.partial(attend_kernel, [len(g) for g in gathered...  19.2 us
    pallas_call x4, Pallas kernels, mlp(): pl.pallas_call(functools.partial(mlp_kernel, len(rows)), in_specs=[vmem]...  12.6 us
    unnamed x38, local copies, waits for them, and re-layouts  9.82 us
    ppermute x7, starting transfers between devices, per_device(): lax.ppermute(packed[i], 'dp', [(j, j ^ i) for j in range(n_dp)])  7.89 us
    pallas_call x1, Pallas kernels, embed(): pl.pallas_call(embed_kernel, grid=(steps,), in_specs=[pl.BlockSpec(memory...  5.88 us
  transfers between devices with their start and end apart: 45, of which 19 were waited for; matrix products, arithmetic and copies ran while one was open for 4% of the time, Pallas kernels for 20%

profile of v3, /device:TPU:0, one launch (start us, length us, event | category | flops | bytes accessed | tf_op | source)
XLA Modules:
  0.0 227.7 jit_solution(11684763437213213317)
XLA Ops:
  6.5 1.9 join.1
  8.5 2.1 pad_maximum_fusion
  11.3 5.9 %embed.1 = (bf16[320,512]{1,0:T(8,128)(2,1)}, bf16[320,512]{1,0:T(8,128)(2,1)}, bf16[320,512]{1,0:T(8,128)(2,1)}, bf16[320,512]{1,0:T(8,128)(2,1)}) custom-call(s32[2]{0:T(128)} %pad_add_fusion.place_ref, s32[8,64]{1,0:T(8,128)} %keep_ref.1, bf16[8,256,1280]{2,1,0:T(8,128)(2,1)} %patches_ref.1, bf16[256,1280]{1,0:T(8,128)(2,1)} %position_ref.1), custom_call_target="tpu_custom_call" | custom-call | flops 4000000000 | bytes 5242880 | tf_op jit(solution)/shard_map/embed/pallas_call | solution.py:58
  17.1 3.0 %collective-permute-start = (bf16[320,512]{1,0:T(8,128)(2,1)}, bf16[320,512]{1,0:T(8,128)(2,1)S(1)}, u32[]{:S(2)}, u32[]{:S(2)}) collective-permute-start(bf16[320,512]{1,0:T(8,128)(2,1)} %get-tuple-element.42), channel_id=1, source_target_pairs={{0,1},{1,0},{2,3},{3,2},{4,5},{5,4},{6,7},{7,6},{8,9},{9,8},{10,11... | collective-permute-start | bytes 983048 | tf_op jit(solution)/shard_map/ppermute | solution.py:488
  20.1 1.5 collective-permute-start.1
  22.5 6.4 %collective-permute-done.refs_1_ = bf16[320,512]{1,0:T(8,128)(2,1)S(1)} collective-permute-done((bf16[320,512]{1,0:T(8,128)(2,1)}, bf16[320,512]{1,0:T(8,128)(2,1)S(1)}, u32[]{:S(2)}, u32[]{:S(2)}) %collective-permute-start) | collective-permute-done | bytes 327712 | tf_op jit(solution)/shard_map/ppermute | solution.py:488
  28.9 7.6 %collective-permute-done.1.refs_2_ = bf16[320,512]{1,0:T(8,128)(2,1)S(1)} collective-permute-done((bf16[320,512]{1,0:T(8,128)(2,1)}, bf16[320,512]{1,0:T(8,128)(2,1)S(1)}, u32[]{:S(2)}, u32[]{:S(2)}) %collective-permute-start.1) | collective-permute-done | bytes 327712 | tf_op jit(solution)/shard_map/ppermute | solution.py:488
  36.5 1.0 copy-done.13
  37.5 3.5 %pack.1 = (bf16[80,640]{1,0:T(8,128)(2,1)S(1)}, bf16[80,640]{1,0:T(8,128)(2,1)S(1)}, bf16[80,640]{1,0:T(8,128)(2,1)S(1)}, bf16[80,640]{1,0:T(8,128)(2,1)S(1)}, b...) custom-call(s32[2]{0:T(128)S(1)} %copy-done.8, ...), custom_call_target="tpu_custom_call" | custom-call | flops 4000000000 | bytes 1310720 | tf_op jit(solution)/shard_map/pack/pallas_call | solution.py:125
  41.1 1.6 collective-permute-start.4
  42.9 7.6 %collective-permute-done.5 = bf16[80,640]{1,0:T(8,128)(2,1)S(1)} collective-permute-done((bf16[80,640]{1,0:T(8,128)(2,1)S(1)}, bf16[80,640]{1,0:T(8,128)(2,1)S(1)}, u32[]{:S(2)}, u32[]{:S(2)}) %collective-permute-start.5) | collective-permute-done | bytes 102432 | tf_op jit(solution)/shard_map/ppermute | solution.py:578
  50.6 2.2 collective-permute-done.4
  52.8 1.5 collective-permute-start.10
  54.4 1.5 collective-permute-start.12
  56.4 1.6 collective-permute-start.9
  58.0 1.4 collective-permute-start.8
  59.9 4.5 %collective-permute-done.10.refs_2_.refs_1_ = bf16[4,80,640]{2,1,0:T(8,128)(2,1)S(1)} collective-permute-done((bf16[4,80,640]{2,1,0:T(8,128)(2,1)S(1)}, bf16[4,80,640]{2,1,0:T(8,128)(2,1)S(1)}, u32[]{:S(2)}, u32[]{:S(2)}) %collective-permute-start.10) | collective-permute-done | bytes 409632 | tf_op jit(solution)/shard_map/ppermute | solution.py:488
  64.4 2.5 %collective-permute-start.6 = (bf16[80,640]{1,0:T(8,128)(2,1)S(1)}, bf16[80,640]{1,0:T(8,128)(2,1)S(1)}, u32[]{:S(2)}, u32[]{:S(2)}) collective-permute-start(bf16[80,640]{1,0:T(8,128)(2,1)S(1)} %get-tuple-element.49), channel_id=1, source_target_pairs={{0,16},{4,20},{8,24},{12,28},{16,0},{20,4},{24,8},{28,12},{1,17},{... | collective-permute-start | bytes 307208 | tf_op jit(solution)/shard_map/ppermute | solution.py:578
  68.5 1.5 collective-permute-start.14
  70.6 1.0 collective-permute-start.15
  71.6 15.9 %collective-permute-done.7 = bf16[80,640]{1,0:T(8,128)(2,1)S(1)} collective-permute-done((bf16[80,640]{1,0:T(8,128)(2,1)S(1)}, bf16[80,640]{1,0:T(8,128)(2,1)S(1)}, u32[]{:S(2)}, u32[]{:S(2)}) %collective-permute-start.7) | collective-permute-done | bytes 102432 | tf_op jit(solution)/shard_map/ppermute | solution.py:578
  87.5 8.9 %collective-permute-done.6 = bf16[80,640]{1,0:T(8,128)(2,1)S(1)} collective-permute-done((bf16[80,640]{1,0:T(8,128)(2,1)S(1)}, bf16[80,640]{1,0:T(8,128)(2,1)S(1)}, u32[]{:S(2)}, u32[]{:S(2)}) %collective-permute-start.6) | collective-permute-done | bytes 102432 | tf_op jit(solution)/shard_map/ppermute | solution.py:578
  96.5 1.3 collective-permute-start.11
  97.8 2.3 collective-permute-start.16
  100.0 1.3 slice.40.refs_4_
  101.4 1.3 collective-permute-start.20
  102.7 1.9 copy-done.2
  104.6 9.4 %attend.2.refs_15_ = bf16[2,2,80,640]{3,2,1,0:T(8,128)(2,1)S(1)} custom-call(s32[2]{0:T(128)S(1)} %copy-done.8, bf16[4,80,640]{2,1,0:T(8,128)(2,1)S(1)} %pad_maximum_fusion.1.refs_0_, bf16[4,80,640]{2,1,0:T(8,128)(2,1)S(1)} %collective-permute-done.10.refs_2_.refs_1_, bf16[4,80,640]{2,1,0:T(8,128)(2,1)S(1)} %collective-permute-done.12.refs_4_.refs_2_, ...), custom_call_target="tpu_custom_call" | custom-call | flops 8000000000 | bytes 6553600 | tf_op jit(solution)/shard_map/attend/pallas_call | solution.py:272
  114.1 13.3 %collective-permute-done.20.refs_5_ = bf16[640,320]{1,0:T(8,128)(2,1)S(1)} collective-permute-done((bf16[640,320]{1,0:T(8,128)(2,1)S(1)}, bf16[640,320]{1,0:T(8,128)(2,1)S(1)}, u32[]{:S(2)}, u32[]{:S(2)}) %collective-permute-start.20) | collective-permute-done | bytes 409632 | tf_op jit(solution)/shard_map/ppermute | solution.py:488
  127.6 1.8 collective-permute-start.25
  129.9 9.8 %attend.3 = (bf16[80,640]{1,0:T(8,128)(2,1)S(1)}, bf16[80,640]{1,0:T(8,128)(2,1)S(1)}, bf16[80,640]{1,0:T(8,128)(2,1)S(1)}, bf16[80,640]{1,0:T(8,128)(2,1)S(1)},...) custom-call(s32[2]{0:T(128)S(1)} %copy-done.8, ...), custom_call_target="tpu_custom_call" | custom-call | flops 8000000000 | bytes 6553600 | tf_op jit(solution)/shard_map/attend/pallas_call | solution.py:272
  140.0 4.6 %collective-permute-done.28.refs_1_ = bf16[80,640]{1,0:T(8,128)(2,1)S(1)} collective-permute-done((bf16[80,640]{1,0:T(8,128)(2,1)S(1)}, bf16[80,640]{1,0:T(8,128)(2,1)S(1)}, u32[]{:S(2)}, u32[]{:S(2)}) %collective-permute-start.28) | collective-permute-done | bytes 102432 | tf_op jit(solution)/shard_map/ppermute | solution.py:488
  145.7 3.6 %collective-permute-done.29.refs_2_ = bf16[80,640]{1,0:T(8,128)(2,1)S(1)} collective-permute-done((bf16[80,640]{1,0:T(8,128)(2,1)S(1)}, bf16[80,640]{1,0:T(8,128)(2,1)S(1)}, u32[]{:S(2)}, u32[]{:S(2)}) %collective-permute-start.29) | collective-permute-done | bytes 102432 | tf_op jit(solution)/shard_map/ppermute | solution.py:488
  149.3 1.7 collective-permute-start.30
  151.0 2.2 own.1
  153.2 2.2 collective-permute-done.30.refs_3_
  155.4 2.5 %collective-permute-start.18 = (bf16[80,640]{1,0:T(8,128)(2,1)S(1)}, bf16[80,640]{1,0:T(8,128)(2,1)S(1)}, u32[]{:S(2)}, u32[]{:S(2)}) collective-permute-start(bf16[80,640]{1,0:T(8,128)(2,1)S(1)} %get-tuple-element.56), channel_id=1, source_target_pairs={{0,2},{1,3},{2,0},{3,1},{4,6},{5,7},{6,4},{7,5},{8,10},{9,11},{10,... | collective-permute-start | bytes 307208 | tf_op jit(solution)/shard_map/ppermute | solution.py:488
  157.9 1.0 collective-permute-start.19
  158.9 2.5 %project.2 = (f32[160,1280]{1,0:T(8,128)S(1)}, bf16[160,1280]{1,0:T(8,128)(2,1)S(1)}) custom-call(s32[2]{0:T(128)S(1)} %copy-done.8, f32[160,1280]{1,0:T(8,128)S(1)} %get-tuple-element.58.base_ref.refs_15_, bf16[80,640]{1,0:T(8,128)(2,1)S(1)} %get-tuple-element.59.refs_0_, bf16[80,640]{1,0:T(8,128)(2,1)S(1)} %collective-permute-done.28.refs_1_, ...), custom_call_target="tpu_custom_call" | custom-call | flops 2000000000 | bytes 3276800 | tf_op jit(solution)/shard_map/project/pallas_call | solution.py:381
  162.0 2.5 %collective-permute-done.19.refs_3_ = bf16[80,640]{1,0:T(8,128)(2,1)S(1)} collective-permute-done((bf16[80,640]{1,0:T(8,128)(2,1)S(1)}, bf16[80,640]{1,0:T(8,128)(2,1)S(1)}, u32[]{:S(2)}, u32[]{:S(2)}) %collective-permute-start.19) | collective-permute-done | bytes 102432 | tf_op jit(solution)/shard_map/ppermute | solution.py:488
  164.5 2.5 %project.3 = (f32[160,1280]{1,0:T(8,128)S(1)}, bf16[160,1280]{1,0:T(8,128)(2,1)S(1)}) custom-call(s32[2]{0:T(128)S(1)} %copy-done.8, f32[160,1280]{1,0:T(8,128)S(1)} %get-tuple-element.53.base_ref, bf16[80,640]{1,0:T(8,128)(2,1)S(1)} %get-tuple-element.54.refs_0_, bf16[80,640]{1,0:T(8,128)(2,1)S(1)} %collective-permute-done.17.refs_1_, ...), custom_call_target="tpu_custom_call" | custom-call | flops 2000000000 | bytes 3276800 | tf_op jit(solution)/shard_map/project/pallas_call | solution.py:381
  167.0 1.0 copy-done.11
  168.1 1.5 collective-permute-start.31
  169.6 0.8 collective-permute-start.32
  170.4 3.5 %collective-permute-done.33.refs_0_ = bf16[160,1280]{1,0:T(8,128)(2,1)S(1)} collective-permute-done((bf16[160,1280]{1,0:T(8,128)(2,1)S(1)}, bf16[160,1280]{1,0:T(8,128)(2,1)S(1)}, u32[]{:S(2)}, u32[]{:S(2)}) %collective-permute-start.33) | collective-permute-done | bytes 409632 | tf_op jit(solution)/shard_map/ppermute | solution.py:488
  174.3 6.1 %collective-permute-done.34.refs_1_ = bf16[160,1280]{1,0:T(8,128)(2,1)S(1)} collective-permute-done((bf16[160,1280]{1,0:T(8,128)(2,1)S(1)}, bf16[160,1280]{1,0:T(8,128)(2,1)S(1)}, u32[]{:S(2)}, u32[]{:S(2)}) %collective-permute-start.34) | collective-permute-done | bytes 409632 | tf_op jit(solution)/shard_map/ppermute | solution.py:488
  180.7 2.9 %copy-done = bf16[1280,2560]{1,0:T(8,128)(2,1)S(1)} copy-done((bf16[1280,2560]{1,0:T(8,128)(2,1)S(1)}, bf16[1280,2560]{1,0:T(8,128)(2,1)}, u32[]{:S(2)}) %copy-start) | copy-done | bytes 6553624
  183.5 2.4 %shard_map.145 = (bf16[160,1280]{1,0:T(8,128)(2,1)S(1)}, bf16[160,1280]{1,0:T(8,128)(2,1)S(1)}) custom-call(bf16[160,1280]{1,0:T(8,128)(2,1)S(1)} %get-tuple-element.63.refs_15_.refs_0_.refs_4_, bf16[160,1280]{1,0:T(8,128)(2,1)S(1)} %get-tuple-element.64.refs_1_, bf16[1280,2560]{1,0:T(8,128)(2,1)S(1)} %copy-done, f32[1,1280]{1,0:T(1,128)S(1)} %copy-done.3, ...), custom_call_target="tpu_custom_call" | custom-call | flops 2097152000 | bytes 6553600 | tf_op jit(solution)/shard_map/pallas_call | solution.py:418
  186.8 3.2 %shard_map.146 = (bf16[160,1280]{1,0:T(8,128)(2,1)S(1)}, bf16[160,1280]{1,0:T(8,128)(2,1)}) custom-call(bf16[160,1280]{1,0:T(8,128)(2,1)S(1)} %collective-permute-done.33.refs_0_, bf16[160,1280]{1,0:T(8,128)(2,1)S(1)} %collective-permute-done.34.refs_1_, bf16[1280,2560]{1,0:T(8,128)(2,1)S(1)} %copy-done.1, f32[1,1280]{1,0:T(1,128)S(1)} %copy-done.3, ...), custom_call_target="tpu_custom_call" | custom-call | flops 2097152000 | bytes 6553600 | tf_op jit(solution)/shard_map/pallas_call | solution.py:418
  190.0 3.6 %shard_map.147 = (bf16[160,1280]{1,0:T(8,128)(2,1)S(1)}, bf16[160,1280]{1,0:T(8,128)(2,1)S(1)}) custom-call(bf16[160,1280]{1,0:T(8,128)(2,1)} %collective-permute-done.31.refs_0_, bf16[160,1280]{1,0:T(8,128)(2,1)} %collective-permute-done.32.refs_1_, bf16[1280,2560]{1,0:T(8,128)(2,1)S(1)} %copy-done.1, f32[1,1280]{1,0:T(1,128)S(1)} %copy-done.3, ...), custom_call_target="tpu_custom_call" | custom-call | flops 2097152000 | bytes 6553600 | tf_op jit(solution)/shard_map/pallas_call | solution.py:418
  193.6 3.4 %shard_map.148 = (bf16[160,1280]{1,0:T(8,128)(2,1)S(1)}, bf16[160,1280]{1,0:T(8,128)(2,1)S(1)}) custom-call(bf16[160,1280]{1,0:T(8,128)(2,1)S(1)} %collective-permute-done.35.refs_0_, bf16[160,1280]{1,0:T(8,128)(2,1)} %collective-permute-done.36.refs_1_, bf16[1280,2560]{1,0:T(8,128)(2,1)S(1)} %copy-done.1, f32[1,1280]{1,0:T(1,128)S(1)} %copy-done.3, ...), custom_call_target="tpu_custom_call" | custom-call | flops 2097152000 | bytes 6553600 | tf_op jit(solution)/shard_map/pallas_call | solution.py:418
  197.0 1.8 collective-permute-start.37
  199.1 1.3 collective-permute-start.39
  201.2 7.3 %collective-permute-done.37 = bf16[160,1280]{1,0:T(8,128)(2,1)S(1)} collective-permute-done((bf16[160,1280]{1,0:T(8,128)(2,1)S(1)}, bf16[160,1280]{1,0:T(8,128)(2,1)S(1)}, u32[]{:S(2)}, u32[]{:S(2)}) %collective-permute-start.37) | collective-permute-done | bytes 409632 | tf_op jit(solution)/shard_map/ppermute | solution.py:488
  208.4 0.9 add_convert_fusion.1
  209.3 0.9 collective-permute-start.38
  210.2 0.8 add_convert_fusion
  211.0 0.8 collective-permute-start.40
  211.8 1.0 collective-permute-done.41.refs_2_
  213.0 1.1 copy-done.10
  214.2 1.1 copy-done.12
  215.6 1.9 collective-permute-done.38.refs_0_
  217.4 1.7 collective-permute-done.40.refs_1_
  219.2 1.6 finish.1
  (118 shorter events, 11.1 us)
Async XLA Ops:
  6.5 93.5 %all-gather.3.cloned.1.call-start = ((), (), s32[]{:S(2)}) async-start(), calls=%async_computation | async-start | bytes 3686400 | tf_op jit(solution)/shard_map/all_gather | solution.py:552
  8.5 172.2 %all-gather.5.cloned.1.call-start = ((), (), s32[]{:S(2)}) async-start(), calls=%async_computation.1 | async-start | bytes 7372800 | tf_op jit(solution)/shard_map/all_gather | solution.py:583
  11.2 10.4 %copy-start.18 = (s32[256]{0:T(256)S(1)}, s32[256]{0:T(256)}, u32[]{:S(2)}) copy-start(s32[256]{0:T(256)} %param.18) | copy-start | bytes 3076
  11.2 10.7 %copy-start.16 = (s32[256]{0:T(256)S(1)}, s32[256]{0:T(256)}, u32[]{:S(2)}) copy-start(s32[256]{0:T(256)} %param.19) | copy-start | bytes 3076
  11.2 11.2 %copy-start.14 = (f32[1,2,1280]{2,1,0:T(2,128)S(1)}, f32[1,2,1280]{2,1,0:T(2,128)}, u32[]{:S(2)}) copy-start(f32[1,2,1280]{2,1,0:T(2,128)} %param.21) | copy-start | bytes 30724
  11.2 11.2 %copy-start.15 = (f32[1,2,1280]{2,1,0:T(2,128)S(1)}, f32[1,2,1280]{2,1,0:T(2,128)}, u32[]{:S(2)}) copy-start(f32[1,2,1280]{2,1,0:T(2,128)} %param.20) | copy-start | bytes 30724
  11.2 25.3 %copy-start.8 = (s32[2]{0:T(128)S(1)}, s32[2]{0:T(128)}, u32[]{:S(2)}) copy-start(s32[2]{0:T(128)} %pad_add_fusion.place_ref) | copy-start | bytes 28
  17.1 11.8 %collective-permute-start = (bf16[320,512]{1,0:T(8,128)(2,1)}, bf16[320,512]{1,0:T(8,128)(2,1)S(1)}, u32[]{:S(2)}, u32[]{:S(2)}) collective-permute-start(bf16[320,512]{1,0:T(8,128)(2,1)} %get-tuple-element.42), channel_id=1, source_target_pairs={{0,1},{1,0},{2,3},{3,2},{4,5},{5,4},{6,7},{7,6},{8,9},{9,8},{10,11... | collective-permute-start | bytes 983048 | tf_op jit(solution)/shard_map/ppermute | solution.py:488
  20.1 16.4 %collective-permute-start.1 = (bf16[320,512]{1,0:T(8,128)(2,1)}, bf16[320,512]{1,0:T(8,128)(2,1)S(1)}, u32[]{:S(2)}, u32[]{:S(2)}) collective-permute-start(bf16[320,512]{1,0:T(8,128)(2,1)} %get-tuple-element.43), channel_id=1, source_target_pairs={{0,2},{1,3},{2,0},{3,1},{4,6},{5,7},{6,4},{7,5},{8,10},{9,11},{10,... | collective-permute-start | bytes 983048 | tf_op jit(solution)/shard_map/ppermute | solution.py:488
  21.7 14.9 %collective-permute-start.2 = (bf16[320,512]{1,0:T(8,128)(2,1)}, bf16[320,512]{1,0:T(8,128)(2,1)S(1)}, u32[]{:S(2)}, u32[]{:S(2)}) collective-permute-start(bf16[320,512]{1,0:T(8,128)(2,1)} %get-tuple-element.44), channel_id=1, source_target_pairs={{0,3},{1,2},{2,1},{3,0},{4,7},{5,6},{6,5},{7,4},{8,11},{9,10},{10,... | collective-permute-start | bytes 983048 | tf_op jit(solution)/shard_map/ppermute | solution.py:488
  36.5 1.0 copy-start.13
  37.5 30.0 %copy-start.17 = (f32[1,3,320]{2,0,1:T(1,128)S(1)}, f32[1,3,320]{2,0,1:T(1,128)}, u32[]{:S(2)}) copy-start(f32[1,3,320]{2,0,1:T(1,128)} %param.23) | copy-start | bytes 11524
  41.0 9.6 %collective-permute-start.5 = (bf16[80,640]{1,0:T(8,128)(2,1)S(1)}, bf16[80,640]{1,0:T(8,128)(2,1)S(1)}, u32[]{:S(2)}, u32[]{:S(2)}) collective-permute-start(bf16[80,640]{1,0:T(8,128)(2,1)S(1)} %get-tuple-element.48), channel_id=1, source_target_pairs={{0,12},{4,8},{8,4},{12,0},{16,28},{20,24},{24,20},{28,16},{1,13},{... | collective-permute-start | bytes 307208 | tf_op jit(solution)/shard_map/ppermute | solution.py:578
  41.1 11.7 %collective-permute-start.4 = (bf16[80,640]{1,0:T(8,128)(2,1)S(1)}, bf16[80,640]{1,0:T(8,128)(2,1)S(1)}, u32[]{:S(2)}, u32[]{:S(2)}) collective-permute-start(bf16[80,640]{1,0:T(8,128)(2,1)S(1)} %get-tuple-element.47), channel_id=1, source_target_pairs={{0,8},{4,12},{8,0},{12,4},{16,24},{20,28},{24,16},{28,20},{1,9},{5... | collective-permute-start | bytes 307208 | tf_op jit(solution)/shard_map/ppermute | solution.py:578
  42.7 10.0 %collective-permute-start.3 = (bf16[80,640]{1,0:T(8,128)(2,1)S(1)}, bf16[80,640]{1,0:T(8,128)(2,1)S(1)}, u32[]{:S(2)}, u32[]{:S(2)}) collective-permute-start(bf16[80,640]{1,0:T(8,128)(2,1)S(1)} %get-tuple-element.46), channel_id=1, source_target_pairs={{0,4},{4,0},{8,12},{12,8},{16,20},{20,16},{24,28},{28,24},{1,5},{5... | collective-permute-start | bytes 307208 | tf_op jit(solution)/shard_map/ppermute | solution.py:578
  52.8 11.6 %collective-permute-start.10 = (bf16[4,80,640]{2,1,0:T(8,128)(2,1)S(1)}, bf16[4,80,640]{2,1,0:T(8,128)(2,1)S(1)}, u32[]{:S(2)}, u32[]{:S(2)}) collective-permute-start(bf16[4,80,640]{2,1,0:T(8,128)(2,1)S(1)} %pad_maximum_fusion.1.refs_0_), channel_id=1, source_target_pairs={{0,1},{1,0},{2,3},{3,2},{4,5},{5,4},{6,7},{7,6},{8,9},{9,8},{10,11... | collective-permute-start | bytes 1228808 | tf_op jit(solution)/shard_map/ppermute | solution.py:488
  54.4 14.0 %collective-permute-start.12 = (bf16[4,80,640]{2,1,0:T(8,128)(2,1)S(1)}, bf16[4,80,640]{2,1,0:T(8,128)(2,1)S(1)}, u32[]{:S(2)}, u32[]{:S(2)}) collective-permute-start(bf16[4,80,640]{2,1,0:T(8,128)(2,1)S(1)} %pad_maximum_fusion.1.refs_0_), channel_id=1, source_target_pairs={{0,2},{1,3},{2,0},{3,1},{4,6},{5,7},{6,4},{7,5},{8,10},{9,11},{10,... | collective-permute-start | bytes 1228808 | tf_op jit(solution)/shard_map/ppermute | solution.py:488
  56.4 14.2 %collective-permute-start.9 = (bf16[80,640]{1,0:T(8,128)(2,1)S(1)}, bf16[80,640]{1,0:T(8,128)(2,1)S(1)}, u32[]{:S(2)}, u32[]{:S(2)}) collective-permute-start(bf16[80,640]{1,0:T(8,128)(2,1)S(1)} %get-tuple-element.52), channel_id=1, source_target_pairs={{0,28},{4,24},{8,20},{12,16},{16,12},{20,8},{24,4},{28,0},{1,29},{... | collective-permute-start | bytes 307208 | tf_op jit(solution)/shard_map/ppermute | solution.py:578
  58.0 13.6 %collective-permute-start.8 = (bf16[80,640]{1,0:T(8,128)(2,1)S(1)}, bf16[80,640]{1,0:T(8,128)(2,1)S(1)}, u32[]{:S(2)}, u32[]{:S(2)}) collective-permute-start(bf16[80,640]{1,0:T(8,128)(2,1)S(1)} %get-tuple-element.51), channel_id=1, source_target_pairs={{0,24},{4,28},{8,16},{12,20},{16,8},{20,12},{24,0},{28,4},{1,25},{... | collective-permute-start | bytes 307208 | tf_op jit(solution)/shard_map/ppermute | solution.py:578
  59.5 28.0 %collective-permute-start.7 = (bf16[80,640]{1,0:T(8,128)(2,1)S(1)}, bf16[80,640]{1,0:T(8,128)(2,1)S(1)}, u32[]{:S(2)}, u32[]{:S(2)}) collective-permute-start(bf16[80,640]{1,0:T(8,128)(2,1)S(1)} %get-tuple-element.50), channel_id=1, source_target_pairs={{0,20},{4,16},{8,28},{12,24},{16,4},{20,0},{24,12},{28,8},{1,21},{... | collective-permute-start | bytes 307208 | tf_op jit(solution)/shard_map/ppermute | solution.py:578
  64.4 32.1 %collective-permute-start.6 = (bf16[80,640]{1,0:T(8,128)(2,1)S(1)}, bf16[80,640]{1,0:T(8,128)(2,1)S(1)}, u32[]{:S(2)}, u32[]{:S(2)}) collective-permute-start(bf16[80,640]{1,0:T(8,128)(2,1)S(1)} %get-tuple-element.49), channel_id=1, source_target_pairs={{0,16},{4,20},{8,24},{12,28},{16,0},{20,4},{24,8},{28,12},{1,17},{... | collective-permute-start | bytes 307208 | tf_op jit(solution)/shard_map/ppermute | solution.py:578
  68.5 33.0 %collective-permute-start.14 = (bf16[2,80,640]{2,1,0:T(8,128)(2,1)}, bf16[2,80,640]{2,1,0:T(8,128)(2,1)S(1)}, u32[]{:S(2)}, u32[]{:S(2)}) collective-permute-start(bf16[2,80,640]{2,1,0:T(8,128)(2,1)} %slice.38), channel_id=1, source_target_pairs={{0,2},{1,3},{2,0},{3,1},{4,6},{5,7},{6,4},{7,5},{8,10},{9,11},{10,... | collective-permute-start | bytes 614408 | tf_op jit(solution)/shard_map/ppermute | solution.py:488
  70.6 32.1 %collective-permute-start.15 = (bf16[2,80,640]{2,1,0:T(8,128)(2,1)}, bf16[2,80,640]{2,1,0:T(8,128)(2,1)}, u32[]{:S(2)}, u32[]{:S(2)}) collective-permute-start(bf16[2,80,640]{2,1,0:T(8,128)(2,1)} %slice.39), channel_id=1, source_target_pairs={{0,1},{1,0},{2,3},{3,2},{4,5},{5,4},{6,7},{7,6},{8,9},{9,8},{10,11... | collective-permute-start | bytes 614408 | tf_op jit(solution)/shard_map/ppermute | solution.py:488
  96.5 32.9 %collective-permute-start.11 = (bf16[4,80,640]{2,1,0:T(8,128)(2,1)S(1)}, bf16[4,80,640]{2,1,0:T(8,128)(2,1)S(1)}, u32[]{:S(2)}, u32[]{:S(2)}) collective-permute-start(bf16[4,80,640]{2,1,0:T(8,128)(2,1)S(1)} %pad_maximum_fusion.2.refs_1_), channel_id=1, source_target_pairs={{0,1},{1,0},{2,3},{3,2},{4,5},{5,4},{6,7},{7,6},{8,9},{9,8},{10,11... | collective-permute-start | bytes 1228808 | tf_op jit(solution)/shard_map/ppermute | solution.py:488
  97.8 31.6 %collective-permute-start.13 = (bf16[4,80,640]{2,1,0:T(8,128)(2,1)S(1)}, bf16[4,80,640]{2,1,0:T(8,128)(2,1)S(1)}, u32[]{:S(2)}, u32[]{:S(2)}) collective-permute-start(bf16[4,80,640]{2,1,0:T(8,128)(2,1)S(1)} %pad_maximum_fusion.2.refs_1_), channel_id=1, source_target_pairs={{0,2},{1,3},{2,0},{3,1},{4,6},{5,7},{6,4},{7,5},{8,10},{9,11},{10,... | collective-permute-start | bytes 1228808 | tf_op jit(solution)/shard_map/ppermute | solution.py:488
  97.8 32.1 %collective-permute-start.16 = (bf16[4,80,640]{2,1,0:T(8,128)(2,1)S(1)}, bf16[4,80,640]{2,1,0:T(8,128)(2,1)}, u32[]{:S(2)}, u32[]{:S(2)}) collective-permute-start(bf16[4,80,640]{2,1,0:T(8,128)(2,1)S(1)} %pad_maximum_fusion.2.refs_1_), channel_id=1, source_target_pairs={{0,3},{1,2},{2,1},{3,0},{4,7},{5,6},{6,5},{7,4},{8,11},{9,10},{10,... | collective-permute-start | bytes 1228808 | tf_op jit(solution)/shard_map/ppermute | solution.py:488
  101.4 26.0 %collective-permute-start.20 = (bf16[640,320]{1,0:T(8,128)(2,1)S(1)}, bf16[640,320]{1,0:T(8,128)(2,1)S(1)}, u32[]{:S(2)}, u32[]{:S(2)}) collective-permute-start(bf16[640,320]{1,0:T(8,128)(2,1)S(1)} %constant_dynamic-slice_fusion.1), channel_id=1, source_target_pairs={{0,1},{1,0},{2,3},{3,2},{4,5},{5,4},{6,7},{7,6},{8,9},{9,8},{10,11... | collective-permute-start | bytes 1228808 | tf_op jit(solution)/shard_map/ppermute | solution.py:488
  102.7 24.8 %collective-permute-start.22 = (bf16[640,320]{1,0:T(8,128)(2,1)S(1)}, bf16[640,320]{1,0:T(8,128)(2,1)S(1)}, u32[]{:S(2)}, u32[]{:S(2)}) collective-permute-start(bf16[640,320]{1,0:T(8,128)(2,1)S(1)} %constant_dynamic-slice_fusion.1), channel_id=1, source_target_pairs={{0,2},{1,3},{2,0},{3,1},{4,6},{5,7},{6,4},{7,5},{8,10},{9,11},{10,... | collective-permute-start | bytes 1228808 | tf_op jit(solution)/shard_map/ppermute | solution.py:488
  102.7 1.9 copy-start.2
  127.4 17.7 %collective-permute-start.24 = (bf16[320,320]{1,0:T(8,128)(2,1)S(1)}, bf16[320,320]{1,0:T(8,128)(2,1)S(1)}, u32[]{:S(2)}, u32[]{:S(2)}) collective-permute-start(bf16[320,320]{1,0:T(8,128)(2,1)S(1)} %slice.41), channel_id=1, source_target_pairs={{0,2},{1,3},{2,0},{3,1},{4,6},{5,7},{6,4},{7,5},{8,10},{9,11},{10,... | collective-permute-start | bytes 614408 | tf_op jit(solution)/shard_map/ppermute | solution.py:488
  127.6 23.4 %copy-start.6 = (f32[1,1280]{1,0:T(1,128)S(1)}, f32[1,1280]{1,0:T(1,128)}, u32[]{:S(2)}) copy-start(f32[1,1280]{1,0:T(1,128)} %refs_9_.1) | copy-start | bytes 15364
  127.6 17.6 %collective-permute-start.25 = (bf16[320,320]{1,0:T(8,128)(2,1)S(1)}, bf16[320,320]{1,0:T(8,128)(2,1)S(1)}, u32[]{:S(2)}, u32[]{:S(2)}) collective-permute-start(bf16[320,320]{1,0:T(8,128)(2,1)S(1)} %slice.42), channel_id=1, source_target_pairs={{0,1},{1,0},{2,3},{3,2},{4,5},{5,4},{6,7},{7,6},{8,9},{9,8},{10,11... | collective-permute-start | bytes 614408 | tf_op jit(solution)/shard_map/ppermute | solution.py:488
  129.4 26.0 %collective-permute-start.21 = (bf16[640,320]{1,0:T(8,128)(2,1)S(1)}, bf16[640,320]{1,0:T(8,128)(2,1)S(1)}, u32[]{:S(2)}, u32[]{:S(2)}) collective-permute-start(bf16[640,320]{1,0:T(8,128)(2,1)S(1)} %collective-permute-done.20.refs_5_), channel_id=1, source_target_pairs={{0,4},{4,0},{8,12},{12,8},{16,20},{20,16},{24,28},{28,24},{1,5},{5... | collective-permute-start | bytes 1228808 | tf_op jit(solution)/shard_map/ppermute | solution.py:561
  129.4 28.5 %collective-permute-start.23 = (bf16[640,320]{1,0:T(8,128)(2,1)S(1)}, bf16[640,320]{1,0:T(8,128)(2,1)S(1)}, u32[]{:S(2)}, u32[]{:S(2)}) collective-permute-start(bf16[640,320]{1,0:T(8,128)(2,1)S(1)} %collective-permute-done.22.refs_7_), channel_id=1, source_target_pairs={{0,4},{4,0},{8,12},{12,8},{16,20},{20,16},{24,28},{28,24},{1,5},{5... | collective-permute-start | bytes 1228808 | tf_op jit(solution)/shard_map/ppermute | solution.py:561
  139.7 4.9 %collective-permute-start.28 = (bf16[80,640]{1,0:T(8,128)(2,1)S(1)}, bf16[80,640]{1,0:T(8,128)(2,1)S(1)}, u32[]{:S(2)}, u32[]{:S(2)}) collective-permute-start(bf16[80,640]{1,0:T(8,128)(2,1)S(1)} %get-tuple-element.60), channel_id=1, source_target_pairs={{0,1},{1,0},{2,3},{3,2},{4,5},{5,4},{6,7},{7,6},{8,9},{9,8},{10,11... | collective-permute-start | bytes 307208 | tf_op jit(solution)/shard_map/ppermute | solution.py:488
  144.6 4.7 %collective-permute-start.29 = (bf16[80,640]{1,0:T(8,128)(2,1)S(1)}, bf16[80,640]{1,0:T(8,128)(2,1)S(1)}, u32[]{:S(2)}, u32[]{:S(2)}) collective-permute-start(bf16[80,640]{1,0:T(8,128)(2,1)S(1)} %get-tuple-element.61), channel_id=1, source_target_pairs={{0,2},{1,3},{2,0},{3,1},{4,6},{5,7},{6,4},{7,5},{8,10},{9,11},{10,... | collective-permute-start | bytes 307208 | tf_op jit(solution)/shard_map/ppermute | solution.py:488
  145.1 13.8 %collective-permute-start.26 = (bf16[320,320]{1,0:T(8,128)(2,1)S(1)}, bf16[320,320]{1,0:T(8,128)(2,1)S(1)}, u32[]{:S(2)}, u32[]{:S(2)}) collective-permute-start(bf16[320,320]{1,0:T(8,128)(2,1)S(1)} %collective-permute-done.24.refs_9_), channel_id=1, source_target_pairs={{0,4},{4,0},{8,12},{12,8},{16,20},{20,16},{24,28},{28,24},{1,5},{5... | collective-permute-start | bytes 614408 | tf_op jit(solution)/shard_map/ppermute | solution.py:561
  145.2 13.7 %collective-permute-start.27 = (bf16[320,320]{1,0:T(8,128)(2,1)S(1)}, bf16[320,320]{1,0:T(8,128)(2,1)S(1)}, u32[]{:S(2)}, u32[]{:S(2)}) collective-permute-start(bf16[320,320]{1,0:T(8,128)(2,1)S(1)} %collective-permute-done.25.refs_10_), channel_id=1, source_target_pairs={{0,4},{4,0},{8,12},{12,8},{16,20},{20,16},{24,28},{28,24},{1,5},{5... | collective-permute-start | bytes 614408 | tf_op jit(solution)/shard_map/ppermute | solution.py:561
  149.3 6.1 %collective-permute-start.30 = (bf16[80,640]{1,0:T(8,128)(2,1)S(1)}, bf16[80,640]{1,0:T(8,128)(2,1)S(1)}, u32[]{:S(2)}, u32[]{:S(2)}) collective-permute-start(bf16[80,640]{1,0:T(8,128)(2,1)S(1)} %get-tuple-element.62), channel_id=1, source_target_pairs={{0,3},{1,2},{2,1},{3,0},{4,7},{5,6},{6,5},{7,4},{8,11},{9,10},{10,... | collective-permute-start | bytes 307208 | tf_op jit(solution)/shard_map/ppermute | solution.py:488
  155.4 6.6 %collective-permute-start.17 = (bf16[80,640]{1,0:T(8,128)(2,1)S(1)}, bf16[80,640]{1,0:T(8,128)(2,1)S(1)}, u32[]{:S(2)}, u32[]{:S(2)}) collective-permute-start(bf16[80,640]{1,0:T(8,128)(2,1)S(1)} %get-tuple-element.55), channel_id=1, source_target_pairs={{0,1},{1,0},{2,3},{3,2},{4,5},{5,4},{6,7},{7,6},{8,9},{9,8},{10,11... | collective-permute-start | bytes 307208 | tf_op jit(solution)/shard_map/ppermute | solution.py:488
  155.4 6.6 %collective-permute-start.18 = (bf16[80,640]{1,0:T(8,128)(2,1)S(1)}, bf16[80,640]{1,0:T(8,128)(2,1)S(1)}, u32[]{:S(2)}, u32[]{:S(2)}) collective-permute-start(bf16[80,640]{1,0:T(8,128)(2,1)S(1)} %get-tuple-element.56), channel_id=1, source_target_pairs={{0,2},{1,3},{2,0},{3,1},{4,6},{5,7},{6,4},{7,5},{8,10},{9,11},{10,... | collective-permute-start | bytes 307208 | tf_op jit(solution)/shard_map/ppermute | solution.py:488
  157.9 6.7 %collective-permute-start.19 = (bf16[80,640]{1,0:T(8,128)(2,1)S(1)}, bf16[80,640]{1,0:T(8,128)(2,1)S(1)}, u32[]{:S(2)}, u32[]{:S(2)}) collective-permute-start(bf16[80,640]{1,0:T(8,128)(2,1)S(1)} %get-tuple-element.57), channel_id=1, source_target_pairs={{0,3},{1,2},{2,1},{3,0},{4,7},{5,6},{6,5},{7,4},{8,11},{9,10},{10,... | collective-permute-start | bytes 307208 | tf_op jit(solution)/shard_map/ppermute | solution.py:488
  161.4 5.6 %copy-start.9 = (f32[160,1280]{1,0:T(8,128)}, f32[160,1280]{1,0:T(8,128)S(1)}, u32[]{:S(2)}) copy-start(f32[160,1280]{1,0:T(8,128)S(1)} %get-tuple-element.73.refs_4_) | copy-start | bytes 2457604
  161.4 12.4 %collective-permute-start.33 = (bf16[160,1280]{1,0:T(8,128)(2,1)S(1)}, bf16[160,1280]{1,0:T(8,128)(2,1)S(1)}, u32[]{:S(2)}, u32[]{:S(2)}) collective-permute-start(bf16[160,1280]{1,0:T(8,128)(2,1)S(1)} %get-tuple-element.63.refs_15_.refs_0_.refs_4_), channel_id=1, source_target_pairs={{0,1},{1,0},{2,3},{3,2},{4,5},{5,4},{6,7},{7,6},{8,9},{9,8},{10,11... | collective-permute-start | bytes 1228808 | tf_op jit(solution)/shard_map/ppermute | solution.py:488
  164.5 16.1 %copy-start.3 = (f32[1,1280]{1,0:T(1,128)S(1)}, f32[1,1280]{1,0:T(1,128)}, u32[]{:S(2)}) copy-start(f32[1,1280]{1,0:T(1,128)} %refs_3_.7) | copy-start | bytes 15364
  167.0 1.0 copy-start.11
  168.0 12.3 %collective-permute-start.34 = (bf16[160,1280]{1,0:T(8,128)(2,1)S(1)}, bf16[160,1280]{1,0:T(8,128)(2,1)S(1)}, u32[]{:S(2)}, u32[]{:S(2)}) collective-permute-start(bf16[160,1280]{1,0:T(8,128)(2,1)S(1)} %get-tuple-element.64.refs_1_), channel_id=1, source_target_pairs={{0,2},{1,3},{2,0},{3,1},{4,6},{5,7},{6,4},{7,5},{8,10},{9,11},{10,... | collective-permute-start | bytes 1228808 | tf_op jit(solution)/shard_map/ppermute | solution.py:488
  168.1 21.9 %collective-permute-start.31 = (bf16[160,1280]{1,0:T(8,128)(2,1)S(1)}, bf16[160,1280]{1,0:T(8,128)(2,1)}, u32[]{:S(2)}, u32[]{:S(2)}) collective-permute-start(bf16[160,1280]{1,0:T(8,128)(2,1)S(1)} %get-tuple-element.64.refs_1_), channel_id=1, source_target_pairs={{0,1},{1,0},{2,3},{3,2},{4,5},{5,4},{6,7},{7,6},{8,9},{9,8},{10,11... | collective-permute-start | bytes 1228808 | tf_op jit(solution)/shard_map/ppermute | solution.py:488
  169.6 20.4 %collective-permute-start.32 = (bf16[160,1280]{1,0:T(8,128)(2,1)S(1)}, bf16[160,1280]{1,0:T(8,128)(2,1)}, u32[]{:S(2)}, u32[]{:S(2)}) collective-permute-start(bf16[160,1280]{1,0:T(8,128)(2,1)S(1)} %get-tuple-element.63.refs_15_.refs_0_.refs_4_), channel_id=1, source_target_pairs={{0,2},{1,3},{2,0},{3,1},{4,6},{5,7},{6,4},{7,5},{8,10},{9,11},{10,... | collective-permute-start | bytes 1228808 | tf_op jit(solution)/shard_map/ppermute | solution.py:488
  173.8 19.7 %collective-permute-start.35 = (bf16[160,1280]{1,0:T(8,128)(2,1)S(1)}, bf16[160,1280]{1,0:T(8,128)(2,1)S(1)}, u32[]{:S(2)}, u32[]{:S(2)}) collective-permute-start(bf16[160,1280]{1,0:T(8,128)(2,1)S(1)} %collective-permute-done.33.refs_0_), channel_id=1, source_target_pairs={{0,2},{1,3},{2,0},{3,1},{4,6},{5,7},{6,4},{7,5},{8,10},{9,11},{10,... | collective-permute-start | bytes 1228808 | tf_op jit(solution)/shard_map/ppermute | solution.py:488
  180.3 13.2 %collective-permute-start.36 = (bf16[160,1280]{1,0:T(8,128)(2,1)S(1)}, bf16[160,1280]{1,0:T(8,128)(2,1)}, u32[]{:S(2)}, u32[]{:S(2)}) collective-permute-start(bf16[160,1280]{1,0:T(8,128)(2,1)S(1)} %collective-permute-done.34.refs_1_), channel_id=1, source_target_pairs={{0,1},{1,0},{2,3},{3,2},{4,5},{5,4},{6,7},{7,6},{8,9},{9,8},{10,11... | collective-permute-start | bytes 1228808 | tf_op jit(solution)/shard_map/ppermute | solution.py:488
  180.7 2.9 %copy-start = (bf16[1280,2560]{1,0:T(8,128)(2,1)S(1)}, bf16[1280,2560]{1,0:T(8,128)(2,1)}, u32[]{:S(2)}) copy-start(bf16[1280,2560]{1,0:T(8,128)(2,1)} %all-gather.5.cloned.1.call-done.refs_2_) | copy-start | bytes 19660804
  183.5 3.2 %copy-start.1 = (bf16[1280,2560]{1,0:T(8,128)(2,1)S(1)}, bf16[1280,2560]{1,0:T(8,128)(2,1)}, u32[]{:S(2)}) copy-start(bf16[1280,2560]{1,0:T(8,128)(2,1)} %all-gather.5.cloned.1.call-done.refs_2_) | copy-start | bytes 19660804
  186.0 0.8 copy-start.4
  197.0 16.0 %copy-start.5 = (bf16[160,1280]{1,0:T(8,128)(2,1)S(1)}, bf16[160,1280]{1,0:T(8,128)(2,1)}, u32[]{:S(2)}) copy-start(bf16[160,1280]{1,0:T(8,128)(2,1)} %copy-done.4) | copy-start | bytes 1228804
  197.0 16.0 %copy-start.7 = (f32[1,1280]{1,0:T(1,128)S(1)}, f32[1,1280]{1,0:T(1,128)}, u32[]{:S(2)}) copy-start(f32[1,1280]{1,0:T(1,128)} %refs_6_.1) | copy-start | bytes 15364
  197.0 11.4 %collective-permute-start.37 = (bf16[160,1280]{1,0:T(8,128)(2,1)S(1)}, bf16[160,1280]{1,0:T(8,128)(2,1)S(1)}, u32[]{:S(2)}, u32[]{:S(2)}) collective-permute-start(bf16[160,1280]{1,0:T(8,128)(2,1)S(1)} %get-tuple-element.69), channel_id=1, source_target_pairs={{0,1},{1,0},{2,3},{3,2},{4,5},{5,4},{6,7},{7,6},{8,9},{9,8},{10,11... | collective-permute-start | bytes 1228808 | tf_op jit(solution)/shard_map/ppermute | solution.py:488
  198.8 14.0 %collective-permute-start.41 = (bf16[160,1280]{1,0:T(8,128)(2,1)S(1)}, bf16[160,1280]{1,0:T(8,128)(2,1)S(1)}, u32[]{:S(2)}, u32[]{:S(2)}) collective-permute-start(bf16[160,1280]{1,0:T(8,128)(2,1)S(1)} %get-tuple-element.66.refs_4_), channel_id=1, source_target_pairs={{0,1},{1,0},{2,3},{3,2},{4,5},{5,4},{6,7},{7,6},{8,9},{9,8},{10,11... | collective-permute-start | bytes 1228808 | tf_op jit(solution)/shard_map/ppermute | solution.py:488
  199.1 11.0 %collective-permute-start.39 = (bf16[160,1280]{1,0:T(8,128)(2,1)S(1)}, bf16[160,1280]{1,0:T(8,128)(2,1)S(1)}, u32[]{:S(2)}, u32[]{:S(2)}) collective-permute-start(bf16[160,1280]{1,0:T(8,128)(2,1)S(1)} %get-tuple-element.70), channel_id=1, source_target_pairs={{0,2},{1,3},{2,0},{3,1},{4,6},{5,7},{6,4},{7,5},{8,10},{9,11},{10,... | collective-permute-start | bytes 1228808 | tf_op jit(solution)/shard_map/ppermute | solution.py:488
  200.4 12.6 %collective-permute-start.42 = (bf16[160,1280]{1,0:T(8,128)(2,1)}, bf16[160,1280]{1,0:T(8,128)(2,1)S(1)}, u32[]{:S(2)}, u32[]{:S(2)}) collective-permute-start(bf16[160,1280]{1,0:T(8,128)(2,1)} %get-tuple-element.72), channel_id=1, source_target_pairs={{0,2},{1,3},{2,0},{3,1},{4,6},{5,7},{6,4},{7,5},{8,10},{9,11},{10,... | collective-permute-start | bytes 1228808 | tf_op jit(solution)/shard_map/ppermute | solution.py:488
  209.3 8.2 %collective-permute-start.38 = (bf16[160,1280]{1,0:T(8,128)(2,1)}, bf16[160,1280]{1,0:T(8,128)(2,1)S(1)}, u32[]{:S(2)}, u32[]{:S(2)}) collective-permute-start(bf16[160,1280]{1,0:T(8,128)(2,1)} %add_convert_fusion.1), channel_id=1, source_target_pairs={{0,2},{1,3},{2,0},{3,1},{4,6},{5,7},{6,4},{7,5},{8,10},{9,11},{10,... | collective-permute-start | bytes 1228808 | tf_op jit(solution)/shard_map/ppermute | solution.py:488
  211.0 8.2 %collective-permute-start.40 = (bf16[160,1280]{1,0:T(8,128)(2,1)}, bf16[160,1280]{1,0:T(8,128)(2,1)S(1)}, u32[]{:S(2)}, u32[]{:S(2)}) collective-permute-start(bf16[160,1280]{1,0:T(8,128)(2,1)} %add_convert_fusion), channel_id=1, source_target_pairs={{0,1},{1,0},{2,3},{3,2},{4,5},{5,4},{6,7},{7,6},{8,9},{9,8},{10,11... | collective-permute-start | bytes 1228808 | tf_op jit(solution)/shard_map/ppermute | solution.py:488
  213.0 1.1 copy-start.10
  214.2 1.1 copy-start.12
Sparse Core Ops, SparseCore 0:
  9.0 42.8 all-gather.2
  53.5 77.6 all-gather.4

commit v4 on v3

--- a/solution.py
+++ b/solution.py
@@ -290,7 +290,7 @@
             pltpu.VMEM((len(blocks), spm, *shape), BF),
         ],
         out_shape=out_shape,
-        compiler_params=params(24),
+        compiler_params=params(14),
         cost_estimate=cost(len(blocks) * 4e9, operands[0].size * 4),
         name="attend",
     )(place, *flat, *operands, *priors)
@@ -349,18 +349,32 @@
     for k, count in enumerate(out_counts):
         left = jnp.concatenate([att_refs[k][:, :hc], att_refs[k][:, hc:]], axis=0)
         if k == 0:
-            pair = [
-                [own_ref[pl.ds(pl.multiple_of(c * half, 128), half)]] for c in (core, 1 - core)
+            sums = [
+                lax.dot_general(
+                    left,
+                    own_ref[pl.ds(pl.multiple_of(c * half, 128), half)],
+                    NT,
+                    preferred_element_type=F32,
+                )
+                for c in (core, 1 - core)
             ]
         else:
-            pair = [[r[...] for r in refs[at : at + count]], [r[...] for r in refs[at + count : at + 2 * count]]]
-            at += 2 * count
-        sums = [
-            jnp.concatenate(
-                [lax.dot_general(left, w, NT, preferred_element_type=F32) for w in ws], axis=1
+            zero = jnp.zeros_like(left)
+            both = jnp.concatenate(
+                [jnp.concatenate([left, zero], axis=1), jnp.concatenate([zero, left], axis=1)], axis=0
             )
-            for ws in pair
-        ]
+            sums = []
+            for _ in range(2):
+                part = jnp.concatenate(
+                    [
+                        lax.dot_general(both, r[...], NT, preferred_element_type=F32)
+                        for r in refs[at : at + count]
+                    ],
+                    axis=1,
+                )
+                rows = left.shape[0]
+                sums.append(jnp.concatenate([part[:rows], part[rows:]], axis=1))
+                at += count
         mine, mate = (sums[0], sums[1]) if mine is None else (mine + sums[0], mate + sums[1])
     total = jnp.concatenate(
         [jnp.where(core == 0, mine, mate), jnp.where(core == 0, mate, mine)], axis=1
@@ -385,7 +399,7 @@
         + [pl.BlockSpec(memory_space=pl.ANY)],
         out_specs=[vmem] * 2,
         out_shape=[jax.ShapeDtypeStruct(base.shape, F32), jax.ShapeDtypeStruct(base.shape, BF)],
-        compiler_params=params(20),
+        compiler_params=params(12),
         cost_estimate=cost(2e9, 16 * base.size),
         name="project",
     )(place, base, *attended, *weights, gain, shift, last)
@@ -554,7 +568,11 @@
     featured = [tokens[0]] + [hop(tokens[k], k, n_mp) for k in range(1, n_mp)]
 
     own = mixed[:, :hc]
-    part = lax.dynamic_slice_in_dim(own, (d % 2) * (width // 2), width // 2)
+    quarter = width // 4
+    part = jnp.concatenate(
+        [lax.dynamic_slice_in_dim(own, (d % 2) * 2 * quarter + i * quarter, quarter) for i in range(2)],
+        axis=1,
+    )
     mate = [(i, i ^ 1) for i in range(n_dp)]
     out_weights = [[[own]]]
     for pieces in gather_blocks([part], n_mp)[1:]:

time: 231 us -> 223 us (0.965)
  waiting for transfers between devices: 101 us -> 87.3 us
  starting transfers between devices: 41.2 us -> 48.8 us
    ppermute x7, waiting for transfers between devices: 34.6 us -> 25.4 us  [per_device(): lax.ppermute(packed[i], 'dp', [(j, j ^ i) for j in range(n_dp)])]
    ppermute x32, waiting for transfers between devices: 66.4 us -> 61.8 us  [hop(): return lax.ppermute(value, 'mp', [(i, i ^ k) for i in range(n)])]
    ppermute x32, starting transfers between devices: 32.3 us -> 36.2 us  [hop(): return lax.ppermute(value, 'mp', [(i, i ^ k) for i in range(n)])]
    ppermute x7, starting transfers between devices: 7.89 us -> 11.6 us  [per_device(): lax.ppermute(packed[i], 'dp', [(j, j ^ i) for j in range(n_dp)])]
  transfers between devices with their start and end apart: 45 -> 45, of which waited for: 19 -> 19; matrix products, arithmetic and copies ran while one was open for 4% -> 4% of each run, Pallas kernels for 20% -> 21%
where the time goes in v4:
time: 223 us; the launch traced here: 221 us
  waiting for transfers between devices  87.3 us (39%)
  Pallas kernels  53.5 us (24%)
  starting transfers between devices  48.8 us (22%)
  between operations  13.7 us (6%)
  local copies, waits for them, and re-layouts  12.4 us (6%)
  other arithmetic  5.27 us (2%)
    ppermute x32, waiting for transfers between devices, hop(): return lax.ppermute(value, 'mp', [(i, i ^ k) for i in range(n)])  61.8 us
    ppermute x32, starting transfers between devices, hop(): return lax.ppermute(value, 'mp', [(i, i ^ k) for i in range(n)])  36.2 us
    ppermute x7, waiting for transfers between devices, per_device(): lax.ppermute(packed[i], 'dp', [(j, j ^ i) for j in range(n_dp)])  25.4 us
    pallas_call x2, Pallas kernels, attend(): pl.pallas_call(functools.partial(attend_kernel, [len(g) for g in gathered...  19.2 us
    pallas_call x4, Pallas kernels, mlp(): pl.pallas_call(functools.partial(mlp_kernel, len(rows)), in_specs=[vmem]...  12.9 us
    ppermute x7, starting transfers between devices, per_device(): lax.ppermute(packed[i], 'dp', [(j, j ^ i) for j in range(n_dp)])  11.6 us
    unnamed x38, local copies, waits for them, and re-layouts  7.88 us
    pallas_call x2, Pallas kernels, project(): pl.pallas_call(functools.partial(project_kernel, [len(w[0]) for w in out_...  6.03 us
  transfers between devices with their start and end apart: 45, of which 19 were waited for; matrix products, arithmetic and copies ran while one was open for 4% of the time, Pallas kernels for 21%

profile of v4, /device:TPU:0, one launch (start us, length us, event | category | flops | bytes accessed | tf_op | source)
XLA Modules:
  0.0 221.0 jit_solution(13673182387046805640)
XLA Ops:
  6.5 1.9 join.1
  8.5 2.1 pad_maximum_fusion
  11.2 5.9 %embed.1 = (bf16[320,512]{1,0:T(8,128)(2,1)}, bf16[320,512]{1,0:T(8,128)(2,1)}, bf16[320,512]{1,0:T(8,128)(2,1)}, bf16[320,512]{1,0:T(8,128)(2,1)}) custom-call(s32[2]{0:T(128)} %pad_add_fusion.place_ref, s32[8,64]{1,0:T(8,128)} %keep_ref.1, bf16[8,256,1280]{2,1,0:T(8,128)(2,1)} %patches_ref.1, bf16[256,1280]{1,0:T(8,128)(2,1)} %position_ref.1), custom_call_target="tpu_custom_call" | custom-call | flops 4000000000 | bytes 5242880 | tf_op jit(solution)/shard_map/embed/pallas_call | solution.py:58
  17.1 3.0 %collective-permute-start = (bf16[320,512]{1,0:T(8,128)(2,1)}, bf16[320,512]{1,0:T(8,128)(2,1)S(1)}, u32[]{:S(2)}, u32[]{:S(2)}) collective-permute-start(bf16[320,512]{1,0:T(8,128)(2,1)} %get-tuple-element.42), channel_id=1, source_target_pairs={{0,1},{1,0},{2,3},{3,2},{4,5},{5,4},{6,7},{7,6},{8,9},{9,8},{10,11... | collective-permute-start | bytes 983048 | tf_op jit(solution)/shard_map/ppermute | solution.py:502
  20.1 1.5 collective-permute-start.1
  22.6 6.3 %collective-permute-done.refs_1_ = bf16[320,512]{1,0:T(8,128)(2,1)S(1)} collective-permute-done((bf16[320,512]{1,0:T(8,128)(2,1)}, bf16[320,512]{1,0:T(8,128)(2,1)S(1)}, u32[]{:S(2)}, u32[]{:S(2)}) %collective-permute-start) | collective-permute-done | bytes 327712 | tf_op jit(solution)/shard_map/ppermute | solution.py:502
  28.8 7.6 %collective-permute-done.1.refs_2_ = bf16[320,512]{1,0:T(8,128)(2,1)S(1)} collective-permute-done((bf16[320,512]{1,0:T(8,128)(2,1)}, bf16[320,512]{1,0:T(8,128)(2,1)S(1)}, u32[]{:S(2)}, u32[]{:S(2)}) %collective-permute-start.1) | collective-permute-done | bytes 327712 | tf_op jit(solution)/shard_map/ppermute | solution.py:502
  36.5 1.0 copy-done.13
  37.4 3.5 %pack.1 = (bf16[80,640]{1,0:T(8,128)(2,1)S(1)}, bf16[80,640]{1,0:T(8,128)(2,1)S(1)}, bf16[80,640]{1,0:T(8,128)(2,1)S(1)}, bf16[80,640]{1,0:T(8,128)(2,1)S(1)}, b...) custom-call(s32[2]{0:T(128)S(1)} %copy-done.8, ...), custom_call_target="tpu_custom_call" | custom-call | flops 4000000000 | bytes 1310720 | tf_op jit(solution)/shard_map/pack/pallas_call | solution.py:125
  41.1 1.6 collective-permute-start.4
  42.9 3.2 %collective-permute-start.9 = (bf16[80,640]{1,0:T(8,128)(2,1)S(1)}, bf16[80,640]{1,0:T(8,128)(2,1)S(1)}, u32[]{:S(2)}, u32[]{:S(2)}) collective-permute-start(bf16[80,640]{1,0:T(8,128)(2,1)S(1)} %get-tuple-element.52), channel_id=1, source_target_pairs={{0,28},{4,24},{8,20},{12,16},{16,12},{20,8},{24,4},{28,0},{1,29},{... | collective-permute-start | bytes 307208 | tf_op jit(solution)/shard_map/ppermute | solution.py:596
  46.1 4.5 %collective-permute-done.5 = bf16[80,640]{1,0:T(8,128)(2,1)S(1)} collective-permute-done((bf16[80,640]{1,0:T(8,128)(2,1)S(1)}, bf16[80,640]{1,0:T(8,128)(2,1)S(1)}, u32[]{:S(2)}, u32[]{:S(2)}) %collective-permute-start.5) | collective-permute-done | bytes 102432 | tf_op jit(solution)/shard_map/ppermute | solution.py:596
  50.6 2.2 collective-permute-done.4
  52.8 1.5 collective-permute-start.10
  54.4 1.5 collective-permute-start.12
  56.3 4.6 %collective-permute-start.8 = (bf16[80,640]{1,0:T(8,128)(2,1)S(1)}, bf16[80,640]{1,0:T(8,128)(2,1)S(1)}, u32[]{:S(2)}, u32[]{:S(2)}) collective-permute-start(bf16[80,640]{1,0:T(8,128)(2,1)S(1)} %get-tuple-element.51), channel_id=1, source_target_pairs={{0,24},{4,28},{8,16},{12,20},{16,8},{20,12},{24,0},{28,4},{1,25},{... | collective-permute-start | bytes 307208 | tf_op jit(solution)/shard_map/ppermute | solution.py:596
  60.9 1.8 collective-permute-start.6
  63.6 1.1 collective-permute-done.8
  64.7 9.0 %collective-permute-done.7 = bf16[80,640]{1,0:T(8,128)(2,1)S(1)} collective-permute-done((bf16[80,640]{1,0:T(8,128)(2,1)S(1)}, bf16[80,640]{1,0:T(8,128)(2,1)S(1)}, u32[]{:S(2)}, u32[]{:S(2)}) %collective-permute-start.7) | collective-permute-done | bytes 102432 | tf_op jit(solution)/shard_map/ppermute | solution.py:596
  73.7 8.6 %collective-permute-done.6 = bf16[80,640]{1,0:T(8,128)(2,1)S(1)} collective-permute-done((bf16[80,640]{1,0:T(8,128)(2,1)S(1)}, bf16[80,640]{1,0:T(8,128)(2,1)S(1)}, u32[]{:S(2)}, u32[]{:S(2)}) %collective-permute-start.6) | collective-permute-done | bytes 102432 | tf_op jit(solution)/shard_map/ppermute | solution.py:596
  82.7 3.2 %collective-permute-start.16 = (bf16[4,80,640]{2,1,0:T(8,128)(2,1)S(1)}, bf16[4,80,640]{2,1,0:T(8,128)(2,1)}, u32[]{:S(2)}, u32[]{:S(2)}) collective-permute-start(bf16[4,80,640]{2,1,0:T(8,128)(2,1)S(1)} %pad_maximum_fusion.2.refs_1_), channel_id=1, source_target_pairs={{0,3},{1,2},{2,1},{3,0},{4,7},{5,6},{6,5},{7,4},{8,11},{9,10},{10,... | collective-permute-start | bytes 1228808 | tf_op jit(solution)/shard_map/ppermute | solution.py:502
  86.0 0.7 slice.38
  86.7 0.7 slice.39
  87.9 1.5 slice.40.refs_4_
  89.6 17.9 %collective-permute-done.14.refs_6_.refs_3_ = bf16[2,80,640]{2,1,0:T(8,128)(2,1)S(1)} collective-permute-done((bf16[2,80,640]{2,1,0:T(8,128)(2,1)}, bf16[2,80,640]{2,1,0:T(8,128)(2,1)S(1)}, u32[]{:S(2)}, u32[]{:S(2)}) %collective-permute-start.14) | collective-permute-done | bytes 204832 | tf_op jit(solution)/shard_map/ppermute | solution.py:502
  107.5 1.7 collective-permute-start.20
  109.4 9.4 %attend.2.refs_15_ = bf16[2,2,80,640]{3,2,1,0:T(8,128)(2,1)S(1)} custom-call(s32[2]{0:T(128)S(1)} %copy-done.8, bf16[4,80,640]{2,1,0:T(8,128)(2,1)S(1)} %pad_maximum_fusion.1.refs_0_, bf16[4,80,640]{2,1,0:T(8,128)(2,1)S(1)} %collective-permute-done.10.refs_2_.refs_1_, bf16[4,80,640]{2,1,0:T(8,128)(2,1)S(1)} %collective-permute-done.12.refs_4_.refs_2_, ...), custom_call_target="tpu_custom_call" | custom-call | flops 8000000000 | bytes 6553600 | tf_op jit(solution)/shard_map/attend/pallas_call | solution.py:272
  118.9 1.8 collective-permute-start.24
  121.7 9.8 %attend.3 = (bf16[80,640]{1,0:T(8,128)(2,1)S(1)}, bf16[80,640]{1,0:T(8,128)(2,1)S(1)}, bf16[80,640]{1,0:T(8,128)(2,1)S(1)}, bf16[80,640]{1,0:T(8,128)(2,1)S(1)},...) custom-call(s32[2]{0:T(128)S(1)} %copy-done.8, ...), custom_call_target="tpu_custom_call" | custom-call | flops 8000000000 | bytes 6553600 | tf_op jit(solution)/shard_map/attend/pallas_call | solution.py:272
  131.4 1.7 collective-permute-start.28
  133.2 3.2 %collective-permute-done.28.refs_1_ = bf16[80,640]{1,0:T(8,128)(2,1)S(1)} collective-permute-done((bf16[80,640]{1,0:T(8,128)(2,1)S(1)}, bf16[80,640]{1,0:T(8,128)(2,1)S(1)}, u32[]{:S(2)}, u32[]{:S(2)}) %collective-permute-start.28) | collective-permute-done | bytes 102432 | tf_op jit(solution)/shard_map/ppermute | solution.py:502
  136.4 0.9 collective-permute-start.29
  137.8 3.2 %collective-permute-done.29.refs_2_ = bf16[80,640]{1,0:T(8,128)(2,1)S(1)} collective-permute-done((bf16[80,640]{1,0:T(8,128)(2,1)S(1)}, bf16[80,640]{1,0:T(8,128)(2,1)S(1)}, u32[]{:S(2)}, u32[]{:S(2)}) %collective-permute-start.29) | collective-permute-done | bytes 102432 | tf_op jit(solution)/shard_map/ppermute | solution.py:502
  141.0 1.4 collective-permute-start.30
  142.4 2.2 %own.1 = (f32[160,1280]{1,0:T(8,128)S(1)}, f32[160,1280]{1,0:T(8,128)S(1)}) custom-call(s32[2]{0:T(128)S(1)} %copy-done.8, bf16[4,80,640]{2,1,0:T(8,128)(2,1)S(1)} %pad_maximum_fusion.1.refs_0_, bf16[4,80,640]{2,1,0:T(8,128)(2,1)S(1)} %pad_maximum_fusion.2.refs_1_, bf16[4,80,640]{2,1,0:T(8,128)(2,1)S(1)} %collective-permute-done.10.refs_2_.refs_1_, ...), custom_call_target="tpu_custom_call" | custom-call | flops 1000000000 | bytes 409600 | tf_op jit(solution)/shard_map/own/pallas_call | solution.py:325
  144.6 2.0 collective-permute-done.30.refs_3_
  146.6 2.4 %collective-permute-start.17 = (bf16[80,640]{1,0:T(8,128)(2,1)S(1)}, bf16[80,640]{1,0:T(8,128)(2,1)S(1)}, u32[]{:S(2)}, u32[]{:S(2)}) collective-permute-start(bf16[80,640]{1,0:T(8,128)(2,1)S(1)} %get-tuple-element.55), channel_id=1, source_target_pairs={{0,1},{1,0},{2,3},{3,2},{4,5},{5,4},{6,7},{7,6},{8,9},{9,8},{10,11... | collective-permute-start | bytes 307208 | tf_op jit(solution)/shard_map/ppermute | solution.py:502
  149.0 1.5 collective-permute-start.19
  150.5 3.0 %project.2 = (f32[160,1280]{1,0:T(8,128)S(1)}, bf16[160,1280]{1,0:T(8,128)(2,1)S(1)}) custom-call(s32[2]{0:T(128)S(1)} %copy-done.8, f32[160,1280]{1,0:T(8,128)S(1)} %get-tuple-element.58.base_ref.refs_15_, bf16[80,640]{1,0:T(8,128)(2,1)S(1)} %get-tuple-element.59.refs_0_, bf16[80,640]{1,0:T(8,128)(2,1)S(1)} %collective-permute-done.28.refs_1_, ...), custom_call_target="tpu_custom_call" | custom-call | flops 2000000000 | bytes 3276800 | tf_op jit(solution)/shard_map/project/pallas_call | solution.py:395
  153.5 2.1 collective-permute-start.33
  155.7 3.0 %project.3 = (f32[160,1280]{1,0:T(8,128)S(1)}, bf16[160,1280]{1,0:T(8,128)(2,1)S(1)}) custom-call(s32[2]{0:T(128)S(1)} %copy-done.8, f32[160,1280]{1,0:T(8,128)S(1)} %get-tuple-element.53.base_ref, bf16[80,640]{1,0:T(8,128)(2,1)S(1)} %get-tuple-element.54.refs_0_, bf16[80,640]{1,0:T(8,128)(2,1)S(1)} %collective-permute-done.17.refs_1_, ...), custom_call_target="tpu_custom_call" | custom-call | flops 2000000000 | bytes 3276800 | tf_op jit(solution)/shard_map/project/pallas_call | solution.py:395
  158.8 0.9 copy-done.11
  159.7 2.0 collective-permute-start.34
  162.3 3.7 %collective-permute-done.33.refs_0_ = bf16[160,1280]{1,0:T(8,128)(2,1)S(1)} collective-permute-done((bf16[160,1280]{1,0:T(8,128)(2,1)S(1)}, bf16[160,1280]{1,0:T(8,128)(2,1)S(1)}, u32[]{:S(2)}, u32[]{:S(2)}) %collective-permute-start.33) | collective-permute-done | bytes 409632 | tf_op jit(solution)/shard_map/ppermute | solution.py:502
  165.9 0.6 collective-permute-start.35
  166.5 5.6 %collective-permute-done.34.refs_1_ = bf16[160,1280]{1,0:T(8,128)(2,1)S(1)} collective-permute-done((bf16[160,1280]{1,0:T(8,128)(2,1)S(1)}, bf16[160,1280]{1,0:T(8,128)(2,1)S(1)}, u32[]{:S(2)}, u32[]{:S(2)}) %collective-permute-start.34) | collective-permute-done | bytes 409632 | tf_op jit(solution)/shard_map/ppermute | solution.py:502
  172.6 2.9 %copy-done = bf16[1280,2560]{1,0:T(8,128)(2,1)S(1)} copy-done((bf16[1280,2560]{1,0:T(8,128)(2,1)S(1)}, bf16[1280,2560]{1,0:T(8,128)(2,1)}, u32[]{:S(2)}) %copy-start) | copy-done | bytes 6553624
  175.4 2.4 %shard_map.145 = (bf16[160,1280]{1,0:T(8,128)(2,1)S(1)}, bf16[160,1280]{1,0:T(8,128)(2,1)S(1)}) custom-call(bf16[160,1280]{1,0:T(8,128)(2,1)S(1)} %get-tuple-element.63.refs_15_.refs_0_.refs_4_, bf16[160,1280]{1,0:T(8,128)(2,1)S(1)} %get-tuple-element.64.refs_1_, bf16[1280,2560]{1,0:T(8,128)(2,1)S(1)} %copy-done, f32[1,1280]{1,0:T(1,128)S(1)} %copy-done.3, ...), custom_call_target="tpu_custom_call" | custom-call | flops 2097152000 | bytes 6553600 | tf_op jit(solution)/shard_map/pallas_call | solution.py:432
  177.9 0.8 copy-done.4
  178.7 3.2 %shard_map.146 = (bf16[160,1280]{1,0:T(8,128)(2,1)S(1)}, bf16[160,1280]{1,0:T(8,128)(2,1)}) custom-call(bf16[160,1280]{1,0:T(8,128)(2,1)S(1)} %collective-permute-done.33.refs_0_, bf16[160,1280]{1,0:T(8,128)(2,1)S(1)} %collective-permute-done.34.refs_1_, bf16[1280,2560]{1,0:T(8,128)(2,1)S(1)} %copy-done.1, f32[1,1280]{1,0:T(1,128)S(1)} %copy-done.3, ...), custom_call_target="tpu_custom_call" | custom-call | flops 2097152000 | bytes 6553600 | tf_op jit(solution)/shard_map/pallas_call | solution.py:432
  181.9 3.6 %shard_map.147 = (bf16[160,1280]{1,0:T(8,128)(2,1)S(1)}, bf16[160,1280]{1,0:T(8,128)(2,1)S(1)}) custom-call(bf16[160,1280]{1,0:T(8,128)(2,1)} %collective-permute-done.31.refs_0_, bf16[160,1280]{1,0:T(8,128)(2,1)} %collective-permute-done.32.refs_1_, bf16[1280,2560]{1,0:T(8,128)(2,1)S(1)} %copy-done.1, f32[1,1280]{1,0:T(1,128)S(1)} %copy-done.3, ...), custom_call_target="tpu_custom_call" | custom-call | flops 2097152000 | bytes 6553600 | tf_op jit(solution)/shard_map/pallas_call | solution.py:432
  185.4 3.7 %shard_map.148 = (bf16[160,1280]{1,0:T(8,128)(2,1)S(1)}, bf16[160,1280]{1,0:T(8,128)(2,1)S(1)}) custom-call(bf16[160,1280]{1,0:T(8,128)(2,1)S(1)} %collective-permute-done.35.refs_0_, bf16[160,1280]{1,0:T(8,128)(2,1)} %collective-permute-done.36.refs_1_, bf16[1280,2560]{1,0:T(8,128)(2,1)S(1)} %copy-done.1, f32[1,1280]{1,0:T(1,128)S(1)} %copy-done.3, ...), custom_call_target="tpu_custom_call" | custom-call | flops 2097152000 | bytes 6553600 | tf_op jit(solution)/shard_map/pallas_call | solution.py:432
  189.2 1.6 collective-permute-start.37
  191.3 1.5 collective-permute-start.39
  193.3 7.9 %collective-permute-done.37 = bf16[160,1280]{1,0:T(8,128)(2,1)S(1)} collective-permute-done((bf16[160,1280]{1,0:T(8,128)(2,1)S(1)}, bf16[160,1280]{1,0:T(8,128)(2,1)S(1)}, u32[]{:S(2)}, u32[]{:S(2)}) %collective-permute-start.37) | collective-permute-done | bytes 409632 | tf_op jit(solution)/shard_map/ppermute | solution.py:502
  201.2 0.9 add_convert_fusion.1
  202.0 1.5 collective-permute-start.38
  203.5 0.8 add_convert_fusion
  204.4 1.2 collective-permute-start.40
  206.1 1.5 collective-permute-done.42.refs_3_
  207.6 1.1 copy-done.10
  208.7 1.1 copy-done.12
  210.1 1.8 collective-permute-done.38.refs_0_
  212.5 1.6 finish.1
  (119 shorter events, 9.9 us)
Async XLA Ops:
  6.5 81.4 %all-gather.3.cloned.1.call-start = ((), (), s32[]{:S(2)}) async-start(), calls=%async_computation | async-start | bytes 3686400 | tf_op jit(solution)/shard_map/all_gather | solution.py:566
  8.5 164.1 %all-gather.5.cloned.1.call-start = ((), (), s32[]{:S(2)}) async-start(), calls=%async_computation.1 | async-start | bytes 7372800 | tf_op jit(solution)/shard_map/all_gather | solution.py:601
  11.2 10.4 %copy-start.18 = (s32[256]{0:T(256)S(1)}, s32[256]{0:T(256)}, u32[]{:S(2)}) copy-start(s32[256]{0:T(256)} %param.18) | copy-start | bytes 3076
  11.2 10.8 %copy-start.16 = (s32[256]{0:T(256)S(1)}, s32[256]{0:T(256)}, u32[]{:S(2)}) copy-start(s32[256]{0:T(256)} %param.19) | copy-start | bytes 3076
  11.2 11.4 %copy-start.14 = (f32[1,2,1280]{2,1,0:T(2,128)S(1)}, f32[1,2,1280]{2,1,0:T(2,128)}, u32[]{:S(2)}) copy-start(f32[1,2,1280]{2,1,0:T(2,128)} %param.21) | copy-start | bytes 30724
  11.2 11.4 %copy-start.15 = (f32[1,2,1280]{2,1,0:T(2,128)S(1)}, f32[1,2,1280]{2,1,0:T(2,128)}, u32[]{:S(2)}) copy-start(f32[1,2,1280]{2,1,0:T(2,128)} %param.20) | copy-start | bytes 30724
  11.2 25.3 %copy-start.8 = (s32[2]{0:T(128)S(1)}, s32[2]{0:T(128)}, u32[]{:S(2)}) copy-start(s32[2]{0:T(128)} %pad_add_fusion.place_ref) | copy-start | bytes 28
  17.1 11.8 %collective-permute-start = (bf16[320,512]{1,0:T(8,128)(2,1)}, bf16[320,512]{1,0:T(8,128)(2,1)S(1)}, u32[]{:S(2)}, u32[]{:S(2)}) collective-permute-start(bf16[320,512]{1,0:T(8,128)(2,1)} %get-tuple-element.42), channel_id=1, source_target_pairs={{0,1},{1,0},{2,3},{3,2},{4,5},{5,4},{6,7},{7,6},{8,9},{9,8},{10,11... | collective-permute-start | bytes 983048 | tf_op jit(solution)/shard_map/ppermute | solution.py:502
  20.1 16.4 %collective-permute-start.1 = (bf16[320,512]{1,0:T(8,128)(2,1)}, bf16[320,512]{1,0:T(8,128)(2,1)S(1)}, u32[]{:S(2)}, u32[]{:S(2)}) collective-permute-start(bf16[320,512]{1,0:T(8,128)(2,1)} %get-tuple-element.43), channel_id=1, source_target_pairs={{0,2},{1,3},{2,0},{3,1},{4,6},{5,7},{6,4},{7,5},{8,10},{9,11},{10,... | collective-permute-start | bytes 983048 | tf_op jit(solution)/shard_map/ppermute | solution.py:502
  21.6 14.9 %collective-permute-start.2 = (bf16[320,512]{1,0:T(8,128)(2,1)}, bf16[320,512]{1,0:T(8,128)(2,1)S(1)}, u32[]{:S(2)}, u32[]{:S(2)}) collective-permute-start(bf16[320,512]{1,0:T(8,128)(2,1)} %get-tuple-element.44), channel_id=1, source_target_pairs={{0,3},{1,2},{2,1},{3,0},{4,7},{5,6},{6,5},{7,4},{8,11},{9,10},{10,... | collective-permute-start | bytes 983048 | tf_op jit(solution)/shard_map/ppermute | solution.py:502
  36.5 1.0 copy-start.13
  37.4 25.9 %copy-start.17 = (f32[1,3,320]{2,0,1:T(1,128)S(1)}, f32[1,3,320]{2,0,1:T(1,128)}, u32[]{:S(2)}) copy-start(f32[1,3,320]{2,0,1:T(1,128)} %param.23) | copy-start | bytes 11524
  40.9 9.6 %collective-permute-start.5 = (bf16[80,640]{1,0:T(8,128)(2,1)S(1)}, bf16[80,640]{1,0:T(8,128)(2,1)S(1)}, u32[]{:S(2)}, u32[]{:S(2)}) collective-permute-start(bf16[80,640]{1,0:T(8,128)(2,1)S(1)} %get-tuple-element.48), channel_id=1, source_target_pairs={{0,12},{4,8},{8,4},{12,0},{16,28},{20,24},{24,20},{28,16},{1,13},{... | collective-permute-start | bytes 307208 | tf_op jit(solution)/shard_map/ppermute | solution.py:596
  41.1 11.7 %collective-permute-start.4 = (bf16[80,640]{1,0:T(8,128)(2,1)S(1)}, bf16[80,640]{1,0:T(8,128)(2,1)S(1)}, u32[]{:S(2)}, u32[]{:S(2)}) collective-permute-start(bf16[80,640]{1,0:T(8,128)(2,1)S(1)} %get-tuple-element.47), channel_id=1, source_target_pairs={{0,8},{4,12},{8,0},{12,4},{16,24},{20,28},{24,16},{28,20},{1,9},{5... | collective-permute-start | bytes 307208 | tf_op jit(solution)/shard_map/ppermute | solution.py:596
  42.6 10.1 %collective-permute-start.3 = (bf16[80,640]{1,0:T(8,128)(2,1)S(1)}, bf16[80,640]{1,0:T(8,128)(2,1)S(1)}, u32[]{:S(2)}, u32[]{:S(2)}) collective-permute-start(bf16[80,640]{1,0:T(8,128)(2,1)S(1)} %get-tuple-element.46), channel_id=1, source_target_pairs={{0,4},{4,0},{8,12},{12,8},{16,20},{20,16},{24,28},{28,24},{1,5},{5... | collective-permute-start | bytes 307208 | tf_op jit(solution)/shard_map/ppermute | solution.py:596
  42.9 18.1 %collective-permute-start.9 = (bf16[80,640]{1,0:T(8,128)(2,1)S(1)}, bf16[80,640]{1,0:T(8,128)(2,1)S(1)}, u32[]{:S(2)}, u32[]{:S(2)}) collective-permute-start(bf16[80,640]{1,0:T(8,128)(2,1)S(1)} %get-tuple-element.52), channel_id=1, source_target_pairs={{0,28},{4,24},{8,20},{12,16},{16,12},{20,8},{24,4},{28,0},{1,29},{... | collective-permute-start | bytes 307208 | tf_op jit(solution)/shard_map/ppermute | solution.py:596
  52.8 33.1 %collective-permute-start.10 = (bf16[4,80,640]{2,1,0:T(8,128)(2,1)S(1)}, bf16[4,80,640]{2,1,0:T(8,128)(2,1)S(1)}, u32[]{:S(2)}, u32[]{:S(2)}) collective-permute-start(bf16[4,80,640]{2,1,0:T(8,128)(2,1)S(1)} %pad_maximum_fusion.1.refs_0_), channel_id=1, source_target_pairs={{0,1},{1,0},{2,3},{3,2},{4,5},{5,4},{6,7},{7,6},{8,9},{9,8},{10,11... | collective-permute-start | bytes 1228808 | tf_op jit(solution)/shard_map/ppermute | solution.py:502
  54.4 32.3 %collective-permute-start.12 = (bf16[4,80,640]{2,1,0:T(8,128)(2,1)S(1)}, bf16[4,80,640]{2,1,0:T(8,128)(2,1)S(1)}, u32[]{:S(2)}, u32[]{:S(2)}) collective-permute-start(bf16[4,80,640]{2,1,0:T(8,128)(2,1)S(1)} %pad_maximum_fusion.1.refs_0_), channel_id=1, source_target_pairs={{0,2},{1,3},{2,0},{3,1},{4,6},{5,7},{6,4},{7,5},{8,10},{9,11},{10,... | collective-permute-start | bytes 1228808 | tf_op jit(solution)/shard_map/ppermute | solution.py:502
  56.3 8.4 %collective-permute-start.8 = (bf16[80,640]{1,0:T(8,128)(2,1)S(1)}, bf16[80,640]{1,0:T(8,128)(2,1)S(1)}, u32[]{:S(2)}, u32[]{:S(2)}) collective-permute-start(bf16[80,640]{1,0:T(8,128)(2,1)S(1)} %get-tuple-element.51), channel_id=1, source_target_pairs={{0,24},{4,28},{8,16},{12,20},{16,8},{20,12},{24,0},{28,4},{1,25},{... | collective-permute-start | bytes 307208 | tf_op jit(solution)/shard_map/ppermute | solution.py:596
  60.9 12.8 %collective-permute-start.7 = (bf16[80,640]{1,0:T(8,128)(2,1)S(1)}, bf16[80,640]{1,0:T(8,128)(2,1)S(1)}, u32[]{:S(2)}, u32[]{:S(2)}) collective-permute-start(bf16[80,640]{1,0:T(8,128)(2,1)S(1)} %get-tuple-element.50), channel_id=1, source_target_pairs={{0,20},{4,16},{8,28},{12,24},{16,4},{20,0},{24,12},{28,8},{1,21},{... | collective-permute-start | bytes 307208 | tf_op jit(solution)/shard_map/ppermute | solution.py:596
  60.9 21.4 %collective-permute-start.6 = (bf16[80,640]{1,0:T(8,128)(2,1)S(1)}, bf16[80,640]{1,0:T(8,128)(2,1)S(1)}, u32[]{:S(2)}, u32[]{:S(2)}) collective-permute-start(bf16[80,640]{1,0:T(8,128)(2,1)S(1)} %get-tuple-element.49), channel_id=1, source_target_pairs={{0,16},{4,20},{8,24},{12,28},{16,0},{20,4},{24,8},{28,12},{1,17},{... | collective-permute-start | bytes 307208 | tf_op jit(solution)/shard_map/ppermute | solution.py:596
  82.4 38.7 %collective-permute-start.11 = (bf16[4,80,640]{2,1,0:T(8,128)(2,1)S(1)}, bf16[4,80,640]{2,1,0:T(8,128)(2,1)S(1)}, u32[]{:S(2)}, u32[]{:S(2)}) collective-permute-start(bf16[4,80,640]{2,1,0:T(8,128)(2,1)S(1)} %pad_maximum_fusion.2.refs_1_), channel_id=1, source_target_pairs={{0,1},{1,0},{2,3},{3,2},{4,5},{5,4},{6,7},{7,6},{8,9},{9,8},{10,11... | collective-permute-start | bytes 1228808 | tf_op jit(solution)/shard_map/ppermute | solution.py:502
  82.7 38.4 %collective-permute-start.13 = (bf16[4,80,640]{2,1,0:T(8,128)(2,1)S(1)}, bf16[4,80,640]{2,1,0:T(8,128)(2,1)S(1)}, u32[]{:S(2)}, u32[]{:S(2)}) collective-permute-start(bf16[4,80,640]{2,1,0:T(8,128)(2,1)S(1)} %pad_maximum_fusion.2.refs_1_), channel_id=1, source_target_pairs={{0,2},{1,3},{2,0},{3,1},{4,6},{5,7},{6,4},{7,5},{8,10},{9,11},{10,... | collective-permute-start | bytes 1228808 | tf_op jit(solution)/shard_map/ppermute | solution.py:502
  82.7 38.9 %collective-permute-start.16 = (bf16[4,80,640]{2,1,0:T(8,128)(2,1)S(1)}, bf16[4,80,640]{2,1,0:T(8,128)(2,1)}, u32[]{:S(2)}, u32[]{:S(2)}) collective-permute-start(bf16[4,80,640]{2,1,0:T(8,128)(2,1)S(1)} %pad_maximum_fusion.2.refs_1_), channel_id=1, source_target_pairs={{0,3},{1,2},{2,1},{3,0},{4,7},{5,6},{6,5},{7,4},{8,11},{9,10},{10,... | collective-permute-start | bytes 1228808 | tf_op jit(solution)/shard_map/ppermute | solution.py:502
  86.7 20.8 %collective-permute-start.14 = (bf16[2,80,640]{2,1,0:T(8,128)(2,1)}, bf16[2,80,640]{2,1,0:T(8,128)(2,1)S(1)}, u32[]{:S(2)}, u32[]{:S(2)}) collective-permute-start(bf16[2,80,640]{2,1,0:T(8,128)(2,1)} %slice.38), channel_id=1, source_target_pairs={{0,2},{1,3},{2,0},{3,1},{4,6},{5,7},{6,4},{7,5},{8,10},{9,11},{10,... | collective-permute-start | bytes 614408 | tf_op jit(solution)/shard_map/ppermute | solution.py:502
  87.4 21.8 %collective-permute-start.15 = (bf16[2,80,640]{2,1,0:T(8,128)(2,1)}, bf16[2,80,640]{2,1,0:T(8,128)(2,1)}, u32[]{:S(2)}, u32[]{:S(2)}) collective-permute-start(bf16[2,80,640]{2,1,0:T(8,128)(2,1)} %slice.39), channel_id=1, source_target_pairs={{0,1},{1,0},{2,3},{3,2},{4,5},{5,4},{6,7},{7,6},{8,9},{9,8},{10,11... | collective-permute-start | bytes 614408 | tf_op jit(solution)/shard_map/ppermute | solution.py:502
  87.9 21.5 %copy-start.2 = (bf16[1280,1280]{1,0:T(8,128)(2,1)S(1)}, bf16[1280,1280]{1,0:T(8,128)(2,1)}, u32[]{:S(2)}) copy-start(bf16[1280,1280]{1,0:T(8,128)(2,1)} %all-gather.3.cloned.1.call-done.refs_5_.refs_9_) | copy-start | bytes 9830404
  107.5 11.4 %collective-permute-start.20 = (bf16[320,640]{1,0:T(8,128)(2,1)S(1)}, bf16[320,640]{1,0:T(8,128)(2,1)S(1)}, u32[]{:S(2)}, u32[]{:S(2)}) collective-permute-start(bf16[320,640]{1,0:T(8,128)(2,1)S(1)} %pad_maximum_fusion.3), channel_id=1, source_target_pairs={{0,1},{1,0},{2,3},{3,2},{4,5},{5,4},{6,7},{7,6},{8,9},{9,8},{10,11... | collective-permute-start | bytes 1228808 | tf_op jit(solution)/shard_map/ppermute | solution.py:502
  109.1 11.5 %collective-permute-start.22 = (bf16[320,640]{1,0:T(8,128)(2,1)S(1)}, bf16[320,640]{1,0:T(8,128)(2,1)S(1)}, u32[]{:S(2)}, u32[]{:S(2)}) collective-permute-start(bf16[320,640]{1,0:T(8,128)(2,1)S(1)} %pad_maximum_fusion.3), channel_id=1, source_target_pairs={{0,2},{1,3},{2,0},{3,1},{4,6},{5,7},{6,4},{7,5},{8,10},{9,11},{10,... | collective-permute-start | bytes 1228808 | tf_op jit(solution)/shard_map/ppermute | solution.py:502
  118.9 18.4 %collective-permute-start.24 = (bf16[160,640]{1,0:T(8,128)(2,1)S(1)}, bf16[160,640]{1,0:T(8,128)(2,1)S(1)}, u32[]{:S(2)}, u32[]{:S(2)}) collective-permute-start(bf16[160,640]{1,0:T(8,128)(2,1)S(1)} %slice.41), channel_id=1, source_target_pairs={{0,2},{1,3},{2,0},{3,1},{4,6},{5,7},{6,4},{7,5},{8,10},{9,11},{10,... | collective-permute-start | bytes 614408 | tf_op jit(solution)/shard_map/ppermute | solution.py:502
  120.7 21.7 %copy-start.6 = (f32[1,1280]{1,0:T(1,128)S(1)}, f32[1,1280]{1,0:T(1,128)}, u32[]{:S(2)}) copy-start(f32[1,1280]{1,0:T(1,128)} %refs_9_.1) | copy-start | bytes 15364
  120.7 16.6 %collective-permute-start.25 = (bf16[160,640]{1,0:T(8,128)(2,1)S(1)}, bf16[160,640]{1,0:T(8,128)(2,1)S(1)}, u32[]{:S(2)}, u32[]{:S(2)}) collective-permute-start(bf16[160,640]{1,0:T(8,128)(2,1)S(1)} %slice.42), channel_id=1, source_target_pairs={{0,1},{1,0},{2,3},{3,2},{4,5},{5,4},{6,7},{7,6},{8,9},{9,8},{10,11... | collective-permute-start | bytes 614408 | tf_op jit(solution)/shard_map/ppermute | solution.py:502
  121.1 27.9 %collective-permute-start.21 = (bf16[320,640]{1,0:T(8,128)(2,1)S(1)}, bf16[320,640]{1,0:T(8,128)(2,1)S(1)}, u32[]{:S(2)}, u32[]{:S(2)}) collective-permute-start(bf16[320,640]{1,0:T(8,128)(2,1)S(1)} %collective-permute-done.20.refs_5_), channel_id=1, source_target_pairs={{0,4},{4,0},{8,12},{12,8},{16,20},{20,16},{24,28},{28,24},{1,5},{5... | collective-permute-start | bytes 1228808 | tf_op jit(solution)/shard_map/ppermute | solution.py:579
  121.2 27.9 %collective-permute-start.23 = (bf16[320,640]{1,0:T(8,128)(2,1)S(1)}, bf16[320,640]{1,0:T(8,128)(2,1)S(1)}, u32[]{:S(2)}, u32[]{:S(2)}) collective-permute-start(bf16[320,640]{1,0:T(8,128)(2,1)S(1)} %collective-permute-done.22.refs_7_), channel_id=1, source_target_pairs={{0,4},{4,0},{8,12},{12,8},{16,20},{20,16},{24,28},{28,24},{1,5},{5... | collective-permute-start | bytes 1228808 | tf_op jit(solution)/shard_map/ppermute | solution.py:579
  131.4 4.9 %collective-permute-start.28 = (bf16[80,640]{1,0:T(8,128)(2,1)S(1)}, bf16[80,640]{1,0:T(8,128)(2,1)S(1)}, u32[]{:S(2)}, u32[]{:S(2)}) collective-permute-start(bf16[80,640]{1,0:T(8,128)(2,1)S(1)} %get-tuple-element.60), channel_id=1, source_target_pairs={{0,1},{1,0},{2,3},{3,2},{4,5},{5,4},{6,7},{7,6},{8,9},{9,8},{10,11... | collective-permute-start | bytes 307208 | tf_op jit(solution)/shard_map/ppermute | solution.py:502
  136.4 4.7 %collective-permute-start.29 = (bf16[80,640]{1,0:T(8,128)(2,1)S(1)}, bf16[80,640]{1,0:T(8,128)(2,1)S(1)}, u32[]{:S(2)}, u32[]{:S(2)}) collective-permute-start(bf16[80,640]{1,0:T(8,128)(2,1)S(1)} %get-tuple-element.61), channel_id=1, source_target_pairs={{0,2},{1,3},{2,0},{3,1},{4,6},{5,7},{6,4},{7,5},{8,10},{9,11},{10,... | collective-permute-start | bytes 307208 | tf_op jit(solution)/shard_map/ppermute | solution.py:502
  137.3 13.2 %collective-permute-start.26 = (bf16[160,640]{1,0:T(8,128)(2,1)S(1)}, bf16[160,640]{1,0:T(8,128)(2,1)S(1)}, u32[]{:S(2)}, u32[]{:S(2)}) collective-permute-start(bf16[160,640]{1,0:T(8,128)(2,1)S(1)} %collective-permute-done.24.refs_9_), channel_id=1, source_target_pairs={{0,4},{4,0},{8,12},{12,8},{16,20},{20,16},{24,28},{28,24},{1,5},{5... | collective-permute-start | bytes 614408 | tf_op jit(solution)/shard_map/ppermute | solution.py:579
  137.3 13.2 %collective-permute-start.27 = (bf16[160,640]{1,0:T(8,128)(2,1)S(1)}, bf16[160,640]{1,0:T(8,128)(2,1)S(1)}, u32[]{:S(2)}, u32[]{:S(2)}) collective-permute-start(bf16[160,640]{1,0:T(8,128)(2,1)S(1)} %collective-permute-done.25.refs_10_), channel_id=1, source_target_pairs={{0,4},{4,0},{8,12},{12,8},{16,20},{20,16},{24,28},{28,24},{1,5},{5... | collective-permute-start | bytes 614408 | tf_op jit(solution)/shard_map/ppermute | solution.py:579
  141.0 5.6 %collective-permute-start.30 = (bf16[80,640]{1,0:T(8,128)(2,1)S(1)}, bf16[80,640]{1,0:T(8,128)(2,1)S(1)}, u32[]{:S(2)}, u32[]{:S(2)}) collective-permute-start(bf16[80,640]{1,0:T(8,128)(2,1)S(1)} %get-tuple-element.62), channel_id=1, source_target_pairs={{0,3},{1,2},{2,1},{3,0},{4,7},{5,6},{6,5},{7,4},{8,11},{9,10},{10,... | collective-permute-start | bytes 307208 | tf_op jit(solution)/shard_map/ppermute | solution.py:502
  146.6 9.0 %collective-permute-start.17 = (bf16[80,640]{1,0:T(8,128)(2,1)S(1)}, bf16[80,640]{1,0:T(8,128)(2,1)S(1)}, u32[]{:S(2)}, u32[]{:S(2)}) collective-permute-start(bf16[80,640]{1,0:T(8,128)(2,1)S(1)} %get-tuple-element.55), channel_id=1, source_target_pairs={{0,1},{1,0},{2,3},{3,2},{4,5},{5,4},{6,7},{7,6},{8,9},{9,8},{10,11... | collective-permute-start | bytes 307208 | tf_op jit(solution)/shard_map/ppermute | solution.py:502
  149.0 6.6 %collective-permute-start.18 = (bf16[80,640]{1,0:T(8,128)(2,1)S(1)}, bf16[80,640]{1,0:T(8,128)(2,1)S(1)}, u32[]{:S(2)}, u32[]{:S(2)}) collective-permute-start(bf16[80,640]{1,0:T(8,128)(2,1)S(1)} %get-tuple-element.56), channel_id=1, source_target_pairs={{0,2},{1,3},{2,0},{3,1},{4,6},{5,7},{6,4},{7,5},{8,10},{9,11},{10,... | collective-permute-start | bytes 307208 | tf_op jit(solution)/shard_map/ppermute | solution.py:502
  149.0 6.7 %collective-permute-start.19 = (bf16[80,640]{1,0:T(8,128)(2,1)S(1)}, bf16[80,640]{1,0:T(8,128)(2,1)S(1)}, u32[]{:S(2)}, u32[]{:S(2)}) collective-permute-start(bf16[80,640]{1,0:T(8,128)(2,1)S(1)} %get-tuple-element.57), channel_id=1, source_target_pairs={{0,3},{1,2},{2,1},{3,0},{4,7},{5,6},{6,5},{7,4},{8,11},{9,10},{10,... | collective-permute-start | bytes 307208 | tf_op jit(solution)/shard_map/ppermute | solution.py:502
  153.5 5.3 %copy-start.9 = (f32[160,1280]{1,0:T(8,128)}, f32[160,1280]{1,0:T(8,128)S(1)}, u32[]{:S(2)}) copy-start(f32[160,1280]{1,0:T(8,128)S(1)} %get-tuple-element.73.refs_4_) | copy-start | bytes 2457604
  153.5 12.4 %collective-permute-start.33 = (bf16[160,1280]{1,0:T(8,128)(2,1)S(1)}, bf16[160,1280]{1,0:T(8,128)(2,1)S(1)}, u32[]{:S(2)}, u32[]{:S(2)}) collective-permute-start(bf16[160,1280]{1,0:T(8,128)(2,1)S(1)} %get-tuple-element.63.refs_15_.refs_0_.refs_4_), channel_id=1, source_target_pairs={{0,1},{1,0},{2,3},{3,2},{4,5},{5,4},{6,7},{7,6},{8,9},{9,8},{10,11... | collective-permute-start | bytes 1228808 | tf_op jit(solution)/shard_map/ppermute | solution.py:502
  155.7 16.8 %copy-start.3 = (f32[1,1280]{1,0:T(1,128)S(1)}, f32[1,1280]{1,0:T(1,128)}, u32[]{:S(2)}) copy-start(f32[1,1280]{1,0:T(1,128)} %refs_3_.7) | copy-start | bytes 15364
  158.8 1.0 copy-start.11
  159.7 12.3 %collective-permute-start.34 = (bf16[160,1280]{1,0:T(8,128)(2,1)S(1)}, bf16[160,1280]{1,0:T(8,128)(2,1)S(1)}, u32[]{:S(2)}, u32[]{:S(2)}) collective-permute-start(bf16[160,1280]{1,0:T(8,128)(2,1)S(1)} %get-tuple-element.64.refs_1_), channel_id=1, source_target_pairs={{0,2},{1,3},{2,0},{3,1},{4,6},{5,7},{6,4},{7,5},{8,10},{9,11},{10,... | collective-permute-start | bytes 1228808 | tf_op jit(solution)/shard_map/ppermute | solution.py:502
  161.7 20.2 %collective-permute-start.31 = (bf16[160,1280]{1,0:T(8,128)(2,1)S(1)}, bf16[160,1280]{1,0:T(8,128)(2,1)}, u32[]{:S(2)}, u32[]{:S(2)}) collective-permute-start(bf16[160,1280]{1,0:T(8,128)(2,1)S(1)} %get-tuple-element.64.refs_1_), channel_id=1, source_target_pairs={{0,1},{1,0},{2,3},{3,2},{4,5},{5,4},{6,7},{7,6},{8,9},{9,8},{10,11... | collective-permute-start | bytes 1228808 | tf_op jit(solution)/shard_map/ppermute | solution.py:502
  161.7 20.2 %collective-permute-start.32 = (bf16[160,1280]{1,0:T(8,128)(2,1)S(1)}, bf16[160,1280]{1,0:T(8,128)(2,1)}, u32[]{:S(2)}, u32[]{:S(2)}) collective-permute-start(bf16[160,1280]{1,0:T(8,128)(2,1)S(1)} %get-tuple-element.63.refs_15_.refs_0_.refs_4_), channel_id=1, source_target_pairs={{0,2},{1,3},{2,0},{3,1},{4,6},{5,7},{6,4},{7,5},{8,10},{9,11},{10,... | collective-permute-start | bytes 1228808 | tf_op jit(solution)/shard_map/ppermute | solution.py:502
  165.9 19.5 %collective-permute-start.35 = (bf16[160,1280]{1,0:T(8,128)(2,1)S(1)}, bf16[160,1280]{1,0:T(8,128)(2,1)S(1)}, u32[]{:S(2)}, u32[]{:S(2)}) collective-permute-start(bf16[160,1280]{1,0:T(8,128)(2,1)S(1)} %collective-permute-done.33.refs_0_), channel_id=1, source_target_pairs={{0,2},{1,3},{2,0},{3,1},{4,6},{5,7},{6,4},{7,5},{8,10},{9,11},{10,... | collective-permute-start | bytes 1228808 | tf_op jit(solution)/shard_map/ppermute | solution.py:502
  172.1 13.4 %collective-permute-start.36 = (bf16[160,1280]{1,0:T(8,128)(2,1)S(1)}, bf16[160,1280]{1,0:T(8,128)(2,1)}, u32[]{:S(2)}, u32[]{:S(2)}) collective-permute-start(bf16[160,1280]{1,0:T(8,128)(2,1)S(1)} %collective-permute-done.34.refs_1_), channel_id=1, source_target_pairs={{0,1},{1,0},{2,3},{3,2},{4,5},{5,4},{6,7},{7,6},{8,9},{9,8},{10,11... | collective-permute-start | bytes 1228808 | tf_op jit(solution)/shard_map/ppermute | solution.py:502
  172.6 2.9 %copy-start = (bf16[1280,2560]{1,0:T(8,128)(2,1)S(1)}, bf16[1280,2560]{1,0:T(8,128)(2,1)}, u32[]{:S(2)}) copy-start(bf16[1280,2560]{1,0:T(8,128)(2,1)} %all-gather.5.cloned.1.call-done.refs_2_) | copy-start | bytes 19660804
  175.4 3.2 %copy-start.1 = (bf16[1280,2560]{1,0:T(8,128)(2,1)S(1)}, bf16[1280,2560]{1,0:T(8,128)(2,1)}, u32[]{:S(2)}) copy-start(bf16[1280,2560]{1,0:T(8,128)(2,1)} %all-gather.5.cloned.1.call-done.refs_2_) | copy-start | bytes 19660804
  177.9 0.8 copy-start.4
  189.1 18.4 %copy-start.5 = (bf16[160,1280]{1,0:T(8,128)(2,1)S(1)}, bf16[160,1280]{1,0:T(8,128)(2,1)}, u32[]{:S(2)}) copy-start(bf16[160,1280]{1,0:T(8,128)(2,1)} %copy-done.4) | copy-start | bytes 1228804
  189.2 18.4 %copy-start.7 = (f32[1,1280]{1,0:T(1,128)S(1)}, f32[1,1280]{1,0:T(1,128)}, u32[]{:S(2)}) copy-start(f32[1,1280]{1,0:T(1,128)} %refs_6_.1) | copy-start | bytes 15364
  189.2 12.0 %collective-permute-start.37 = (bf16[160,1280]{1,0:T(8,128)(2,1)S(1)}, bf16[160,1280]{1,0:T(8,128)(2,1)S(1)}, u32[]{:S(2)}, u32[]{:S(2)}) collective-permute-start(bf16[160,1280]{1,0:T(8,128)(2,1)S(1)} %get-tuple-element.69), channel_id=1, source_target_pairs={{0,1},{1,0},{2,3},{3,2},{4,5},{5,4},{6,7},{7,6},{8,9},{9,8},{10,11... | collective-permute-start | bytes 1228808 | tf_op jit(solution)/shard_map/ppermute | solution.py:502
  190.8 15.4 %collective-permute-start.41 = (bf16[160,1280]{1,0:T(8,128)(2,1)S(1)}, bf16[160,1280]{1,0:T(8,128)(2,1)S(1)}, u32[]{:S(2)}, u32[]{:S(2)}) collective-permute-start(bf16[160,1280]{1,0:T(8,128)(2,1)S(1)} %get-tuple-element.66.refs_4_), channel_id=1, source_target_pairs={{0,1},{1,0},{2,3},{3,2},{4,5},{5,4},{6,7},{7,6},{8,9},{9,8},{10,11... | collective-permute-start | bytes 1228808 | tf_op jit(solution)/shard_map/ppermute | solution.py:502
  191.3 12.3 %collective-permute-start.39 = (bf16[160,1280]{1,0:T(8,128)(2,1)S(1)}, bf16[160,1280]{1,0:T(8,128)(2,1)S(1)}, u32[]{:S(2)}, u32[]{:S(2)}) collective-permute-start(bf16[160,1280]{1,0:T(8,128)(2,1)S(1)} %get-tuple-element.70), channel_id=1, source_target_pairs={{0,2},{1,3},{2,0},{3,1},{4,6},{5,7},{6,4},{7,5},{8,10},{9,11},{10,... | collective-permute-start | bytes 1228808 | tf_op jit(solution)/shard_map/ppermute | solution.py:502
  192.8 14.8 %collective-permute-start.42 = (bf16[160,1280]{1,0:T(8,128)(2,1)}, bf16[160,1280]{1,0:T(8,128)(2,1)S(1)}, u32[]{:S(2)}, u32[]{:S(2)}) collective-permute-start(bf16[160,1280]{1,0:T(8,128)(2,1)} %get-tuple-element.72), channel_id=1, source_target_pairs={{0,2},{1,3},{2,0},{3,1},{4,6},{5,7},{6,4},{7,5},{8,10},{9,11},{10,... | collective-permute-start | bytes 1228808 | tf_op jit(solution)/shard_map/ppermute | solution.py:502
  202.0 9.9 %collective-permute-start.38 = (bf16[160,1280]{1,0:T(8,128)(2,1)}, bf16[160,1280]{1,0:T(8,128)(2,1)S(1)}, u32[]{:S(2)}, u32[]{:S(2)}) collective-permute-start(bf16[160,1280]{1,0:T(8,128)(2,1)} %add_convert_fusion.1), channel_id=1, source_target_pairs={{0,2},{1,3},{2,0},{3,1},{4,6},{5,7},{6,4},{7,5},{8,10},{9,11},{10,... | collective-permute-start | bytes 1228808 | tf_op jit(solution)/shard_map/ppermute | solution.py:502
  204.4 8.2 %collective-permute-start.40 = (bf16[160,1280]{1,0:T(8,128)(2,1)}, bf16[160,1280]{1,0:T(8,128)(2,1)S(1)}, u32[]{:S(2)}, u32[]{:S(2)}) collective-permute-start(bf16[160,1280]{1,0:T(8,128)(2,1)} %add_convert_fusion), channel_id=1, source_target_pairs={{0,1},{1,0},{2,3},{3,2},{4,5},{5,4},{6,7},{7,6},{8,9},{9,8},{10,11... | collective-permute-start | bytes 1228808 | tf_op jit(solution)/shard_map/ppermute | solution.py:502
  207.6 1.1 copy-start.10
  208.7 1.1 copy-start.12
Sparse Core Ops, SparseCore 0:
  9.0 42.9 all-gather.2
  53.6 73.4 all-gather.4
